TPU v7x, 32 devices: a whole 2x2x4 slice. The times are simulated.
32 devices in a mesh: groups: 2 (over y), geom: 4 (over z), design: 2 (over x), head: 2 (over core).
Axes of the slice: x: 2, y: 2, z: 4, core: 2. Of those that a mesh axis runs over, the one named last changes fastest.
Arguments:
- point_feats: bfloat16 [4, 12288, 192], P(('groups', 'design'), ('geom', 'head')), parts along dimension 0, may hold values from -6 to 6
- block_anchor: int32 [4, 96], P(('groups', 'design'), ('geom', 'head')), parts along dimension 0, may hold values from 0 to 127, as said below
- anchor_feats: bfloat16 [4, 128, 192], P(('groups', 'design'), ('geom', 'head')), parts along dimension 0, may hold values from -4 to 4
- query_feats: bfloat16 [4, 4096, 192], P(('groups', 'design'), ('geom', 'head')), parts along dimension 0, may hold values from -6 to 6
- out_grad: bfloat16 [4, 4096, 192], P(('groups', 'design'), ('geom', 'head')), parts along dimension 0, may hold values from -6 to 6
- norm_gain: float32 [192], replicated, may hold values from 0.5 to 1.5
- w_in: bfloat16 [192, 384], replicated, may hold values from -0.4375 to 0.4375
- w_out: bfloat16 [384, 192], replicated, may hold values from -0.3125 to 0.3125
- w_query: bfloat16 [192, 192], replicated, may hold values from -0.4375 to 0.4375
- w_key: bfloat16 [192, 192], replicated, may hold values from -0.4375 to 0.4375
- w_value: bfloat16 [192, 192], replicated, may hold values from -0.4375 to 0.4375
- w_proj: bfloat16 [192, 192], replicated, may hold values from -0.4375 to 0.4375
Outputs:
- attended: bfloat16 [4, 4096, 192], P(('groups', 'design'), ('geom', 'head')), parts along dimension 0
- point_grad: bfloat16 [4, 12288, 192], P(('groups', 'design'), ('geom', 'head')), parts along dimension 0
- grad_in: float32 [384, 384], P('groups'), parts along dimension 0
- grad_out: float32 [768, 192], P('groups'), parts along dimension 0
- grad_query: float32 [384, 192], P('groups'), parts along dimension 0
- grad_key: float32 [384, 192], P('groups'), parts along dimension 0
- grad_value: float32 [384, 192], P('groups'), parts along dimension 0
- grad_proj: float32 [384, 192], P('groups'), parts along dimension 0
- grad_gain: float32 [384], P('groups'), parts along dimension 0
There are 2 independent parts, one for each index of `groups`. A program takes and returns all parts, laid end to end along the dimension named above; an argument that names none is the same for every part. Nothing has to cross between parts.
Inputs may be any that keep to these rules, and one draw needn't show every extreme that they name: `block_anchor`: block index // 12 is the device that holds the block. Each device assigns at most 2 of its blocks to anchors of any one owner (anchor // 16); in every design one owner gets exactly 2 blocks from every device.
All inputs are finite; a program needn't handle non-finite values.
Results may differ from a plain program's by a relative error of at most 0.03.
Values may be sent and summed in bfloat16 or wider, within the bound.
No kernel may reach another device: no remote copies, remote signals or barrier semaphores. Data moves between devices by JAX's collectives and lax.ppermute only.
A program may use at most 64 MiB of HBM per device.

v0:
```python
import jax
import jax.numpy as jnp
from jax import lax
from jax.sharding import PartitionSpec as P

HEADS = 3
CAP = 2


def gelu_tanh(values):
    return jax.nn.gelu(values, approximate=True)


def contract_rows(first_arg, second_arg, precision=None):
    return lax.dot_general(
        first_arg,
        second_arg,
        (((0,), (0,)), ((), ())),
        precision=precision,
        preferred_element_type=jnp.float32,
    )


def times_transposed(first_arg, second_arg):
    return lax.dot_general(
        first_arg, second_arg, (((1,), (1,)), ((), ())), preferred_element_type=jnp.float32
    )


def head_split(matrix):
    return matrix.reshape(matrix.shape[0], HEADS, matrix.shape[1] // HEADS)


def on_device(
    point_feats,
    block_anchor,
    anchor_feats,
    query_feats,
    out_grad,
    norm_gain,
    w_in,
    w_out,
    w_query,
    w_key,
    w_value,
    w_proj,
):
    exact_mode = lax.Precision.HIGHEST
    owners = lax.axis_size(("geom", "head"))
    points = point_feats[0]
    assigned = block_anchor[0]
    anchor_rows = anchor_feats[0]
    query_rows = query_feats[0]
    cotangent = out_grad[0]
    blocks = assigned.shape[0]
    feature_width = points.shape[1]
    hidden_width = w_in.shape[1]
    anchors_here = anchor_rows.shape[0]
    block_size = points.shape[0] // blocks
    slot_count = owners * CAP
    target = assigned // anchors_here
    within = assigned - target * anchors_here
    block_order = jnp.arange(blocks)
    earlier = (target[None, :] == target[:, None]) & (block_order[None, :] < block_order[:, None])
    slot_of = target * CAP + jnp.sum(earlier.astype(jnp.int32), axis=1)
    selector = jnp.arange(slot_count)[:, None] == slot_of[None, :]
    select_bf = selector.astype(jnp.bfloat16)
    slot_anchor = jnp.sum(jnp.where(selector, within[None, :] + 1, 0), axis=1) - 1
    pre_act = jnp.dot(points, w_in, preferred_element_type=jnp.float32)
    hidden = gelu_tanh(pre_act).astype(jnp.bfloat16)
    message = jnp.dot(hidden, w_out, preferred_element_type=jnp.float32)
    block_sums = message.reshape(blocks, block_size, feature_width).sum(axis=1)
    outgoing_sums = jnp.dot(selector.astype(jnp.float32), block_sums, precision=exact_mode)
    arrived_sums, arrived_ids = (
        lax.all_to_all(
            outgoing_sums.reshape(owners, CAP, feature_width).astype(jnp.bfloat16),
            ("geom", "head"),
            split_axis=0,
            concat_axis=0,
            tiled=True,
        ).astype(jnp.float32),
        lax.all_to_all(
            slot_anchor.astype(jnp.float32).reshape(owners, CAP).astype(jnp.bfloat16),
            ("geom", "head"),
            split_axis=0,
            concat_axis=0,
            tiled=True,
        ).astype(jnp.float32),
    )
    slot_sums = arrived_sums.reshape(slot_count, feature_width)
    slot_ids = arrived_ids.reshape(slot_count).astype(jnp.int32)
    member = (jnp.arange(anchors_here)[:, None] == slot_ids[None, :]).astype(jnp.float32)
    pooled = jnp.dot(member, slot_sums, precision=exact_mode)
    divisor = jnp.maximum(jnp.sum(member, axis=1) * block_size, 1.0)
    anchor_sum = anchor_rows.astype(jnp.float32) + pooled / divisor[:, None]
    inv_rms = lax.rsqrt(jnp.mean(anchor_sum * anchor_sum, axis=1, keepdims=True) + 1e-06)
    normed = (anchor_sum * inv_rms * norm_gain).astype(jnp.bfloat16)
    key_local = jnp.dot(normed, w_key, preferred_element_type=jnp.float32).astype(jnp.bfloat16)
    value_local = jnp.dot(normed, w_value, preferred_element_type=jnp.float32).astype(jnp.bfloat16)
    all_keys, all_values = (
        lax.all_gather(key_local, ("geom", "head"), axis=0, tiled=True),
        lax.all_gather(value_local, ("geom", "head"), axis=0, tiled=True),
    )
    query_proj = jnp.dot(query_rows, w_query, preferred_element_type=jnp.float32).astype(
        jnp.bfloat16
    )
    score_scale = 1.0 / (feature_width // HEADS) ** 0.5
    query_heads = head_split(query_proj)
    key_heads = head_split(all_keys)
    value_heads = head_split(all_values)
    scores = (
        jnp.einsum("qhd,khd->hqk", query_heads, key_heads, preferred_element_type=jnp.float32)
        * score_scale
    )
    softmax_w = jax.nn.softmax(scores, axis=-1)
    softmax_bf = softmax_w.astype(jnp.bfloat16)
    mixed_heads = (
        jnp.einsum("hqk,khd->qhd", softmax_bf, value_heads, preferred_element_type=jnp.float32)
        .reshape(-1, feature_width)
        .astype(jnp.bfloat16)
    )
    attended = jnp.dot(mixed_heads, w_proj, preferred_element_type=jnp.float32).astype(jnp.bfloat16)
    grad_proj = contract_rows(mixed_heads, cotangent)
    d_mixed = times_transposed(cotangent, w_proj).astype(jnp.bfloat16)
    dmix_heads = head_split(d_mixed)
    d_probs = jnp.einsum(
        "qhd,khd->hqk", dmix_heads, value_heads, preferred_element_type=jnp.float32
    )
    d_scores = (
        softmax_w * (d_probs - jnp.sum(softmax_w * d_probs, axis=-1, keepdims=True)) * score_scale
    ).astype(jnp.bfloat16)
    d_query = (
        jnp.einsum("hqk,khd->qhd", d_scores, key_heads, preferred_element_type=jnp.float32)
        .reshape(-1, feature_width)
        .astype(jnp.bfloat16)
    )
    key_terms = jnp.einsum(
        "hqk,qhd->khd", d_scores, query_heads, preferred_element_type=jnp.float32
    ).reshape(-1, feature_width)
    value_terms = jnp.einsum(
        "hqk,qhd->khd", softmax_bf, dmix_heads, preferred_element_type=jnp.float32
    ).reshape(-1, feature_width)
    grad_query = contract_rows(query_rows, d_query)
    key_sum, value_sum = (
        lax.psum_scatter(
            key_terms.astype(jnp.bfloat16), ("geom", "head"), scatter_dimension=0, tiled=True
        ).astype(jnp.float32),
        lax.psum_scatter(
            value_terms.astype(jnp.bfloat16), ("geom", "head"), scatter_dimension=0, tiled=True
        ).astype(jnp.float32),
    )
    key_grad = key_sum.astype(jnp.bfloat16)
    value_grad = value_sum.astype(jnp.bfloat16)
    grad_key = contract_rows(normed, key_grad)
    grad_value = contract_rows(normed, value_grad)
    d_normed = times_transposed(key_grad, w_key) + times_transposed(value_grad, w_value)
    scaled = d_normed * norm_gain
    grad_gain = jnp.sum(d_normed * anchor_sum * inv_rms, axis=0)
    d_sum = inv_rms * scaled - anchor_sum * inv_rms**3 * jnp.mean(
        scaled * anchor_sum, axis=1, keepdims=True
    )
    d_pooled = d_sum / divisor[:, None]
    slot_grad = contract_rows(member, d_pooled, exact_mode).astype(jnp.bfloat16)
    returned_grad = lax.all_to_all(
        slot_grad.reshape(owners, CAP, feature_width),
        ("geom", "head"),
        split_axis=0,
        concat_axis=0,
        tiled=True,
    )
    block_grad = contract_rows(select_bf, returned_grad.reshape(slot_count, feature_width)).astype(
        jnp.bfloat16
    )
    d_hidden_block = times_transposed(block_grad, w_out)
    d_hidden = jnp.broadcast_to(
        d_hidden_block[:, None, :], (blocks, block_size, hidden_width)
    ).reshape(-1, hidden_width)
    unused_out, gelu_back = jax.vjp(gelu_tanh, pre_act)
    d_pre = gelu_back(d_hidden)[0].astype(jnp.bfloat16)
    hidden_sum = jnp.sum(
        hidden.reshape(blocks, block_size, hidden_width), axis=1, dtype=jnp.float32
    )
    grad_out = contract_rows(hidden_sum, block_grad.astype(jnp.float32), exact_mode)
    grad_in = contract_rows(points, d_pre)
    d_input = times_transposed(d_pre, w_in).astype(jnp.bfloat16)
    reduced = lax.psum(
        (grad_in, grad_out, grad_query, grad_key, grad_value, grad_proj, grad_gain),
        ("geom", "design", "head"),
    )
    return (
        attended[None],
        d_input[None],
        reduced[0],
        reduced[1],
        reduced[2],
        reduced[3],
        reduced[4],
        reduced[5],
        reduced[6],
    )


def solution(mesh):
    placed = (
        P(("groups", "design"), ("geom", "head"), None),
        P(("groups", "design"), ("geom", "head")),
        P(("groups", "design"), ("geom", "head"), None),
        P(("groups", "design"), ("geom", "head"), None),
        P(("groups", "design"), ("geom", "head"), None),
        P(),
        P(),
        P(),
        P(),
        P(),
        P(),
        P(),
    )
    return jax.shard_map(
        on_device,
        mesh=mesh,
        in_specs=placed,
        out_specs=(
            P(("groups", "design"), ("geom", "head"), None),
            P(("groups", "design"), ("geom", "head"), None),
            P("groups", None),
            P("groups", None),
            P("groups", None),
            P("groups", None),
            P("groups", None),
            P("groups", None),
            P("groups"),
        ),
        check_vma=False,
    )
```

profile of v0, /device:TPU:0, one launch (start us, length us, event | category | flops | bytes accessed | tf_op | source)
XLA Modules:
  0.0 259.6 jit_solution(16616870421361154867)
XLA Ops:
  7.2 0.7 and_select_fusion
  7.9 0.7 add_bitcast_fusion
  8.9 0.7 convert_element_type.190
  9.6 6.4 %all-to-all-start = ((bf16[8,1,2]{2,1,0:T(2,128)(2,1)}), bf16[8,1,2]{2,1,0:T(2,128)(2,1)S(1)}, u32[]{:S(2)}, u32[]{:S(2)}) async-start(bf16[8,1,2]{2,1,0:T(2,128)(2,1)} %convert_element_type.190), calls=%async_computation | async-start | bytes 8192 | tf_op jit(solution)/shard_map/all_to_all | solution.py:82
  16.0 3.2 %multiply_convert_fusion = (bf16[1536,384]{1,0:T(8,128)(2,1)S(1)}, f32[1536,384]{1,0:T(8,128)}) fusion(bf16[192,384]{1,0:T(8,128)(2,1)} %param.18, bf16[1,1536,192]{1,2,0:T(8,128)(2,1)S(1)} %copy-done), kind=kOutput, calls=%fused_computation.19 | convolution fusion | flops 231800832 | bytes 4276224 | tf_op jit(solution)/shard_map/dot_general | solution.py:69
  19.2 0.8 convert_reduce_fusion
  20.0 0.6 fusion.64
  20.9 1.2 convolution_convert_fusion.5
  22.1 1.2 convolution_convert_fusion.1
  23.3 0.5 reduce_sum.95
  23.9 0.7 copy.50
  24.6 5.1 %all-to-all-start.1 = ((bf16[8,2,192]{2,1,0:T(2,128)(2,1)}), bf16[8,2,192]{2,1,0:T(2,128)(2,1)S(1)}, u32[]{:S(2)}, u32[]{:S(2)}) async-start(bf16[8,2,192]{2,1,0:T(2,128)(2,1)} %copy.50), calls=%async_computation.1 | async-start | bytes 16384 | tf_op jit(solution)/shard_map/all_to_all | solution.py:75
  30.0 5.3 %all-to-all-done.1 = bf16[8,2,192]{2,1,0:T(2,128)(2,1)S(1)} async-done(((bf16[8,2,192]{2,1,0:T(2,128)(2,1)}), bf16[8,2,192]{2,1,0:T(2,128)(2,1)S(1)}, u32[]{:S(2)}, u32[]{:S(2)}) %all-to-all-start.1) | async-done | bytes 6176 | tf_op jit(solution)/shard_map/all_to_all | solution.py:75
  35.4 0.2 multiply_reduce_fusion.3
  36.0 14.0 %all_gather.6 = bf16[128,192]{1,0:T(8,128)(2,1)S(1)} all-gather(bf16[16,192]{1,0:T(8,128)(2,1)S(1)} %convolution_convert_fusion.11), channel_id=1, replica_groups=mesh['groups'=2,'geom'=4,'design'=2,'head'=2] {'geom','head'}, dimensions={0}, use_global_device_ids=true | all-gather | bytes 55296 | tf_op jit(solution)/shard_map/all_gather | solution.py:102
  50.1 14.0 %all_gather.7 = bf16[128,192]{1,0:T(8,128)(2,1)S(1)} all-gather(bf16[16,192]{1,0:T(8,128)(2,1)S(1)} %convolution_convert_fusion.10), channel_id=1, replica_groups=mesh['groups'=2,'geom'=4,'design'=2,'head'=2] {'geom','head'}, dimensions={0}, use_global_device_ids=true | all-gather | bytes 55296 | tf_op jit(solution)/shard_map/all_gather | solution.py:101
  64.2 0.3 fusion.65
  64.5 1.3 fusion.63
  65.8 1.8 convolution_convert_fusion.7
  67.6 1.8 convolution_convert_fusion.2
  69.4 0.6 convolution_convert_fusion.4
  70.0 0.9 convolution_bitcast_fusion.1
  70.9 0.7 copy.64
  71.7 0.9 fusion.30
  72.6 0.6 convolution_convert_fusion.6
  73.2 0.7 copy.66
  74.0 26.5 %reduce-scatter.7.cloned.1.call-done = bf16[16,192]{1,0:T(8,128)(2,1)} async-done(((bf16[128,192]{1,0:T(8,128)(2,1)}), bf16[16,192]{1,0:T(8,128)(2,1)}) %reduce-scatter.7.cloned.1.call-update) | async-done | bytes 6160
  100.5 0.8 fusion.66
  101.4 30.6 %reduce-scatter.9.cloned.1.call-done = bf16[16,192]{1,0:T(8,128)(2,1)} async-done(((bf16[128,192]{1,0:T(8,128)(2,1)}), bf16[16,192]{1,0:T(8,128)(2,1)}) %reduce-scatter.9.cloned.1.call-update) | async-done | bytes 6160
  132.0 1.0 multiply_reduce_fusion.1
  133.2 0.6 reshape.172
  133.8 3.3 %all-to-all-start.2 = ((bf16[8,2,192]{2,1,0:T(2,128)(2,1)}), bf16[8,2,192]{2,1,0:T(2,128)(2,1)S(1)}, u32[]{:S(2)}, u32[]{:S(2)}) async-start(bf16[8,2,192]{2,1,0:T(2,128)(2,1)} %reshape.172), calls=%async_computation.2 | async-start | bytes 16384 | tf_op jit(solution)/shard_map/all_to_all | solution.py:164
  137.2 1.6 fusion.70
  138.8 1.6 fusion.69
  140.4 2.3 all-to-all-done.2
  143.0 1.1 fusion.68
  144.1 3.2 %fusion.9 = bf16[1536,384]{1,0:T(8,128)(2,1)S(1)} fusion(f32[1536,384]{1,0:T(8,128)} %get-tuple-element.58, f32[12,384]{1,0:T(8,128)S(1)} %fusion.67), kind=kLoop, calls=%fused_computation.14 | loop fusion | flops 11796480 | bytes 3557376 | tf_op jit(solution)/shard_map/convert_element_type | solution.py:179
  147.4 1.2 convolution_bitcast_fusion
  148.6 0.9 fusion.19
  149.5 32.4 %psum.55 = f32[192]{0:T(256)} all-reduce(f32[192]{0:T(256)S(1)} %get-tuple-element.45), channel_id=1, replica_groups=mesh['groups'=2,'geom'=4,'design'=2,'head'=2] {'geom','design','head'}, use_global_device_ids=true, to_apply=%region_19.20 | all-reduce | flops 192 | bytes 1536 | tf_op jit(solution)/shard_map/psum | solution.py:186
  181.9 1.4 fusion.2
  183.3 60.8 %all-reduce.3.cloned.1.call-done = (f32[192,384]{1,0:T(8,128)}, f32[384,192]{0,1:T(8,128)}, f32[192,192]{0,1:T(8,128)}, f32[192,192]{1,0:T(8,128)}, f32[192,192]{1,0:T(8,128)}, /*index=5*/f32[192,192]{1,0:T(8,128)}) async-done(((f32[192,384]{1,0:T(8,128)}, f32[384,192]{0,1:T(8,128)}, f32[192,192]{0,1:T(8,128)}, f32[192,192]{1,0:T(8,128)}, f32[192,192]{1,0:T(8,128)}, /*index=5*/f32[192,192]{1,0:T(8,128)}), ...) | async-done | bytes 1179664 | tf_op jit(solution)/shard_map/psum | solution.py:186
  244.0 1.8 copy.57
  245.8 1.7 copy.74
  247.5 1.7 copy.75
  249.2 1.6 copy.76
  250.8 1.6 copy.77
  252.4 0.7 copy.78
  (56 shorter events, 2.4 us)
Async XLA Ops:
  7.2 8.8 %copy-start = (bf16[1,1536,192]{1,2,0:T(8,128)(2,1)S(1)}, bf16[1,1536,192]{1,2,0:T(8,128)(2,1)}, u32[]{:S(2)}) copy-start(bf16[1,1536,192]{1,2,0:T(8,128)(2,1)} %param.12) | copy-start | bytes 1769476
  9.6 15.0 %all-to-all-start = ((bf16[8,1,2]{2,1,0:T(2,128)(2,1)}), bf16[8,1,2]{2,1,0:T(2,128)(2,1)S(1)}, u32[]{:S(2)}, u32[]{:S(2)}) async-start(bf16[8,1,2]{2,1,0:T(2,128)(2,1)} %convert_element_type.190), calls=%async_computation | async-start | bytes 8192 | tf_op jit(solution)/shard_map/all_to_all | solution.py:82
  16.0 4.0 %copy-start.3 = (bf16[384,192]{0,1:T(8,128)(2,1)S(1)}, bf16[384,192]{0,1:T(8,128)(2,1)}, u32[]{:S(2)}) copy-start(bf16[384,192]{0,1:T(8,128)(2,1)} %param.19) | copy-start | bytes 442372
  20.0 0.9 copy-start.1
  20.6 15.0 %copy-start.11 = (f32[192]{0:T(256)S(1)}, f32[192]{0:T(256)}, u32[]{:S(2)}) copy-start(f32[192]{0:T(256)} %param.17) | copy-start | bytes 2308
  20.9 14.4 %copy-start.12 = (bf16[1,16,192]{2,1,0:T(8,128)(2,1)S(1)}, bf16[1,16,192]{2,1,0:T(8,128)(2,1)}, u32[]{:S(2)}) copy-start(bf16[1,16,192]{2,1,0:T(8,128)(2,1)} %param.14) | copy-start | bytes 18436
  20.9 14.8 %copy-start.6 = (bf16[192,192]{1,0:T(8,128)(2,1)S(1)}, bf16[192,192]{1,0:T(8,128)(2,1)}, u32[]{:S(2)}) copy-start(bf16[192,192]{1,0:T(8,128)(2,1)} %param.21) | copy-start | bytes 221188
  20.9 14.9 %copy-start.5 = (bf16[192,192]{1,0:T(8,128)(2,1)S(1)}, bf16[192,192]{1,0:T(8,128)(2,1)}, u32[]{:S(2)}) copy-start(bf16[192,192]{1,0:T(8,128)(2,1)} %param.22) | copy-start | bytes 221188
  24.6 10.7 %all-to-all-start.1 = ((bf16[8,2,192]{2,1,0:T(2,128)(2,1)}), bf16[8,2,192]{2,1,0:T(2,128)(2,1)S(1)}, u32[]{:S(2)}, u32[]{:S(2)}) async-start(bf16[8,2,192]{2,1,0:T(2,128)(2,1)} %copy.50), calls=%async_computation.1 | async-start | bytes 16384 | tf_op jit(solution)/shard_map/all_to_all | solution.py:75
  29.7 70.8 %reduce-scatter.7.cloned.1.call-start = ((), (), s32[]{:S(2)}) async-start(), calls=%async_computation.5 | async-start | bytes 73728
  69.4 2.3 copy-start.2
  71.7 60.3 %reduce-scatter.9.cloned.1.call-start = ((), (), s32[]{:S(2)}) async-start(), calls=%async_computation.6 | async-start | bytes 73728
  72.6 70.3 %copy-start.4 = (bf16[384,192]{0,1:T(8,128)(2,1)S(1)}, bf16[384,192]{0,1:T(8,128)(2,1)}, u32[]{:S(2)}) copy-start(bf16[384,192]{0,1:T(8,128)(2,1)} %param.19) | copy-start | bytes 442372
  72.6 70.4 %copy-start.10 = (f32[12,384]{1,0:T(8,128)S(1)}, f32[12,384]{1,0:T(8,128)}, u32[]{:S(2)}) copy-start(f32[12,384]{1,0:T(8,128)} %convert_reduce_fusion) | copy-start | bytes 55300
  133.8 8.9 %all-to-all-start.2 = ((bf16[8,2,192]{2,1,0:T(2,128)(2,1)}), bf16[8,2,192]{2,1,0:T(2,128)(2,1)S(1)}, u32[]{:S(2)}, u32[]{:S(2)}) async-start(bf16[8,2,192]{2,1,0:T(2,128)(2,1)} %reshape.172), calls=%async_computation.2 | async-start | bytes 16384 | tf_op jit(solution)/shard_map/all_to_all | solution.py:164
  137.1 106.9 %all-reduce.3.cloned.1.call-start = ((), (), s32[]{:S(2)}) async-start(), calls=%async_computation.7 | async-start | bytes 2752512 | tf_op jit(solution)/shard_map/psum | solution.py:186
  147.3 1.2 copy-start.7
  147.3 34.6 %copy-start.9 = (bf16[192,384]{1,0:T(8,128)(2,1)S(1)}, bf16[192,384]{1,0:T(8,128)(2,1)}, u32[]{:S(2)}) copy-start(bf16[192,384]{1,0:T(8,128)(2,1)} %param.18) | copy-start | bytes 442372
  244.0 8.4 %copy-start.8 = (f32[192,192]{1,0:T(8,128)S(1)}, f32[192,192]{1,0:T(8,128)}, u32[]{:S(2)}) copy-start(f32[192,192]{1,0:T(8,128)} %get-tuple-element.71) | copy-start | bytes 442372
Sparse Core Ops, SparseCore 0:
  71.8 28.6 reduce-scatter.6
  103.3 28.5 reduce-scatter.8
  148.7 95.3 all-reduce.2
where the time goes:
time: 260 us
  waiting for transfers between devices  126 us (48%)
  blocking collectives  60.4 us (23%)
  matrix products  25.1 us (10%)
  starting transfers between devices  14.9 us (6%)
  between operations  14 us (5%)
  local copies, waits for them, and re-layouts  13.3 us (5%)
  other arithmetic  6.46 us (2%)
    psum x1, waiting for transfers between devices, on_device(): lax.psum((grad_in, grad_out, grad_query, grad_key, grad_value, grad_proj,...  60.8 us
    unnamed x5, waiting for transfers between devices  57.2 us
    psum x1, blocking collectives, on_device(): lax.psum((grad_in, grad_out, grad_query, grad_key, grad_value, grad_proj,...  32.4 us
    all_gather x1, blocking collectives, on_device(): lax.all_gather(key_local, ('geom', 'head'), axis=0, tiled=True)  14 us
    all_gather x1, blocking collectives, on_device(): lax.all_gather(value_local, ('geom', 'head'), axis=0, tiled=True)  14 us
    unnamed x34, local copies, waits for them, and re-layouts  10.7 us
    dot_general x8, matrix products, contract_rows(): lax.dot_general(first_arg, second_arg, (((0,), (0,)), ((), ())), precisio...  7.61 us
    all_to_all x1, starting transfers between devices, on_device(): lax.all_to_all(slot_anchor.astype(jnp.float32).reshape(owners, CAP).astyp...  6.35 us
  transfers between devices with their start and end apart: 6, of which 5 were waited for; matrix products, arithmetic and copies ran while one was open for 7% of the time, Pallas kernels for 0%

commit v1 on v0

v1 whole, which is shorter than its diff:
```python
import functools

import jax
import jax.numpy as jnp
from jax import lax
from jax.experimental import pallas as pl
from jax.experimental.pallas import tpu as pltpu
from jax.sharding import PartitionSpec as P

HEADS = 3
LANES = 128
DIGIT = 128
INTERPRET = False
BF = jnp.bfloat16
F32 = jnp.float32
GELU_C = 0.7978845608028654
GELU_A = 0.044715


def dg(a, b, ca, cb):
    return lax.dot_general(a, b, (((ca,), (cb,)), ((), ())), preferred_element_type=F32)


def split_bf(x):
    high = x.astype(BF)
    return high, (x - high.astype(F32)).astype(BF)


def call(kernel, outs, *args, scratch=(), smem=0):
    specs = [pl.BlockSpec(memory_space=pltpu.SMEM)] * smem
    specs += [pl.BlockSpec(memory_space=pltpu.VMEM)] * (len(args) - smem)
    return pl.pallas_call(
        kernel,
        out_shape=[jax.ShapeDtypeStruct(shape, dtype) for shape, dtype in outs],
        in_specs=specs,
        out_specs=[pl.BlockSpec(memory_space=pltpu.VMEM)] * len(outs),
        scratch_shapes=list(scratch),
        interpret=INTERPRET,
    )(*args)


def round_up(n, k):
    return (n + k - 1) // k * k


def iota(shape, dim):
    return lax.broadcasted_iota(jnp.int32, shape, dim)


def pool_kernel(blocks, x_ref, win_ref, wout_ref, anchor_ref, id_ref, send_ref, slope_ref, hsum_ref):
    width, points = x_ref.shape
    size = points // blocks
    hid = win_ref.shape[1]
    owners, rows, _ = send_ref.shape
    win = win_ref[...]
    step = 2 if blocks % 2 == 0 else 1
    hsum = jnp.zeros((round_up(blocks, 8), hid), F32)
    for first in range(0, blocks, step):
        cols = pl.ds(first * size, step * size)
        pre = dg(win, x_ref[:, cols], 0, 0)
        square = pre * pre
        tanh = jnp.tanh(pre * (GELU_C + (GELU_C * GELU_A) * square))
        half = 0.5 + 0.5 * tanh
        hidden = (pre * half).astype(BF)
        slope = half + pre * ((half * (1.0 - tanh)) * (GELU_C + (3.0 * GELU_C * GELU_A) * square))
        slope_ref[:, cols] = slope.astype(slope_ref.dtype)
        shape = (hsum.shape[0], step * size)
        pick = (iota(shape, 0) == first + iota(shape, 1) // size).astype(F32).astype(BF)
        hsum = hsum + dg(pick, hidden, 1, 1)
    hsum_ref[...] = hsum
    high, low = split_bf(hsum)
    wout = wout_ref[...]
    sums = dg(high, wout, 1, 1) + dg(low, wout, 1, 1)
    ids = id_ref[...]
    digits = jnp.concatenate([ids % DIGIT, ids // DIGIT], axis=0).astype(F32)
    packed = jnp.zeros((rows, 2 * width), F32)
    packed = jnp.concatenate(
        [
            jnp.concatenate(
                [anchor_ref[...].astype(F32)]
                + ([jnp.zeros((rows - anchor_ref.shape[0], width), F32)] if rows > anchor_ref.shape[0] else []),
                axis=0,
            ),
            jnp.concatenate(
                [
                    sums[:blocks],
                    jnp.concatenate([digits, jnp.zeros((2, width - blocks), F32)], axis=1),
                    jnp.zeros((rows - blocks - 2, width), F32),
                ],
                axis=0,
            ),
        ],
        axis=1,
    ).astype(BF)
    for owner in range(owners):
        send_ref[owner] = packed


def query_kernel(x_ref, g_ref, wq_ref, wp_ref, q_ref, dmix_ref):
    q_ref[...] = dg(wq_ref[...], x_ref[...], 0, 0).astype(BF)
    dmix_ref[...] = dg(wp_ref[...], g_ref[...], 1, 0).astype(BF)


def attend_kernel(
    blocks, size, per_owner,
    got_ref, gain_ref, wk_ref, wv_ref, q_ref, dmix_ref,
    rows_ref, normed_ref, k_ref, v_ref, p_ref, ds_ref, kt_ref, vt_ref, gain_out_ref,
):
    owners, rows, both = got_ref.shape
    width = both // 2
    total = owners * rows
    anchors = owners * per_owner
    got = got_ref[...].astype(F32)
    side = got[:, :, width:]
    sums = side.reshape(total, width)
    low = jnp.broadcast_to(side[:, blocks : blocks + 1, :], side.shape).reshape(total, width)
    high = jnp.broadcast_to(side[:, blocks + 1 : blocks + 2, :], side.shape).reshape(total, width)
    lane = iota((total, width), 1)
    place = iota((total, width), 0) % rows
    ids = jnp.sum(jnp.where(lane == place, low + high * DIGIT, 0.0), axis=1, keepdims=True)
    valid = (iota((total, 1), 0) % rows) < blocks
    ids = jnp.where(valid, ids, -1.0).astype(jnp.int32)
    member = (ids == iota((total, anchors), 1)).astype(F32).astype(BF)
    sums_bf = sums.astype(BF)
    pooled = dg(member, sums_bf, 0, 0)
    count = dg(member, jnp.ones((total, LANES), BF), 0, 0)[:, :1]
    inv_div = 1.0 / jnp.maximum(count * size, 1.0)
    anchor_rows = got[:, :per_owner, :width].reshape(anchors, width)
    asum = anchor_rows + pooled * inv_div
    inv = lax.rsqrt(jnp.mean(asum * asum, axis=1, keepdims=True) + 1e-6)
    gain = gain_ref[...]
    unit = asum * inv
    normed = (unit * gain).astype(BF)
    normed_ref[...] = normed
    keys = dg(wk_ref[...], normed, 0, 1).astype(BF)
    values = dg(wv_ref[...], normed, 0, 1).astype(BF)
    k_ref[...] = keys
    v_ref[...] = values
    depth = width // HEADS
    scale = 1.0 / depth**0.5
    for head in range(HEADS):
        part = slice(head * depth, (head + 1) * depth)
        q = q_ref[part, :]
        dmix = dmix_ref[part, :]
        scores = dg(keys[part], q, 0, 0) * scale
        top = jnp.max(scores, axis=0, keepdims=True)
        weight = jnp.exp(scores - top)
        probs = weight * (1.0 / jnp.sum(weight, axis=0, keepdims=True))
        probs_bf = probs.astype(BF)
        p_ref[head] = probs_bf
        dprobs = dg(values[part], dmix, 0, 0)
        inner = jnp.sum(probs * dprobs, axis=0, keepdims=True)
        dscore = (probs * (dprobs - inner) * scale).astype(BF)
        ds_ref[head] = dscore
        kt_ref[part, :] = dg(q, dscore, 1, 1).astype(BF)
        vt_ref[part, :] = dg(dmix, probs_bf, 1, 1).astype(BF)
    dnorm = dg(kt_ref[...], wk_ref[...], 0, 1) + dg(vt_ref[...], wv_ref[...], 0, 1)
    gain_out_ref[...] = jnp.sum(dnorm * unit, axis=0, keepdims=True)
    scaled = dnorm * gain
    dsum = inv * scaled - asum * (inv * inv * inv) * jnp.mean(scaled * asum, axis=1, keepdims=True)
    dpool = (dsum * inv_div).astype(BF)
    rows_ref[...] = dg(member, dpool, 1, 0).astype(BF).reshape(owners, rows, width)


def put_rows(ref, chunk, start, value):
    done = 0
    while done < value.shape[0]:
        index, offset = divmod(start + done, chunk)
        take = min(chunk - offset, value.shape[0] - done)
        ref[index, offset : offset + take, :] = value[done : done + take]
        done += take


def get_rows(read, chunk, start, count):
    pieces = []
    done = 0
    while done < count:
        index, offset = divmod(start + done, chunk)
        take = min(chunk - offset, count - done)
        pieces.append(read(index, offset, take))
        done += take
    return pieces[0] if len(pieces) == 1 else jnp.concatenate(pieces, axis=0)


def pack_square(ref, chunk, mats, start):
    width = mats[0].shape[0]
    for mat in mats:
        put_rows(ref, chunk, start, mat[:, :LANES])
        start += width
    for first in range(0, len(mats), 2):
        pair = jnp.concatenate([mats[first][:, LANES:], mats[first + 1][:, LANES:]], axis=1)
        put_rows(ref, chunk, start, pair)
        start += width
    return start


def swap_halves(head_ref, scratch, keep_ref, send_ref):
    half = keep_ref.shape[0]
    head = head_ref[0]
    keep_ref[...] = scratch[pl.ds(head * half, half)].astype(keep_ref.dtype)
    send_ref[...] = scratch[pl.ds((1 - head) * half, half)].astype(send_ref.dtype)


def finish_kernel(
    chunk, head_ref, p_ref, ds_ref, k_ref, v_ref, kt_ref, vt_ref, normed_ref, gain_ref, x_ref, g_ref,
    wp_ref, out_ref, keep_ref, send_ref, mixed_ref, dq_ref, pack_ref,
):
    width = k_ref.shape[0]
    depth = width // HEADS
    for head in range(HEADS):
        part = slice(head * depth, (head + 1) * depth)
        mixed_ref[part, :] = dg(v_ref[part, :], p_ref[head], 1, 0).astype(BF)
        dq_ref[part, :] = dg(k_ref[part, :], ds_ref[head], 1, 0).astype(BF)
    mixed = mixed_ref[...]
    out_ref[...] = dg(wp_ref[...], mixed, 0, 0).astype(BF)
    mats = [
        dg(x_ref[...], dq_ref[...], 1, 1),
        dg(normed_ref[...], kt_ref[...], 0, 1),
        dg(normed_ref[...], vt_ref[...], 0, 1),
        dg(mixed, g_ref[...], 1, 1),
    ]
    pieces, rows, _ = pack_ref.shape
    pack_square(pack_ref, chunk, mats, 0)
    gain = gain_ref[...]
    pack_ref[:, chunk:, :] = jnp.zeros((pieces, rows - chunk, LANES), F32)
    pack_ref[0, chunk : chunk + 1, :] = gain[:, :LANES]
    rest = width - LANES
    pack_ref[0, chunk + 1 : chunk + 2, :] = jnp.concatenate(
        [gain[:, LANES:], jnp.zeros((1, LANES - rest), F32)], axis=1
    )
    swap_halves(head_ref, pack_ref, keep_ref, send_ref)


def back_kernel(
    blocks, chunk, head_ref, got_ref, wout_ref, slope_ref, x_ref, hsum_ref,
    dpre_ref, keep_ref, send_ref, pack_ref,
):
    width, points = x_ref.shape
    size = points // blocks
    grad = jnp.sum(got_ref[...].astype(F32), axis=0)[: hsum_ref.shape[0]].astype(BF)
    dhid = dg(wout_ref[...], grad, 0, 1)
    for block in range(blocks):
        cols = pl.ds(block * size, size)
        dpre_ref[:, cols] = (slope_ref[:, cols].astype(F32) * dhid[:, block : block + 1]).astype(BF)
    gin = dg(x_ref[...], dpre_ref[...], 1, 1)
    high, low = split_bf(hsum_ref[...])
    gout = dg(grad, high, 0, 0) + dg(grad, low, 0, 0)
    start = 0
    for mat in (gin, gout):
        for lane in range(0, mat.shape[1], LANES):
            put_rows(pack_ref, chunk, start, mat[:, lane : lane + LANES])
            start += width
    swap_halves(head_ref, pack_ref, keep_ref, send_ref)


def point_grad_kernel(win_ref, dpre_ref, out_ref):
    out_ref[...] = dg(win_ref[...], dpre_ref[...], 1, 0).astype(BF)


def join_kernel(ka_ref, ra_ref, kp_ref, rp_ref, out_ref):
    rows = ka_ref.shape[1]
    out_ref[:, :rows, :] = (ka_ref[...] + ra_ref[...].astype(F32)).astype(BF)
    out_ref[:, rows:, :] = (kp_ref[...] + rp_ref[...].astype(F32)).astype(BF)


def sum_kernel(got_ref, out_ref):
    total = jnp.sum(got_ref[...].astype(F32), axis=0).astype(BF)
    for peer in range(out_ref.shape[0]):
        out_ref[peer] = total


def unpack_kernel(
    chunk_a, rows_a, chunk_p, head_ref, mine_ref, other_ref,
    gin_ref, gout_ref, gq_ref, gk_ref, gv_ref, gp_ref, gain_ref, all_ref,
):
    peers = mine_ref.shape[0]
    head = head_ref[0]
    all_ref[pl.ds(head * peers, peers)] = mine_ref[...]
    all_ref[pl.ds((1 - head) * peers, peers)] = other_ref[...]

    def read_a(index, offset, take):
        return all_ref[index, offset : offset + take, :].astype(F32)

    def read_p(index, offset, take):
        return all_ref[index, rows_a + offset : rows_a + offset + take, :].astype(F32)

    width = gq_ref.shape[0]
    squares = (gq_ref, gk_ref, gv_ref, gp_ref)
    start = 0
    for ref in squares:
        ref[:, :LANES] = get_rows(read_a, chunk_a, start, width)
        start += width
    rest = width - LANES
    for first in range(0, len(squares), 2):
        pair = get_rows(read_a, chunk_a, start, width)
        squares[first][:, LANES:] = pair[:, :rest]
        squares[first + 1][:, LANES:] = pair[:, rest:]
        start += width
    tail = all_ref[0, chunk_a:rows_a, :].astype(F32)
    gain_ref[...] = jnp.concatenate([tail[:1], tail[1:2, :rest]], axis=1)
    start = 0
    for ref in (gin_ref, gout_ref):
        for lane in range(0, ref.shape[1], LANES):
            ref[:, lane : lane + LANES] = get_rows(read_p, chunk_p, start, width)
            start += width


def on_device(
    point_feats, block_anchor, anchor_feats, query_feats, out_grad, norm_gain,
    w_in, w_out, w_query, w_key, w_value, w_proj,
):
    team = ("geom", "head")
    crowd = ("geom", "design")
    owners = lax.axis_size(team)
    peers = lax.axis_size(crowd)
    xt = point_feats[0].T
    qt = query_feats[0].T
    gt = out_grad[0].T
    wot = w_out.T
    blocks = block_anchor.shape[1]
    per_owner, width = anchor_feats.shape[1:]
    points = xt.shape[1]
    queries = qt.shape[1]
    hid = w_in.shape[1]
    size = points // blocks
    anchors = owners * per_owner
    rows = round_up(max(per_owner, blocks + 2), 16)
    head = lax.axis_index("head").astype(jnp.int32).reshape(1)
    pieces = 2 * peers
    chunk_a = 6 * width // pieces
    rows_a = chunk_a + 8
    chunk_p = 2 * width * hid // LANES // pieces

    send, slope, hsum = call(
        functools.partial(pool_kernel, blocks),
        [((owners, rows, 2 * width), BF), ((hid, points), BF), ((round_up(blocks, 8), hid), F32)],
        xt, w_in, wot, anchor_feats[0], block_anchor,
    )
    got = lax.all_to_all(send, team, 0, 0, tiled=True)
    qp, dmix = call(
        query_kernel, [((width, queries), BF), ((width, queries), BF)], qt, gt, w_query, w_proj
    )
    pair_shape = (HEADS, anchors, queries)
    rows_out, normed, keys, values, probs, dscore, kt, vt, gain_part = call(
        functools.partial(attend_kernel, blocks, size, per_owner),
        [
            ((owners, rows, width), BF),
            ((anchors, width), BF),
            ((width, anchors), BF),
            ((width, anchors), BF),
            (pair_shape, BF),
            (pair_shape, BF),
            ((width, anchors), BF),
            ((width, anchors), BF),
            ((1, width), F32),
        ],
        got, norm_gain.reshape(1, width), w_key, w_value, qp, dmix,
    )
    back = lax.all_to_all(rows_out, team, 0, 0, tiled=True)
    attended, keep_a, send_a = call(
        functools.partial(finish_kernel, chunk_a),
        [((width, queries), BF), ((peers, rows_a, LANES), F32), ((peers, rows_a, LANES), BF)],
        head, probs, dscore, keys, values, kt, vt, normed, gain_part, qt, gt, w_proj,
        scratch=[
            pltpu.VMEM((width, queries), BF),
            pltpu.VMEM((width, queries), BF),
            pltpu.VMEM((pieces, rows_a, LANES), F32),
        ],
        smem=1,
    )
    swap = [(0, 1), (1, 0)]
    recv_a = lax.ppermute(send_a, "head", swap)
    dpre, keep_p, send_p = call(
        functools.partial(back_kernel, blocks, chunk_p),
        [((hid, points), BF), ((peers, chunk_p, LANES), F32), ((peers, chunk_p, LANES), BF)],
        head, back, wot, slope, xt, hsum,
        scratch=[pltpu.VMEM((pieces, chunk_p, LANES), F32)],
        smem=1,
    )
    recv_p = lax.ppermute(send_p, "head", swap)
    (joined,) = call(join_kernel, [((peers, rows_a + chunk_p, LANES), BF)], keep_a, recv_a, keep_p, recv_p)
    scattered = lax.all_to_all(joined, crowd, 0, 0, tiled=True)
    (point_grad,) = call(point_grad_kernel, [((width, points), BF)], w_in, dpre)
    (summed,) = call(sum_kernel, [((peers, rows_a + chunk_p, LANES), BF)], scattered)
    mine = lax.all_to_all(summed, crowd, 0, 0, tiled=True)
    other = lax.ppermute(mine, "head", swap)
    square = ((width, width), F32)
    gin, gout, gq, gk, gv, gp, gain = call(
        functools.partial(unpack_kernel, chunk_a, rows_a, chunk_p),
        [((width, hid), F32), ((width, hid), F32), square, square, square, square, ((1, width), F32)],
        head, mine, other,
        scratch=[pltpu.VMEM((pieces, rows_a + chunk_p, LANES), BF)],
        smem=1,
    )
    return (
        attended.T[None], point_grad.T[None], gin, gout.T, gq, gk, gv, gp, gain.reshape(width),
    )


def solution(mesh):
    split = P(("groups", "design"), ("geom", "head"), None)
    placed = (split, P(("groups", "design"), ("geom", "head")), split, split, split) + (P(),) * 7
    grads = (P("groups", None),) * 6 + (P("groups"),)
    return jax.shard_map(
        on_device, mesh=mesh, in_specs=placed, out_specs=(split, split) + grads, check_vma=False
    )
```

time: 260 us -> 77.3 us (0.30)
  waiting for transfers between devices: 126 us -> 8.36 us
  blocking collectives: 60.4 us -> 28.8 us
  Pallas kernels: 0 us -> 25.9 us
  matrix products: 25.1 us -> 0 us
  between operations: 14 us -> 0.69 us
  local copies, waits for them, and re-layouts: 13.3 us -> 2.66 us
  other arithmetic: 6.46 us -> 0 us
  starting transfers between devices: 14.9 us -> 10.1 us
    psum x1 -> x0, waiting for transfers between devices: 60.8 us -> none  [on_device(): lax.psum((grad_in, grad_out, grad_query, grad_key, grad_value, grad_proj,...]
    unnamed x5 -> x0, waiting for transfers between devices: 57.2 us -> none
    psum x1 -> x0, blocking collectives: 32.4 us -> none  [on_device(): lax.psum((grad_in, grad_out, grad_query, grad_key, grad_value, grad_proj,...]
    all_to_all x0 -> x2, blocking collectives: none -> 28.8 us  [the longest x1 15.3 us: on_device(): scattered = lax.all_to_all(joined, crowd, 0, 0, tiled=True)]
    all_gather x2 -> x0, blocking collectives: 28 us -> none  [the longest x1 14 us: on_device(): lax.all_gather(key_local, ('geom', 'head'), axis=0, tiled=True)]
    pallas_call x0 -> x9, Pallas kernels: none -> 25.9 us  [call(): pl.pallas_call(kernel, out_shape=[jax.ShapeDtypeStruct(shape, dtype) for...]
    dot_general x26 -> x0, matrix products: 23.7 us -> none  [the longest x8 7.61 us: contract_rows(): lax.dot_general(first_arg, second_arg, (((0,), (0,)), ((), ())), precisio...]
    unnamed x34 -> x12, local copies, waits for them, and re-layouts: 10.7 us -> 2.66 us
  transfers between devices with their start and end apart: 6 -> 5, of which waited for: 5 -> 3; matrix products, arithmetic and copies ran while one was open for 7% -> 0% of each run, Pallas kernels for 0% -> 15%
where the time goes in v1:
time: 77.3 us; the launch traced here: 76.5 us
  blocking collectives  28.8 us (37%)
  Pallas kernels  25.9 us (34%)
  starting transfers between devices  10.1 us (13%)
  waiting for transfers between devices  8.36 us (11%)
  local copies, waits for them, and re-layouts  2.66 us (3%)
    pallas_call x9, Pallas kernels, call(): pl.pallas_call(kernel, out_shape=[jax.ShapeDtypeStruct(shape, dtype) for...  25.9 us
    all_to_all x1, blocking collectives, on_device(): scattered = lax.all_to_all(joined, crowd, 0, 0, tiled=True)  15.3 us
    all_to_all x1, blocking collectives, on_device(): mine = lax.all_to_all(summed, crowd, 0, 0, tiled=True)  13.6 us
    all_to_all x1, starting transfers between devices, on_device(): got = lax.all_to_all(send, team, 0, 0, tiled=True)  6.35 us
    all_to_all x1, waiting for transfers between devices, on_device(): got = lax.all_to_all(send, team, 0, 0, tiled=True)  4.2 us
    all_to_all x1, starting transfers between devices, on_device(): back = lax.all_to_all(rows_out, team, 0, 0, tiled=True)  3.36 us
    unnamed x12, local copies, waits for them, and re-layouts  2.66 us
    all_to_all x1, waiting for transfers between devices, on_device(): back = lax.all_to_all(rows_out, team, 0, 0, tiled=True)  2.59 us
  transfers between devices with their start and end apart: 5, of which 3 were waited for; matrix products, arithmetic and copies ran while one was open for 0% of the time, Pallas kernels for 15%

profile of v1, /device:TPU:0, one launch (start us, length us, event | category | flops | bytes accessed | tf_op | source)
XLA Modules:
  0.0 76.5 jit_solution(17163208401446809376)
XLA Ops:
  0.6 4.3 %shard_map.187 = (bf16[8,16,384]{2,1,0:T(8,128)(2,1)}, bf16[384,1536]{1,0:T(8,128)(2,1)}, f32[16,384]{1,0:T(8,128)}) custom-call(bf16[192,1536]{1,0:T(8,128)(2,1)} %bitcast.21, bf16[192,384]{1,0:T(8,128)(2,1)} %win_ref.3, bf16[192,384]{1,0:T(8,128)(2,1)} %bitcast.27, bf16[16,192]{1,0:T(8,128)(2,1)} %bitcast.30, s32[1,12]{1,0:T(1,128)} %id_ref.1), custom_call_target="tpu_custom_call" | custom-call | tf_op jit(solution)/shard_map/pallas_call | solution.py:32
  4.9 6.4 %all-to-all-start = ((bf16[8,16,384]{2,1,0:T(8,128)(2,1)}), bf16[8,16,384]{2,1,0:T(8,128)(2,1)S(1)}, u32[]{:S(2)}, u32[]{:S(2)}) async-start(bf16[8,16,384]{2,1,0:T(8,128)(2,1)} %get-tuple-element.36), calls=%async_computation | async-start | bytes 196608 | tf_op jit(solution)/shard_map/all_to_all | solution.py:339
  11.3 2.1 %shard_map.188 = (bf16[192,512]{1,0:T(8,128)(2,1)}, bf16[192,512]{1,0:T(8,128)(2,1)}) custom-call(bf16[192,512]{1,0:T(8,128)(2,1)} %bitcast.23, bf16[192,512]{1,0:T(8,128)(2,1)} %bitcast.25, bf16[192,192]{1,0:T(8,128)(2,1)} %wq_ref.1, bf16[192,192]{1,0:T(8,128)(2,1)} %wp_ref.3), custom_call_target="tpu_custom_call" | custom-call | tf_op jit(solution)/shard_map/pallas_call | solution.py:32
  13.4 4.2 %all-to-all-done.got_ref = bf16[8,16,384]{2,1,0:T(8,128)(2,1)S(1)} async-done(((bf16[8,16,384]{2,1,0:T(8,128)(2,1)}), bf16[8,16,384]{2,1,0:T(8,128)(2,1)S(1)}, u32[]{:S(2)}, u32[]{:S(2)}) %all-to-all-start) | async-done | bytes 98336 | tf_op jit(solution)/shard_map/all_to_all | solution.py:339
  17.6 0.0 copy-start.1
  17.6 0.6 copy-done.1
  18.2 4.1 %shard_map.189 = (bf16[8,16,192]{2,1,0:T(8,128)(2,1)}, bf16[128,192]{1,0:T(8,128)(2,1)}, bf16[192,128]{1,0:T(8,128)(2,1)}, bf16[192,128]{1,0:T(8,128)(2,1)}, bf1...) custom-call(bf16[8,16,384]{2,1,0:T(8,128)(2,1)} %copy-done.1, ...), custom_call_target="tpu_custom_call" | custom-call | tf_op jit(solution)/shard_map/pallas_call | solution.py:32
  22.4 3.4 %all-to-all-start.1 = ((bf16[8,16,192]{2,1,0:T(8,128)(2,1)}), bf16[8,16,192]{2,1,0:T(8,128)(2,1)S(1)}, u32[]{:S(2)}, u32[]{:S(2)}) async-start(bf16[8,16,192]{2,1,0:T(8,128)(2,1)} %get-tuple-element.48), calls=%async_computation.1 | async-start | bytes 131072 | tf_op jit(solution)/shard_map/all_to_all | solution.py:359
  25.7 2.9 %shard_map.190 = (bf16[192,512]{1,0:T(8,128)(2,1)}, f32[8,80,128]{2,1,0:T(8,128)}, bf16[8,80,128]{2,1,0:T(8,128)(2,1)}) custom-call(s32[1]{0:T(128)} %bitcast.head_ref, bf16[3,128,512]{2,1,0:T(8,128)(2,1)} %get-tuple-element.39.p_ref, bf16[3,128,512]{2,1,0:T(8,128)(2,1)} %get-tuple-element.40.ds_ref, bf16[192,128]{1,0:T(8,128)(2,1)} %get-tuple-element.41.k_ref, ...), custom_call_target="tpu_custom_call" | custom-call | tf_op jit(solution)/shard_map/pallas_call | solution.py:32
  28.6 0.4 collective-permute-start
  29.0 2.6 %all-to-all-done.1.got_ref = bf16[8,16,192]{2,1,0:T(8,128)(2,1)S(1)} async-done(((bf16[8,16,192]{2,1,0:T(8,128)(2,1)}), bf16[8,16,192]{2,1,0:T(8,128)(2,1)S(1)}, u32[]{:S(2)}, u32[]{:S(2)}) %all-to-all-start.1) | async-done | bytes 49184 | tf_op jit(solution)/shard_map/all_to_all | solution.py:359
  31.6 0.0 copy-start.3
  31.6 0.6 copy-done.3
  32.2 3.9 %shard_map.191 = (bf16[384,1536]{1,0:T(8,128)(2,1)}, f32[8,72,128]{2,1,0:T(8,128)}, bf16[8,72,128]{2,1,0:T(8,128)(2,1)}) custom-call(s32[1]{0:T(128)} %bitcast.head_ref, bf16[8,16,192]{2,1,0:T(8,128)(2,1)} %copy-done.3, bf16[192,384]{1,0:T(8,128)(2,1)} %bitcast.28, bf16[384,1536]{1,0:T(8,128)(2,1)} %get-tuple-element.49.slope_ref, ...), custom_call_target="tpu_custom_call" | custom-call | tf_op jit(solution)/shard_map/pallas_call | solution.py:32
  36.1 0.0 collective-permute-start.1
  36.1 0.0 collective-permute-done.ra_ref
  36.1 0.0 copy-start.4
  36.1 1.6 %collective-permute-done.1.rp_ref = bf16[8,72,128]{2,1,0:T(8,128)(2,1)S(1)} collective-permute-done((bf16[8,72,128]{2,1,0:T(8,128)(2,1)}, bf16[8,72,128]{2,1,0:T(8,128)(2,1)S(1)}, u32[]{:S(2)}, u32[]{:S(2)}) %collective-permute-start.1) | collective-permute-done | bytes 147488 | tf_op jit(solution)/shard_map/ppermute | solution.py:380
  37.7 0.0 copy-start.5
  37.7 0.0 copy-done.4
  37.7 0.7 copy-done.5
  38.3 2.0 %shard_map.193 = bf16[8,152,128]{2,1,0:T(8,128)(2,1)} custom-call(f32[8,80,128]{2,1,0:T(8,128)} %get-tuple-element.52.ka_ref, bf16[8,80,128]{2,1,0:T(8,128)(2,1)} %copy-done.4, f32[8,72,128]{2,1,0:T(8,128)} %get-tuple-element.54.kp_ref, bf16[8,72,128]{2,1,0:T(8,128)(2,1)} %copy-done.5), custom_call_target="tpu_custom_call" | custom-call | tf_op jit(solution)/shard_map/pallas_call | solution.py:32
  40.3 15.3 %all_to_all.20.got_ref = bf16[8,152,128]{2,1,0:T(8,128)(2,1)} all-to-all(bf16[8,152,128]{2,1,0:T(8,128)(2,1)} %shard_map.193), channel_id=1, replica_groups=mesh['groups'=2,'geom'=4,'design'=2,'head'=2] {'geom','design'}, dimensions={0} | all-to-all | bytes 622592 | tf_op jit(solution)/shard_map/all_to_all | solution.py:382
  55.6 1.7 %shard_map.194 = bf16[8,152,128]{2,1,0:T(8,128)(2,1)} custom-call(bf16[8,152,128]{2,1,0:T(8,128)(2,1)} %all_to_all.20.got_ref), custom_call_target="tpu_custom_call" | custom-call | tf_op jit(solution)/shard_map/pallas_call | solution.py:32
  57.3 13.6 %all_to_all.21.mine_ref = bf16[8,152,128]{2,1,0:T(8,128)(2,1)S(1)} all-to-all(bf16[8,152,128]{2,1,0:T(8,128)(2,1)} %shard_map.194), channel_id=1, replica_groups=mesh['groups'=2,'geom'=4,'design'=2,'head'=2] {'geom','design'}, dimensions={0} | all-to-all | bytes 622592 | tf_op jit(solution)/shard_map/all_to_all | solution.py:385
  70.9 0.0 copy-start
  70.9 0.0 collective-permute-start.2
  70.9 2.7 %shard_map.192 = bf16[192,1536]{1,0:T(8,128)(2,1)} custom-call(bf16[192,384]{1,0:T(8,128)(2,1)} %win_ref.3, bf16[384,1536]{1,0:T(8,128)(2,1)} %get-tuple-element.51.dpre_ref), custom_call_target="tpu_custom_call" | custom-call | tf_op jit(solution)/shard_map/pallas_call | solution.py:32
  73.6 0.0 collective-permute-done.2.other_ref
  73.6 0.0 copy-done
  73.6 0.0 copy-start.2
  73.6 0.7 copy-done.2
  74.3 2.2 %shard_map.195 = (f32[192,384]{1,0:T(8,128)}, f32[192,384]{1,0:T(8,128)}, f32[192,192]{1,0:T(8,128)}, f32[192,192]{1,0:T(8,128)}, f32[192,192]{1,0:T(8,128)}, /*index=5*/f32[192,192]{1,0:T(8,128)}, f32[1,192]{1,0:T(1,128)}) custom-call(s32[1]{0:T(128)} %bitcast.head_ref, bf16[8,152,128]{2,1,0:T(8,128)(2,1)} %copy-done, bf16[8,152,128]{2,1,0:T(8,128)(2,1)} %copy-done.2), custom_call_target="tpu_custom_call" | custom-call | tf_op jit(solution)/shard_map/pallas_call | solution.py:32
Async XLA Ops:
  4.9 12.7 %all-to-all-start = ((bf16[8,16,384]{2,1,0:T(8,128)(2,1)}), bf16[8,16,384]{2,1,0:T(8,128)(2,1)S(1)}, u32[]{:S(2)}, u32[]{:S(2)}) async-start(bf16[8,16,384]{2,1,0:T(8,128)(2,1)} %get-tuple-element.36), calls=%async_computation | async-start | bytes 196608 | tf_op jit(solution)/shard_map/all_to_all | solution.py:339
  17.6 0.6 copy-start.1
  22.4 9.2 %all-to-all-start.1 = ((bf16[8,16,192]{2,1,0:T(8,128)(2,1)}), bf16[8,16,192]{2,1,0:T(8,128)(2,1)S(1)}, u32[]{:S(2)}, u32[]{:S(2)}) async-start(bf16[8,16,192]{2,1,0:T(8,128)(2,1)} %get-tuple-element.48), calls=%async_computation.1 | async-start | bytes 131072 | tf_op jit(solution)/shard_map/all_to_all | solution.py:359
  28.6 7.5 %collective-permute-start = (bf16[8,80,128]{2,1,0:T(8,128)(2,1)}, bf16[8,80,128]{2,1,0:T(8,128)(2,1)S(1)}, u32[]{:S(2)}, u32[]{:S(2)}) collective-permute-start(bf16[8,80,128]{2,1,0:T(8,128)(2,1)} %get-tuple-element.53), channel_id=1, source_target_pairs={{0,1},{1,0},{2,3},{3,2},{4,5},{5,4},{6,7},{7,6},{8,9},{9,8},{10,11... | collective-permute-start | bytes 491528 | tf_op jit(solution)/shard_map/ppermute | solution.py:372
  31.6 0.6 copy-start.3
  36.1 1.6 %collective-permute-start.1 = (bf16[8,72,128]{2,1,0:T(8,128)(2,1)}, bf16[8,72,128]{2,1,0:T(8,128)(2,1)S(1)}, u32[]{:S(2)}, u32[]{:S(2)}) collective-permute-start(bf16[8,72,128]{2,1,0:T(8,128)(2,1)} %get-tuple-element.55), channel_id=1, source_target_pairs={{0,1},{1,0},{2,3},{3,2},{4,5},{5,4},{6,7},{7,6},{8,9},{9,8},{10,11... | collective-permute-start | bytes 442376 | tf_op jit(solution)/shard_map/ppermute | solution.py:380
  36.1 1.6 %copy-start.4 = (bf16[8,80,128]{2,1,0:T(8,128)(2,1)}, bf16[8,80,128]{2,1,0:T(8,128)(2,1)S(1)}, u32[]{:S(2)}) copy-start(bf16[8,80,128]{2,1,0:T(8,128)(2,1)S(1)} %collective-permute-done.ra_ref) | copy-start | bytes 491524
  37.7 0.7 copy-start.5
  70.9 2.7 %copy-start = (bf16[8,152,128]{2,1,0:T(8,128)(2,1)}, bf16[8,152,128]{2,1,0:T(8,128)(2,1)S(1)}, u32[]{:S(2)}) copy-start(bf16[8,152,128]{2,1,0:T(8,128)(2,1)S(1)} %all_to_all.21.mine_ref) | copy-start | bytes 933892
  70.9 2.7 %collective-permute-start.2 = (bf16[8,152,128]{2,1,0:T(8,128)(2,1)S(1)}, bf16[8,152,128]{2,1,0:T(8,128)(2,1)S(1)}, u32[]{:S(2)}, u32[]{:S(2)}) collective-permute-start(bf16[8,152,128]{2,1,0:T(8,128)(2,1)S(1)} %all_to_all.21.mine_ref), channel_id=1, source_target_pairs={{0,1},{1,0},{2,3},{3,2},{4,5},{5,4},{6,7},{7,6},{8,9},{9,8},{10,11... | collective-permute-start | bytes 933896 | tf_op jit(solution)/shard_map/ppermute | solution.py:386
  73.6 0.7 copy-start.2

commit v2 on v1

--- a/solution.py
+++ b/solution.py
@@ -11,6 +11,7 @@
 LANES = 128
 DIGIT = 128
 INTERPRET = False
+VMEM_LIMIT = 24 << 20
 BF = jnp.bfloat16
 F32 = jnp.float32
 GELU_C = 0.7978845608028654
@@ -26,17 +27,47 @@
     return high, (x - high.astype(F32)).astype(BF)
 
 
-def call(kernel, outs, *args, scratch=(), smem=0):
+class Held:
+    def __init__(self, value, space):
+        self.value, self.space = value, space
+
+
+def near(*values):
+    return tuple(Held(value, pltpu.VMEM) for value in values)
+
+
+def call(kernel, outs, *args, scratch=(), smem=0, final=(), raw=()):
+    held = [Held(arg, None) for arg in args[:smem]]
+    held += [arg if isinstance(arg, Held) else Held(arg, pltpu.HBM) for arg in args[smem:]]
     specs = [pl.BlockSpec(memory_space=pltpu.SMEM)] * smem
-    specs += [pl.BlockSpec(memory_space=pltpu.VMEM)] * (len(args) - smem)
+    for arg in held[smem:]:
+        near_spec = pl.BlockSpec(memory_space=pltpu.VMEM)
+        specs.append(near_spec if arg.space is pltpu.VMEM else pl.BlockSpec())
+    held += [arg if isinstance(arg, Held) else Held(arg, pltpu.HBM) for arg in raw]
+    specs += [pl.BlockSpec(memory_space=pl.ANY)] * len(raw)
+    operands = [
+        arg.value
+        if INTERPRET or arg.space is None
+        else pltpu.with_memory_space_constraint(arg.value, arg.space)
+        for arg in held
+    ]
     return pl.pallas_call(
         kernel,
-        out_shape=[jax.ShapeDtypeStruct(shape, dtype) for shape, dtype in outs],
+        out_shape=[
+            jax.ShapeDtypeStruct(shape, dtype)
+            if INTERPRET
+            else (pltpu.HBM if place in final else pltpu.VMEM)(shape, dtype)
+            for place, (shape, dtype) in enumerate(outs)
+        ],
         in_specs=specs,
-        out_specs=[pl.BlockSpec(memory_space=pltpu.VMEM)] * len(outs),
+        out_specs=[
+            pl.BlockSpec() if place in final else pl.BlockSpec(memory_space=pltpu.VMEM)
+            for place in range(len(outs))
+        ],
         scratch_shapes=list(scratch),
+        compiler_params=pltpu.CompilerParams(vmem_limit_bytes=VMEM_LIMIT),
         interpret=INTERPRET,
-    )(*args)
+    )(*operands)
 
 
 def round_up(n, k):
@@ -47,7 +78,14 @@
     return lax.broadcasted_iota(jnp.int32, shape, dim)
 
 
-def pool_kernel(blocks, x_ref, win_ref, wout_ref, anchor_ref, id_ref, send_ref, slope_ref, hsum_ref):
+def gelu_terms(win, x):
+    pre = dg(win, x, 0, 0)
+    square = pre * pre
+    tanh = jnp.tanh(pre * (GELU_C + (GELU_C * GELU_A) * square))
+    return pre, square, tanh
+
+
+def pool_kernel(blocks, x_ref, win_ref, wout_ref, anchor_ref, id_ref, send_ref, hsum_ref):
     width, points = x_ref.shape
     size = points // blocks
     hid = win_ref.shape[1]
@@ -56,14 +94,9 @@
     step = 2 if blocks % 2 == 0 else 1
     hsum = jnp.zeros((round_up(blocks, 8), hid), F32)
     for first in range(0, blocks, step):
-        cols = pl.ds(first * size, step * size)
-        pre = dg(win, x_ref[:, cols], 0, 0)
-        square = pre * pre
-        tanh = jnp.tanh(pre * (GELU_C + (GELU_C * GELU_A) * square))
-        half = 0.5 + 0.5 * tanh
-        hidden = (pre * half).astype(BF)
-        slope = half + pre * ((half * (1.0 - tanh)) * (GELU_C + (3.0 * GELU_C * GELU_A) * square))
-        slope_ref[:, cols] = slope.astype(slope_ref.dtype)
+        pre, _, tanh = gelu_terms(win, x_ref[:, pl.ds(first * size, step * size)])
+        half = 0.5 * pre
+        hidden = (half + half * tanh).astype(BF)
         shape = (hsum.shape[0], step * size)
         pick = (iota(shape, 0) == first + iota(shape, 1) // size).astype(F32).astype(BF)
         hsum = hsum + dg(pick, hidden, 1, 1)
@@ -96,9 +129,23 @@
         send_ref[owner] = packed
 
 
-def query_kernel(x_ref, g_ref, wq_ref, wp_ref, q_ref, dmix_ref):
+def query_kernel(
+    blocks, x_ref, g_ref, wq_ref, wp_ref, wk_ref, wv_ref, gain_ref, xp_ref, win_ref,
+    q_ref, dmix_ref, wk_out, wv_out, gain_out, slope_ref,
+):
+    wk_out[...] = wk_ref[...]
+    wv_out[...] = wv_ref[...]
+    gain_out[...] = gain_ref[...]
     q_ref[...] = dg(wq_ref[...], x_ref[...], 0, 0).astype(BF)
     dmix_ref[...] = dg(wp_ref[...], g_ref[...], 1, 0).astype(BF)
+    win = win_ref[...]
+    points = xp_ref.shape[1]
+    step = points // blocks * (2 if blocks % 2 == 0 else 1)
+    for first in range(0, points, step):
+        pre, square, tanh = gelu_terms(win, xp_ref[:, pl.ds(first, step)])
+        half = 0.5 + 0.5 * tanh
+        slope = half + pre * ((half * (1.0 - tanh)) * (GELU_C + (3.0 * GELU_C * GELU_A) * square))
+        slope_ref[:, pl.ds(first, step)] = slope.astype(BF)
 
 
 def attend_kernel(
@@ -203,8 +250,20 @@
 
 def finish_kernel(
     chunk, head_ref, p_ref, ds_ref, k_ref, v_ref, kt_ref, vt_ref, normed_ref, gain_ref, x_ref, g_ref,
-    wp_ref, out_ref, keep_ref, send_ref, mixed_ref, dq_ref, pack_ref,
+    wp_ref, *refs,
 ):
+    count = (len(refs) - 6) // 2
+    out_ref, keep_ref, send_ref = refs[count : count + 3]
+    mixed_ref, dq_ref, pack_ref, sems = refs[-4:]
+    points = refs[0].shape[1]
+    both = refs[count + 3]
+    targets = [both.at[:, :points], both.at[:, points:]] + list(refs[count + 4 : -4])
+    copies = [
+        pltpu.make_async_copy(source, target, sems.at[place])
+        for place, (source, target) in enumerate(zip(refs[:count], targets))
+    ]
+    for copy in copies:
+        copy.start()
     width = k_ref.shape[0]
     depth = width // HEADS
     for head in range(HEADS):
@@ -229,14 +288,19 @@
         [gain[:, LANES:], jnp.zeros((1, LANES - rest), F32)], axis=1
     )
     swap_halves(head_ref, pack_ref, keep_ref, send_ref)
+    for copy in copies:
+        copy.wait()
 
 
 def back_kernel(
-    blocks, chunk, head_ref, got_ref, wout_ref, slope_ref, x_ref, hsum_ref,
-    dpre_ref, keep_ref, send_ref, pack_ref,
+    blocks, chunk, head_ref, got_ref, both_ref, slope_ref, hsum_ref, *refs,
 ):
-    width, points = x_ref.shape
+    dpre_ref, keep_ref, send_ref, pack_ref = refs[-4:]
+    width = both_ref.shape[0]
+    points = slope_ref.shape[1]
     size = points // blocks
+    x_ref = both_ref.at[:, :points]
+    wout_ref = both_ref.at[:, points:]
     grad = jnp.sum(got_ref[...].astype(F32), axis=0)[: hsum_ref.shape[0]].astype(BF)
     dhid = dg(wout_ref[...], grad, 0, 1)
     for block in range(blocks):
@@ -253,17 +317,18 @@
     swap_halves(head_ref, pack_ref, keep_ref, send_ref)
 
 
-def point_grad_kernel(win_ref, dpre_ref, out_ref):
+def point_grad_kernel(win_ref, dpre_ref, after_ref, out_ref):
     out_ref[...] = dg(win_ref[...], dpre_ref[...], 1, 0).astype(BF)
 
 
-def join_kernel(ka_ref, ra_ref, kp_ref, rp_ref, out_ref):
+def join_kernel(ka_ref, ra_ref, kp_ref, rp_ref, after_ref, out_ref):
     rows = ka_ref.shape[1]
-    out_ref[:, :rows, :] = (ka_ref[...] + ra_ref[...].astype(F32)).astype(BF)
-    out_ref[:, rows:, :] = (kp_ref[...] + rp_ref[...].astype(F32)).astype(BF)
-
-
-def sum_kernel(got_ref, out_ref):
+    out_ref[:, :rows, :] = (ka_ref[...].astype(F32) + ra_ref[...].astype(F32)).astype(BF)
+    out_ref[:, rows:, :] = (kp_ref[...].astype(F32) + rp_ref[...].astype(F32)).astype(BF)
+
+
+def sum_kernel(got_ref, *refs):
+    out_ref = refs[-1]
     total = jnp.sum(got_ref[...].astype(F32), axis=0).astype(BF)
     for peer in range(out_ref.shape[0]):
         out_ref[peer] = total
@@ -331,14 +396,25 @@
     rows_a = chunk_a + 8
     chunk_p = 2 * width * hid // LANES // pieces
 
-    send, slope, hsum = call(
+    send, hsum = call(
         functools.partial(pool_kernel, blocks),
-        [((owners, rows, 2 * width), BF), ((hid, points), BF), ((round_up(blocks, 8), hid), F32)],
+        [((owners, rows, 2 * width), BF), ((round_up(blocks, 8), hid), F32)],
         xt, w_in, wot, anchor_feats[0], block_anchor,
+        final=(1,),
     )
     got = lax.all_to_all(send, team, 0, 0, tiled=True)
-    qp, dmix = call(
-        query_kernel, [((width, queries), BF), ((width, queries), BF)], qt, gt, w_query, w_proj
+    qp, dmix, wk, wv, gain_row, slope = call(
+        functools.partial(query_kernel, blocks),
+        [
+            ((width, queries), BF),
+            ((width, queries), BF),
+            ((width, width), BF),
+            ((width, width), BF),
+            ((1, width), F32),
+            ((hid, points), BF),
+        ],
+        qt, gt, w_query, w_proj, w_key, w_value, norm_gain.reshape(1, width), xt, w_in,
+        final=(5,),
     )
     pair_shape = (HEADS, anchors, queries)
     rows_out, normed, keys, values, probs, dscore, kt, vt, gain_part = call(
@@ -354,43 +430,61 @@
             ((width, anchors), BF),
             ((1, width), F32),
         ],
-        got, norm_gain.reshape(1, width), w_key, w_value, qp, dmix,
+        *near(got, gain_row, wk, wv, qp, dmix),
     )
     back = lax.all_to_all(rows_out, team, 0, 0, tiled=True)
-    attended, keep_a, send_a = call(
+    attended, keep_a, send_a, both, slope, hsum, win = call(
         functools.partial(finish_kernel, chunk_a),
-        [((width, queries), BF), ((peers, rows_a, LANES), F32), ((peers, rows_a, LANES), BF)],
-        head, probs, dscore, keys, values, kt, vt, normed, gain_part, qt, gt, w_proj,
+        [
+            ((width, queries), BF),
+            ((peers, rows_a, LANES), BF),
+            ((peers, rows_a, LANES), BF),
+            ((width, points + hid), BF),
+            ((hid, points), BF),
+            (hsum.shape, F32),
+            ((width, hid), BF),
+        ],
+        head, *near(probs, dscore, keys, values, kt, vt, normed, gain_part), qt, gt, w_proj,
+        raw=(xt, wot, slope, hsum, w_in),
         scratch=[
             pltpu.VMEM((width, queries), BF),
             pltpu.VMEM((width, queries), BF),
             pltpu.VMEM((pieces, rows_a, LANES), F32),
+            pltpu.SemaphoreType.DMA((5,)),
         ],
         smem=1,
+        final=(0,),
     )
     swap = [(0, 1), (1, 0)]
+    shape_p = ((peers, chunk_p, LANES), BF)
+    shape_all = ((peers, rows_a + chunk_p, LANES), BF)
     recv_a = lax.ppermute(send_a, "head", swap)
     dpre, keep_p, send_p = call(
         functools.partial(back_kernel, blocks, chunk_p),
-        [((hid, points), BF), ((peers, chunk_p, LANES), F32), ((peers, chunk_p, LANES), BF)],
-        head, back, wot, slope, xt, hsum,
+        [((hid, points), BF), shape_p, shape_p],
+        head, *near(back, both, slope, hsum),
         scratch=[pltpu.VMEM((pieces, chunk_p, LANES), F32)],
         smem=1,
     )
     recv_p = lax.ppermute(send_p, "head", swap)
-    (joined,) = call(join_kernel, [((peers, rows_a + chunk_p, LANES), BF)], keep_a, recv_a, keep_p, recv_p)
+    (point_grad,) = call(
+        point_grad_kernel, [((width, points), BF)], *near(win, dpre), final=(0,), raw=near(send_p)
+    )
+    (joined,) = call(
+        join_kernel, [shape_all], *near(keep_a, recv_a, keep_p, recv_p), raw=(point_grad,)
+    )
     scattered = lax.all_to_all(joined, crowd, 0, 0, tiled=True)
-    (point_grad,) = call(point_grad_kernel, [((width, points), BF)], w_in, dpre)
-    (summed,) = call(sum_kernel, [((peers, rows_a + chunk_p, LANES), BF)], scattered)
+    (summed,) = call(sum_kernel, [shape_all], *near(scattered))
     mine = lax.all_to_all(summed, crowd, 0, 0, tiled=True)
     other = lax.ppermute(mine, "head", swap)
     square = ((width, width), F32)
     gin, gout, gq, gk, gv, gp, gain = call(
         functools.partial(unpack_kernel, chunk_a, rows_a, chunk_p),
         [((width, hid), F32), ((width, hid), F32), square, square, square, square, ((1, width), F32)],
-        head, mine, other,
+        head, *near(mine, other),
         scratch=[pltpu.VMEM((pieces, rows_a + chunk_p, LANES), BF)],
         smem=1,
+        final=range(7),
     )
     return (
         attended.T[None], point_grad.T[None], gin, gout.T, gq, gk, gv, gp, gain.reshape(width),

time: 77.3 us -> 63.5 us (0.82)
  Pallas kernels: 25.9 us -> 18.1 us
  local copies, waits for them, and re-layouts: 2.66 us -> 0 us
  waiting for transfers between devices: 8.36 us -> 6.03 us
  blocking collectives: 28.8 us -> 28 us
    pallas_call x9, Pallas kernels: 25.9 us -> 18.1 us  [call(): pl.pallas_call(kernel, out_shape=[jax.ShapeDtypeStruct(shape, dtype) if I...]
    unnamed x12 -> x0, local copies, waits for them, and re-layouts: 2.66 us -> none
    all_to_all x1, waiting for transfers between devices: 4.2 us -> 2.41 us  [on_device(): got = lax.all_to_all(send, team, 0, 0, tiled=True)]
    ppermute x1, waiting for transfers between devices: 0.01 us -> 1.6 us  [on_device(): other = lax.ppermute(mine, 'head', swap)]
    ppermute x1, waiting for transfers between devices: 1.56 us -> 0.06 us  [on_device(): recv_p = lax.ppermute(send_p, 'head', swap)]
  transfers between devices with their start and end apart: 5 -> 5, of which waited for: 3 -> 4; matrix products, arithmetic and copies ran while one was open for 0% -> 0% of each run, Pallas kernels for 15% -> 16%
where the time goes in v2:
time: 63.5 us; the launch traced here: 63.1 us
  blocking collectives  28 us (44%)
  Pallas kernels  18.1 us (29%)
  starting transfers between devices  10.2 us (16%)
  waiting for transfers between devices  6.03 us (9%)
  between operations  0.69 us (1%)
    pallas_call x9, Pallas kernels, call(): pl.pallas_call(kernel, out_shape=[jax.ShapeDtypeStruct(shape, dtype) if I...  18.1 us
    all_to_all x1, blocking collectives, on_device(): scattered = lax.all_to_all(joined, crowd, 0, 0, tiled=True)  14.8 us
    all_to_all x1, blocking collectives, on_device(): mine = lax.all_to_all(summed, crowd, 0, 0, tiled=True)  13.3 us
    all_to_all x1, starting transfers between devices, on_device(): got = lax.all_to_all(send, team, 0, 0, tiled=True)  6.35 us
    all_to_all x1, starting transfers between devices, on_device(): back = lax.all_to_all(rows_out, team, 0, 0, tiled=True)  3.35 us
    all_to_all x1, waiting for transfers between devices, on_device(): got = lax.all_to_all(send, team, 0, 0, tiled=True)  2.41 us
    all_to_all x1, waiting for transfers between devices, on_device(): back = lax.all_to_all(rows_out, team, 0, 0, tiled=True)  1.95 us
    ppermute x1, waiting for transfers between devices, on_device(): other = lax.ppermute(mine, 'head', swap)  1.6 us
  transfers between devices with their start and end apart: 5, of which 4 were waited for; matrix products, arithmetic and copies ran while one was open for 0% of the time, Pallas kernels for 16%

profile of v2, /device:TPU:0, one launch (start us, length us, event | category | flops | bytes accessed | tf_op | source)
XLA Modules:
  0.0 63.1 jit_solution(490343637928232354)
XLA Ops:
  0.6 3.8 %shard_map.187 = (bf16[8,16,384]{2,1,0:T(8,128)(2,1)}, f32[16,384]{1,0:T(8,128)}) custom-call(bf16[192,1536]{1,0:T(8,128)(2,1)} %bitcast.21, bf16[192,384]{1,0:T(8,128)(2,1)} %refs_4_.1, bf16[192,384]{1,0:T(8,128)(2,1)} %bitcast.29, bf16[16,192]{1,0:T(8,128)(2,1)} %bitcast.31, s32[1,12]{1,0:T(1,128)} %id_ref.1), custom_call_target="tpu_custom_call" | custom-call | tf_op jit(solution)/shard_map/pallas_call | solution.py:54
  4.4 6.4 %all-to-all-start = ((bf16[8,16,384]{2,1,0:T(8,128)(2,1)}), bf16[8,16,384]{2,1,0:T(8,128)(2,1)S(1)}, u32[]{:S(2)}, u32[]{:S(2)}) async-start(bf16[8,16,384]{2,1,0:T(8,128)(2,1)} %get-tuple-element.43), calls=%async_computation | async-start | bytes 196608 | tf_op jit(solution)/shard_map/all_to_all | solution.py:405
  10.8 3.9 %shard_map.188 = (bf16[192,512]{1,0:T(8,128)(2,1)S(1)}, bf16[192,512]{1,0:T(8,128)(2,1)S(1)}, bf16[192,192]{1,0:T(8,128)(2,1)S(1)}, bf16[192,192]{1,0:T(8,128)(2...) custom-call(bf16[192,512]{1,0:T(8,128)(2,1)} %bitcast.25, bf16[192,512]{1,0:T(8,128)(2,1)} %bitcast.27, ...), custom_call_target="tpu_custom_call" | custom-call | tf_op jit(solution)/shard_map/pallas_call | solution.py:54
  14.7 2.4 %all-to-all-done.got_ref = bf16[8,16,384]{2,1,0:T(8,128)(2,1)S(1)} async-done(((bf16[8,16,384]{2,1,0:T(8,128)(2,1)}), bf16[8,16,384]{2,1,0:T(8,128)(2,1)S(1)}, u32[]{:S(2)}, u32[]{:S(2)}) %all-to-all-start) | async-done | bytes 98336 | tf_op jit(solution)/shard_map/all_to_all | solution.py:405
  17.1 3.0 %shard_map.189 = (bf16[8,16,192]{2,1,0:T(8,128)(2,1)}, bf16[128,192]{1,0:T(8,128)(2,1)S(1)}, bf16[192,128]{1,0:T(8,128)(2,1)S(1)}, bf16[192,128]{1,0:T(8,128)(2,...) custom-call(bf16[8,16,384]{2,1,0:T(8,128)(2,1)S(1)} %all-to-all-done, ...), custom_call_target="tpu_custom_call" | custom-call | tf_op jit(solution)/shard_map/pallas_call | solution.py:54
  20.0 3.4 %all-to-all-start.1 = ((bf16[8,16,192]{2,1,0:T(8,128)(2,1)}), bf16[8,16,192]{2,1,0:T(8,128)(2,1)S(1)}, u32[]{:S(2)}, u32[]{:S(2)}) async-start(bf16[8,16,192]{2,1,0:T(8,128)(2,1)} %get-tuple-element.61), calls=%async_computation.1 | async-start | bytes 131072 | tf_op jit(solution)/shard_map/all_to_all | solution.py:435
  23.4 3.4 %shard_map.190 = (bf16[192,512]{1,0:T(8,128)(2,1)}, bf16[8,80,128]{2,1,0:T(8,128)(2,1)S(1)}, bf16[8,80,128]{2,1,0:T(8,128)(2,1)S(1)}, bf16[192,1920]{1,0:T(8,128...) custom-call(s32[1]{0:T(128)} %bitcast.head_ref, ...), custom_call_target="tpu_custom_call" | custom-call | tf_op jit(solution)/shard_map/pallas_call | solution.py:54
  26.8 0.5 collective-permute-start
  27.3 1.9 %all-to-all-done.1.got_ref = bf16[8,16,192]{2,1,0:T(8,128)(2,1)S(1)} async-done(((bf16[8,16,192]{2,1,0:T(8,128)(2,1)}), bf16[8,16,192]{2,1,0:T(8,128)(2,1)S(1)}, u32[]{:S(2)}, u32[]{:S(2)}) %all-to-all-start.1) | async-done | bytes 49184 | tf_op jit(solution)/shard_map/all_to_all | solution.py:435
  29.2 1.5 %shard_map.191 = (bf16[384,1536]{1,0:T(8,128)(2,1)S(1)}, bf16[8,72,128]{2,1,0:T(8,128)(2,1)S(1)}, bf16[8,72,128]{2,1,0:T(8,128)(2,1)S(1)}) custom-call(s32[1]{0:T(128)} %bitcast.head_ref, bf16[8,16,192]{2,1,0:T(8,128)(2,1)S(1)} %all-to-all-done.1.got_ref, bf16[192,1920]{1,0:T(8,128)(2,1)S(1)} %get-tuple-element.62.both_ref, ...), custom_call_target="tpu_custom_call" | custom-call | tf_op jit(solution)/shard_map/pallas_call | solution.py:54
  30.7 0.1 collective-permute-start.1
  30.8 1.3 %shard_map.192.after_ref = bf16[192,1536]{1,0:T(8,128)(2,1)} custom-call(bf16[192,384]{1,0:T(8,128)(2,1)S(1)} %get-tuple-element.60.win_ref, bf16[384,1536]{1,0:T(8,128)(2,1)S(1)} %get-tuple-element.65.dpre_ref, bf16[8,72,128]{2,1,0:T(8,128)(2,1)S(1)} %get-tuple-element.66.after_ref), custom_call_target="tpu_custom_call" | custom-call | tf_op jit(solution)/shard_map/pallas_call | solution.py:54
  32.1 0.0 collective-permute-done.ra_ref
  32.1 0.1 collective-permute-done.1.rp_ref
  32.1 0.1 shard_map.193
  32.2 14.8 %all_to_all.20.got_ref = bf16[8,152,128]{2,1,0:T(8,128)(2,1)S(1)} all-to-all(bf16[8,152,128]{2,1,0:T(8,128)(2,1)S(1)} %shard_map.193), channel_id=1, replica_groups=mesh['groups'=2,'geom'=4,'design'=2,'head'=2] {'geom','design'}, dimensions={0} | all-to-all | bytes 622592 | tf_op jit(solution)/shard_map/all_to_all | solution.py:476
  47.0 0.1 shard_map.194
  47.0 13.3 %all_to_all.21.mine_ref = bf16[8,152,128]{2,1,0:T(8,128)(2,1)S(1)} all-to-all(bf16[8,152,128]{2,1,0:T(8,128)(2,1)S(1)} %shard_map.194), channel_id=1, replica_groups=mesh['groups'=2,'geom'=4,'design'=2,'head'=2] {'geom','design'}, dimensions={0} | all-to-all | bytes 622592 | tf_op jit(solution)/shard_map/all_to_all | solution.py:478
  60.3 0.0 collective-permute-start.2
  60.3 1.6 %collective-permute-done.2.other_ref = bf16[8,152,128]{2,1,0:T(8,128)(2,1)S(1)} collective-permute-done((bf16[8,152,128]{2,1,0:T(8,128)(2,1)S(1)}, bf16[8,152,128]{2,1,0:T(8,128)(2,1)S(1)}, u32[]{:S(2)}, u32[]{:S(2)}) %collective-permute-start.2) | collective-permute-done | bytes 311328 | tf_op jit(solution)/shard_map/ppermute | solution.py:479
  61.9 1.1 %shard_map.195 = (f32[192,384]{1,0:T(8,128)}, f32[192,384]{1,0:T(8,128)}, f32[192,192]{1,0:T(8,128)}, f32[192,192]{1,0:T(8,128)}, f32[192,192]{1,0:T(8,128)}, /*index=5*/f32[192,192]{1,0:T(8,128)}, f32[1,192]{1,0:T(1,128)}) custom-call(s32[1]{0:T(128)} %bitcast.head_ref, bf16[8,152,128]{2,1,0:T(8,128)(2,1)S(1)} %all_to_all.21.mine_ref, ...), custom_call_target="tpu_custom_call" | custom-call | tf_op jit(solution)/shard_map/pallas_call | solution.py:54
Async XLA Ops:
  4.4 12.7 %all-to-all-start = ((bf16[8,16,384]{2,1,0:T(8,128)(2,1)}), bf16[8,16,384]{2,1,0:T(8,128)(2,1)S(1)}, u32[]{:S(2)}, u32[]{:S(2)}) async-start(bf16[8,16,384]{2,1,0:T(8,128)(2,1)} %get-tuple-element.43), calls=%async_computation | async-start | bytes 196608 | tf_op jit(solution)/shard_map/all_to_all | solution.py:405
  20.0 9.2 %all-to-all-start.1 = ((bf16[8,16,192]{2,1,0:T(8,128)(2,1)}), bf16[8,16,192]{2,1,0:T(8,128)(2,1)S(1)}, u32[]{:S(2)}, u32[]{:S(2)}) async-start(bf16[8,16,192]{2,1,0:T(8,128)(2,1)} %get-tuple-element.61), calls=%async_computation.1 | async-start | bytes 131072 | tf_op jit(solution)/shard_map/all_to_all | solution.py:435
  26.8 5.2 %collective-permute-start = (bf16[8,80,128]{2,1,0:T(8,128)(2,1)S(1)}, bf16[8,80,128]{2,1,0:T(8,128)(2,1)S(1)}, u32[]{:S(2)}, u32[]{:S(2)}) collective-permute-start(bf16[8,80,128]{2,1,0:T(8,128)(2,1)S(1)} %get-tuple-element.68), channel_id=1, source_target_pairs={{0,1},{1,0},{2,3},{3,2},{4,5},{5,4},{6,7},{7,6},{8,9},{9,8},{10,11... | collective-permute-start | bytes 491528 | tf_op jit(solution)/shard_map/ppermute | solution.py:461
  30.7 1.4 %collective-permute-start.1 = (bf16[8,72,128]{2,1,0:T(8,128)(2,1)S(1)}, bf16[8,72,128]{2,1,0:T(8,128)(2,1)S(1)}, u32[]{:S(2)}, u32[]{:S(2)}) collective-permute-start(bf16[8,72,128]{2,1,0:T(8,128)(2,1)S(1)} %get-tuple-element.66.after_ref), channel_id=1, source_target_pairs={{0,1},{1,0},{2,3},{3,2},{4,5},{5,4},{6,7},{7,6},{8,9},{9,8},{10,11... | collective-permute-start | bytes 442376 | tf_op jit(solution)/shard_map/ppermute | solution.py:469
  60.3 1.6 %collective-permute-start.2 = (bf16[8,152,128]{2,1,0:T(8,128)(2,1)S(1)}, bf16[8,152,128]{2,1,0:T(8,128)(2,1)S(1)}, u32[]{:S(2)}, u32[]{:S(2)}) collective-permute-start(bf16[8,152,128]{2,1,0:T(8,128)(2,1)S(1)} %all_to_all.21.mine_ref), channel_id=1, source_target_pairs={{0,1},{1,0},{2,3},{3,2},{4,5},{5,4},{6,7},{7,6},{8,9},{9,8},{10,11... | collective-permute-start | bytes 933896 | tf_op jit(solution)/shard_map/ppermute | solution.py:479

commit v3 on v2

--- a/solution.py
+++ b/solution.py
@@ -6,6 +6,7 @@
 from jax.experimental import pallas as pl
 from jax.experimental.pallas import tpu as pltpu
 from jax.sharding import PartitionSpec as P
+
 
 HEADS = 3
 LANES = 128
@@ -51,6 +52,10 @@
         else pltpu.with_memory_space_constraint(arg.value, arg.space)
         for arg in held
     ]
+    return build(kernel, outs, operands, specs, scratch, final)
+
+
+def build(kernel, outs, operands, specs, scratch, final):
     return pl.pallas_call(
         kernel,
         out_shape=[
@@ -92,14 +97,15 @@
     owners, rows, _ = send_ref.shape
     win = win_ref[...]
     step = 2 if blocks % 2 == 0 else 1
-    hsum = jnp.zeros((round_up(blocks, 8), hid), F32)
+    hsum = jnp.zeros((hid, round_up(blocks, 8)), F32)
     for first in range(0, blocks, step):
         pre, _, tanh = gelu_terms(win, x_ref[:, pl.ds(first * size, step * size)])
         half = 0.5 * pre
         hidden = (half + half * tanh).astype(BF)
-        shape = (hsum.shape[0], step * size)
-        pick = (iota(shape, 0) == first + iota(shape, 1) // size).astype(F32).astype(BF)
-        hsum = hsum + dg(pick, hidden, 1, 1)
+        shape = (step * size, hsum.shape[1])
+        pick = (iota(shape, 1) == first + iota(shape, 0) // size).astype(F32).astype(BF)
+        hsum = hsum + dg(hidden, pick, 1, 0)
+    hsum = hsum.T
     hsum_ref[...] = hsum
     high, low = split_bf(hsum)
     wout = wout_ref[...]
@@ -131,8 +137,11 @@
 
 def query_kernel(
     blocks, x_ref, g_ref, wq_ref, wp_ref, wk_ref, wv_ref, gain_ref, xp_ref, win_ref,
-    q_ref, dmix_ref, wk_out, wv_out, gain_out, slope_ref,
+    q_ref, dmix_ref, wk_out, wv_out, gain_out, x_out, g_out, wp_out, slope_ref,
 ):
+    x_out[...] = x_ref[...]
+    g_out[...] = g_ref[...]
+    wp_out[...] = wp_ref[...]
     wk_out[...] = wk_ref[...]
     wv_out[...] = wv_ref[...]
     gain_out[...] = gain_ref[...]
@@ -248,22 +257,26 @@
     send_ref[...] = scratch[pl.ds((1 - head) * half, half)].astype(send_ref.dtype)
 
 
-def finish_kernel(
-    chunk, head_ref, p_ref, ds_ref, k_ref, v_ref, kt_ref, vt_ref, normed_ref, gain_ref, x_ref, g_ref,
-    wp_ref, *refs,
-):
-    count = (len(refs) - 6) // 2
-    out_ref, keep_ref, send_ref = refs[count : count + 3]
-    mixed_ref, dq_ref, pack_ref, sems = refs[-4:]
-    points = refs[0].shape[1]
-    both = refs[count + 3]
-    targets = [both.at[:, :points], both.at[:, points:]] + list(refs[count + 4 : -4])
+def fetch_kernel(*refs):
+    *refs, sems = refs
+    count = len(refs) // 2
+    sources, (both, *rest) = refs[:count], refs[count + 1 :]
+    points = sources[0].shape[1]
+    targets = [both.at[:, :points], both.at[:, points:]] + rest
     copies = [
         pltpu.make_async_copy(source, target, sems.at[place])
-        for place, (source, target) in enumerate(zip(refs[:count], targets))
+        for place, (source, target) in enumerate(zip(sources, targets))
     ]
     for copy in copies:
         copy.start()
+    for copy in copies:
+        copy.wait()
+
+
+def finish_kernel(
+    chunk, head_ref, p_ref, ds_ref, k_ref, v_ref, kt_ref, vt_ref, normed_ref, gain_ref, x_ref, g_ref,
+    wp_ref, out_ref, keep_ref, send_ref, mixed_ref, dq_ref, pack_ref,
+):
     width = k_ref.shape[0]
     depth = width // HEADS
     for head in range(HEADS):
@@ -288,8 +301,6 @@
         [gain[:, LANES:], jnp.zeros((1, LANES - rest), F32)], axis=1
     )
     swap_halves(head_ref, pack_ref, keep_ref, send_ref)
-    for copy in copies:
-        copy.wait()
 
 
 def back_kernel(
@@ -321,30 +332,62 @@
     out_ref[...] = dg(win_ref[...], dpre_ref[...], 1, 0).astype(BF)
 
 
-def join_kernel(ka_ref, ra_ref, kp_ref, rp_ref, after_ref, out_ref):
-    rows = ka_ref.shape[1]
-    out_ref[:, :rows, :] = (ka_ref[...].astype(F32) + ra_ref[...].astype(F32)).astype(BF)
-    out_ref[:, rows:, :] = (kp_ref[...].astype(F32) + rp_ref[...].astype(F32)).astype(BF)
-
-
-def sum_kernel(got_ref, *refs):
-    out_ref = refs[-1]
-    total = jnp.sum(got_ref[...].astype(F32), axis=0).astype(BF)
-    for peer in range(out_ref.shape[0]):
-        out_ref[peer] = total
+def design_kernel(shares, share_ref, keep_ref, got_ref, *refs):
+    total_ref = refs[-1]
+    total = keep_ref[...].astype(F32) + got_ref[...].astype(F32)
+    total_ref[...] = total.reshape(total_ref.shape)
+    for shift in range(shares):
+        share = lax.rem(share_ref[0] + shift, shares)
+        refs[shift][...] = total_ref[:, pl.ds(share, 1)][:, 0].astype(BF)
+
+
+def join_kernel(shares, *refs):
+    _, out_ref = refs[-2:]
+    ka_ref, kp_ref, rp_ref = refs[:3]
+    total = ka_ref[...].astype(F32)
+    for ref in refs[3:-2]:
+        total = total + ref[...].astype(F32)
+    groups, rows, _ = total.shape
+    part = rows // shares
+    total = total.astype(BF)
+    for group in range(groups):
+        for share in range(shares):
+            out_ref[group * shares + share, :part, :] = total[group, share * part : (share + 1) * part]
+    out_ref[:, part:, :] = (kp_ref[...].astype(F32) + rp_ref[...].astype(F32)).astype(BF)
+
+
+def sum_kernel(shares, part, got_ref, out_ref):
+    peers = out_ref.shape[0]
+    for share in range(shares):
+        total = got_ref[share, :part, :].astype(F32)
+        for peer in range(share + shares, peers, shares):
+            total = total + got_ref[peer, :part, :].astype(F32)
+        total = total.astype(BF)
+        for peer in range(peers):
+            out_ref[peer, share * part : (share + 1) * part, :] = total
+    total = jnp.sum(got_ref[:, part:, :].astype(F32), axis=0).astype(BF)
+    for peer in range(peers):
+        out_ref[peer, shares * part :, :] = total
 
 
 def unpack_kernel(
-    chunk_a, rows_a, chunk_p, head_ref, mine_ref, other_ref,
+    shares, chunk_a, rows_a, chunk_p, head_ref, mine_ref, other_ref,
     gin_ref, gout_ref, gq_ref, gk_ref, gv_ref, gp_ref, gain_ref, all_ref,
 ):
     peers = mine_ref.shape[0]
     head = head_ref[0]
     all_ref[pl.ds(head * peers, peers)] = mine_ref[...]
     all_ref[pl.ds((1 - head) * peers, peers)] = other_ref[...]
+    part = rows_a // shares
 
     def read_a(index, offset, take):
-        return all_ref[index, offset : offset + take, :].astype(F32)
+        group, share = divmod(index, shares)
+
+        def read(source, start, count):
+            row = share * part + start
+            return all_ref[group * shares + source, row : row + count, :].astype(F32)
+
+        return get_rows(read, part, offset, take)
 
     def read_p(index, offset, take):
         return all_ref[index, rows_a + offset : rows_a + offset + take, :].astype(F32)
@@ -361,7 +404,7 @@
         squares[first][:, LANES:] = pair[:, :rest]
         squares[first + 1][:, LANES:] = pair[:, rest:]
         start += width
-    tail = all_ref[0, chunk_a:rows_a, :].astype(F32)
+    tail = read_a(0, chunk_a, 2)
     gain_ref[...] = jnp.concatenate([tail[:1], tail[1:2, :rest]], axis=1)
     start = 0
     for ref in (gin_ref, gout_ref):
@@ -390,10 +433,12 @@
     size = points // blocks
     anchors = owners * per_owner
     rows = round_up(max(per_owner, blocks + 2), 16)
+    shares = lax.axis_size("design")
     head = lax.axis_index("head").astype(jnp.int32).reshape(1)
+    share = lax.axis_index("design").astype(jnp.int32).reshape(1)
     pieces = 2 * peers
     chunk_a = 6 * width // pieces
-    rows_a = chunk_a + 8
+    rows_a = round_up(chunk_a + 2, 8 * shares)
     chunk_p = 2 * width * hid // LANES // pieces
 
     send, hsum = call(
@@ -403,7 +448,7 @@
         final=(1,),
     )
     got = lax.all_to_all(send, team, 0, 0, tiled=True)
-    qp, dmix, wk, wv, gain_row, slope = call(
+    qp, dmix, wk, wv, gain_row, qn, gn, wpn, slope = call(
         functools.partial(query_kernel, blocks),
         [
             ((width, queries), BF),
@@ -411,10 +456,13 @@
             ((width, width), BF),
             ((width, width), BF),
             ((1, width), F32),
+            ((width, queries), BF),
+            ((width, queries), BF),
+            ((width, width), BF),
             ((hid, points), BF),
         ],
         qt, gt, w_query, w_proj, w_key, w_value, norm_gain.reshape(1, width), xt, w_in,
-        final=(5,),
+        final=(8,),
     )
     pair_shape = (HEADS, anchors, queries)
     rows_out, normed, keys, values, probs, dscore, kt, vt, gain_part = call(
@@ -433,53 +481,69 @@
         *near(got, gain_row, wk, wv, qp, dmix),
     )
     back = lax.all_to_all(rows_out, team, 0, 0, tiled=True)
-    attended, keep_a, send_a, both, slope, hsum, win = call(
+    shape_a = ((peers, rows_a, LANES), BF)
+    attended, keep_a, send_a = call(
         functools.partial(finish_kernel, chunk_a),
-        [
-            ((width, queries), BF),
-            ((peers, rows_a, LANES), BF),
-            ((peers, rows_a, LANES), BF),
-            ((width, points + hid), BF),
-            ((hid, points), BF),
-            (hsum.shape, F32),
-            ((width, hid), BF),
-        ],
-        head, *near(probs, dscore, keys, values, kt, vt, normed, gain_part), qt, gt, w_proj,
-        raw=(xt, wot, slope, hsum, w_in),
+        [((width, queries), BF), shape_a, shape_a],
+        head, *near(probs, dscore, keys, values, kt, vt, normed, gain_part, qn, gn, wpn),
         scratch=[
             pltpu.VMEM((width, queries), BF),
             pltpu.VMEM((width, queries), BF),
             pltpu.VMEM((pieces, rows_a, LANES), F32),
-            pltpu.SemaphoreType.DMA((5,)),
         ],
         smem=1,
         final=(0,),
     )
+    both, slope, hsum, win = call(
+        fetch_kernel,
+        [((width, points + hid), BF), ((hid, points), BF), (hsum.shape, F32), ((width, hid), BF)],
+        scratch=[pltpu.SemaphoreType.DMA((5,))],
+        raw=(xt, wot, slope, hsum, w_in) + near(send_a),
+    )
     swap = [(0, 1), (1, 0)]
     shape_p = ((peers, chunk_p, LANES), BF)
-    shape_all = ((peers, rows_a + chunk_p, LANES), BF)
     recv_a = lax.ppermute(send_a, "head", swap)
+    groups = peers // shares
+    shape_d = ((groups, rows_a, LANES), BF)
+    keep_d, *sends_d = call(
+        functools.partial(design_kernel, shares),
+        [shape_d] * shares,
+        share, *near(keep_a, recv_a),
+        scratch=[pltpu.VMEM((groups, shares, rows_a, LANES), F32)],
+        smem=1,
+    )
+    recvs_d = [
+        lax.ppermute(send, "design", [(i, (i + shift) % shares) for i in range(shares)])
+        for shift, send in enumerate(sends_d, 1)
+    ]
     dpre, keep_p, send_p = call(
         functools.partial(back_kernel, blocks, chunk_p),
         [((hid, points), BF), shape_p, shape_p],
         head, *near(back, both, slope, hsum),
         scratch=[pltpu.VMEM((pieces, chunk_p, LANES), F32)],
         smem=1,
+        raw=near(keep_d),
     )
     recv_p = lax.ppermute(send_p, "head", swap)
     (point_grad,) = call(
         point_grad_kernel, [((width, points), BF)], *near(win, dpre), final=(0,), raw=near(send_p)
     )
     (joined,) = call(
-        join_kernel, [shape_all], *near(keep_a, recv_a, keep_p, recv_p), raw=(point_grad,)
+        functools.partial(join_kernel, shares),
+        [((peers, rows_a // shares + chunk_p, LANES), BF)],
+        *near(keep_d, keep_p, recv_p, *recvs_d), raw=(point_grad,),
     )
     scattered = lax.all_to_all(joined, crowd, 0, 0, tiled=True)
-    (summed,) = call(sum_kernel, [shape_all], *near(scattered))
+    (summed,) = call(
+        functools.partial(sum_kernel, shares, rows_a // shares),
+        [((peers, rows_a + chunk_p, LANES), BF)],
+        *near(scattered),
+    )
     mine = lax.all_to_all(summed, crowd, 0, 0, tiled=True)
     other = lax.ppermute(mine, "head", swap)
     square = ((width, width), F32)
     gin, gout, gq, gk, gv, gp, gain = call(
-        functools.partial(unpack_kernel, chunk_a, rows_a, chunk_p),
+        functools.partial(unpack_kernel, shares, chunk_a, rows_a, chunk_p),
         [((width, hid), F32), ((width, hid), F32), square, square, square, square, ((1, width), F32)],
         head, *near(mine, other),
         scratch=[pltpu.VMEM((pieces, rows_a + chunk_p, LANES), BF)],
@@ -495,6 +559,7 @@
     split = P(("groups", "design"), ("geom", "head"), None)
     placed = (split, P(("groups", "design"), ("geom", "head")), split, split, split) + (P(),) * 7
     grads = (P("groups", None),) * 6 + (P("groups"),)
+
     return jax.shard_map(
         on_device, mesh=mesh, in_specs=placed, out_specs=(split, split) + grads, check_vma=False
     )

time: 63.5 us -> 64.3 us (1.013)
  waiting for transfers between devices: 6.03 us -> 10.2 us
  blocking collectives: 28 us -> 24.5 us
  starting transfers between devices: 10.2 us -> 11.3 us
  Pallas kernels: 18.1 us -> 17.1 us
    all_to_all x1, blocking collectives: 14.8 us -> 11 us  [on_device(): scattered = lax.all_to_all(joined, crowd, 0, 0, tiled=True)]
    all_to_all x1, waiting for transfers between devices: 1.95 us -> 4.19 us  [on_device(): back = lax.all_to_all(rows_out, team, 0, 0, tiled=True)]
    ppermute x0 -> x1, waiting for transfers between devices: none -> 2 us  [on_device(): lax.ppermute(send, 'design', [(i, (i + shift) % shares) for i in range(sh...]
    ppermute x0 -> x1, starting transfers between devices: none -> 1.55 us  [on_device(): lax.ppermute(send, 'design', [(i, (i + shift) % shares) for i in range(sh...]
    pallas_call x9 -> x11, Pallas kernels: 18.1 us -> 17.1 us  [build(): pl.pallas_call(kernel, out_shape=[jax.ShapeDtypeStruct(shape, dtype) if I...]
  transfers between devices with their start and end apart: 5 -> 6, of which waited for: 4 -> 4; matrix products, arithmetic and copies ran while one was open for 0% -> 0% of each run, Pallas kernels for 16% -> 11%
where the time goes in v3:
time: 64.3 us; the launch traced here: 63.8 us
  blocking collectives  24.5 us (38%)
  Pallas kernels  17.1 us (27%)
  starting transfers between devices  11.3 us (18%)
  waiting for transfers between devices  10.2 us (16%)
  between operations  0.71 us (1%)
    pallas_call x11, Pallas kernels, build(): pl.pallas_call(kernel, out_shape=[jax.ShapeDtypeStruct(shape, dtype) if I...  17.1 us
    all_to_all x1, blocking collectives, on_device(): mine = lax.all_to_all(summed, crowd, 0, 0, tiled=True)  13.5 us
    all_to_all x1, blocking collectives, on_device(): scattered = lax.all_to_all(joined, crowd, 0, 0, tiled=True)  11 us
    all_to_all x1, starting transfers between devices, on_device(): got = lax.all_to_all(send, team, 0, 0, tiled=True)  6.35 us
    all_to_all x1, waiting for transfers between devices, on_device(): back = lax.all_to_all(rows_out, team, 0, 0, tiled=True)  4.19 us
    all_to_all x1, starting transfers between devices, on_device(): back = lax.all_to_all(rows_out, team, 0, 0, tiled=True)  3.35 us
    all_to_all x1, waiting for transfers between devices, on_device(): got = lax.all_to_all(send, team, 0, 0, tiled=True)  2.38 us
    ppermute x1, waiting for transfers between devices, on_device(): lax.ppermute(send, 'design', [(i, (i + shift) % shares) for i in range(sh...  2 us
  transfers between devices with their start and end apart: 6, of which 4 were waited for; matrix products, arithmetic and copies ran while one was open for 0% of the time, Pallas kernels for 11%

profile of v3, /device:TPU:0, one launch (start us, length us, event | category | flops | bytes accessed | tf_op | source)
XLA Modules:
  0.0 63.8 jit_solution(10224162159189925901)
XLA Ops:
  0.6 3.3 %shard_map.187 = (bf16[8,16,384]{2,1,0:T(8,128)(2,1)}, f32[16,384]{1,0:T(8,128)}) custom-call(bf16[192,1536]{1,0:T(8,128)(2,1)} %bitcast.22, bf16[192,384]{1,0:T(8,128)(2,1)} %refs_4_.1, bf16[192,384]{1,0:T(8,128)(2,1)} %bitcast.26, bf16[16,192]{1,0:T(8,128)(2,1)} %bitcast.30, s32[1,12]{1,0:T(1,128)} %id_ref.1), custom_call_target="tpu_custom_call" | custom-call | tf_op jit(solution)/shard_map/pallas_call | solution.py:59
  4.0 6.4 %all-to-all-start = ((bf16[8,16,384]{2,1,0:T(8,128)(2,1)}), bf16[8,16,384]{2,1,0:T(8,128)(2,1)S(1)}, u32[]{:S(2)}, u32[]{:S(2)}) async-start(bf16[8,16,384]{2,1,0:T(8,128)(2,1)} %get-tuple-element.48), calls=%async_computation | async-start | bytes 196608 | tf_op jit(solution)/shard_map/all_to_all | solution.py:450
  10.3 3.9 %shard_map.188 = (bf16[192,512]{1,0:T(8,128)(2,1)S(1)}, bf16[192,512]{1,0:T(8,128)(2,1)S(1)}, bf16[192,192]{1,0:T(8,128)(2,1)S(1)}, bf16[192,192]{1,0:T(8,128)(2...) custom-call(bf16[192,512]{1,0:T(8,128)(2,1)} %bitcast.28, ...), custom_call_target="tpu_custom_call" | custom-call | tf_op jit(solution)/shard_map/pallas_call | solution.py:59
  14.2 2.4 %all-to-all-done.got_ref = bf16[8,16,384]{2,1,0:T(8,128)(2,1)S(1)} async-done(((bf16[8,16,384]{2,1,0:T(8,128)(2,1)}), bf16[8,16,384]{2,1,0:T(8,128)(2,1)S(1)}, u32[]{:S(2)}, u32[]{:S(2)}) %all-to-all-start) | async-done | bytes 98336 | tf_op jit(solution)/shard_map/all_to_all | solution.py:450
  16.6 3.0 %shard_map.189 = (bf16[8,16,192]{2,1,0:T(8,128)(2,1)}, bf16[128,192]{1,0:T(8,128)(2,1)S(1)}, bf16[192,128]{1,0:T(8,128)(2,1)S(1)}, bf16[192,128]{1,0:T(8,128)(2,...) custom-call(bf16[8,16,384]{2,1,0:T(8,128)(2,1)S(1)} %all-to-all-done, ...), custom_call_target="tpu_custom_call" | custom-call | tf_op jit(solution)/shard_map/pallas_call | solution.py:59
  19.6 1.3 %shard_map.190 = (bf16[192,512]{1,0:T(8,128)(2,1)}, bf16[8,80,128]{2,1,0:T(8,128)(2,1)S(1)}, bf16[8,80,128]{2,1,0:T(8,128)(2,1)S(1)}) custom-call(s32[1]{0:T(128)} %bitcast.head_ref, bf16[3,128,512]{2,1,0:T(8,128)(2,1)S(1)} %get-tuple-element.54.p_ref, bf16[3,128,512]{2,1,0:T(8,128)(2,1)S(1)} %get-tuple-element.55.ds_ref, ...), custom_call_target="tpu_custom_call" | custom-call | tf_op jit(solution)/shard_map/pallas_call | solution.py:59
  20.8 0.0 collective-permute-start
  20.8 3.4 %all-to-all-start.1 = ((bf16[8,16,192]{2,1,0:T(8,128)(2,1)}), bf16[8,16,192]{2,1,0:T(8,128)(2,1)S(1)}, u32[]{:S(2)}, u32[]{:S(2)}) async-start(bf16[8,16,192]{2,1,0:T(8,128)(2,1)} %get-tuple-element.70), calls=%async_computation.1 | async-start | bytes 131072 | tf_op jit(solution)/shard_map/all_to_all | solution.py:483
  24.2 1.6 %shard_map.191 = (bf16[192,1920]{1,0:T(8,128)(2,1)S(1)}, bf16[384,1536]{1,0:T(8,128)(2,1)S(1)}, f32[16,384]{1,0:T(8,128)S(1)}, bf16[192,384]{1,0:T(8,128)(2,1)S(1)}) custom-call(bf16[192,1536]{1,0:T(8,128)(2,1)} %bitcast.24, bf16[192,384]{1,0:T(8,128)(2,1)} %bitcast.27, bf16[384,1536]{1,0:T(8,128)(2,1)} %get-tuple-element.66.refs_2_, ...), custom_call_target="tpu_custom_call" | custom-call | tf_op jit(solution)/shard_map/pallas_call | solution.py:59
  25.8 0.0 collective-permute-done.got_ref
  25.8 0.1 shard_map.192
  25.9 4.2 %all-to-all-done.1.got_ref = bf16[8,16,192]{2,1,0:T(8,128)(2,1)S(1)} async-done(((bf16[8,16,192]{2,1,0:T(8,128)(2,1)}), bf16[8,16,192]{2,1,0:T(8,128)(2,1)S(1)}, u32[]{:S(2)}, u32[]{:S(2)}) %all-to-all-start.1) | async-done | bytes 49184 | tf_op jit(solution)/shard_map/all_to_all | solution.py:483
  30.1 1.5 %shard_map.193 = (bf16[384,1536]{1,0:T(8,128)(2,1)S(1)}, bf16[8,72,128]{2,1,0:T(8,128)(2,1)S(1)}, bf16[8,72,128]{2,1,0:T(8,128)(2,1)S(1)}) custom-call(s32[1]{0:T(128)} %bitcast.head_ref, bf16[8,16,192]{2,1,0:T(8,128)(2,1)S(1)} %all-to-all-done.1.got_ref, bf16[192,1920]{1,0:T(8,128)(2,1)S(1)} %get-tuple-element.71.both_ref, ...), custom_call_target="tpu_custom_call" | custom-call | tf_op jit(solution)/shard_map/pallas_call | solution.py:59
  31.5 0.1 collective-permute-start.1
  31.6 1.6 %collective-permute-start.2 = (bf16[4,80,128]{2,1,0:T(8,128)(2,1)S(1)}, bf16[4,80,128]{2,1,0:T(8,128)(2,1)S(1)}, u32[]{:S(2)}, u32[]{:S(2)}) collective-permute-start(bf16[4,80,128]{2,1,0:T(8,128)(2,1)S(1)} %get-tuple-element.79), channel_id=1, source_target_pairs={{0,2},{2,0},{1,3},{3,1},{4,6},{6,4},{5,7},{7,5},{8,10},{10,8},{9,1... | collective-permute-start | bytes 245768 | tf_op jit(solution)/shard_map/ppermute | solution.py:516
  33.2 1.3 %shard_map.194.refs_4_ = bf16[192,1536]{1,0:T(8,128)(2,1)} custom-call(bf16[192,384]{1,0:T(8,128)(2,1)S(1)} %get-tuple-element.69.win_ref, bf16[384,1536]{1,0:T(8,128)(2,1)S(1)} %get-tuple-element.76.dpre_ref, bf16[8,72,128]{2,1,0:T(8,128)(2,1)S(1)} %get-tuple-element.77.after_ref), custom_call_target="tpu_custom_call" | custom-call | tf_op jit(solution)/shard_map/pallas_call | solution.py:59
  34.4 2.0 %collective-permute-done.2.refs_3_ = bf16[4,80,128]{2,1,0:T(8,128)(2,1)S(1)} collective-permute-done((bf16[4,80,128]{2,1,0:T(8,128)(2,1)S(1)}, bf16[4,80,128]{2,1,0:T(8,128)(2,1)S(1)}, u32[]{:S(2)}, u32[]{:S(2)}) %collective-permute-start.2) | collective-permute-done | bytes 81952 | tf_op jit(solution)/shard_map/ppermute | solution.py:516
  36.5 0.0 collective-permute-done.1.refs_2_
  36.5 0.1 shard_map.195
  36.5 11.0 %all_to_all.20.got_ref = bf16[8,112,128]{2,1,0:T(8,128)(2,1)S(1)} all-to-all(bf16[8,112,128]{2,1,0:T(8,128)(2,1)S(1)} %shard_map.195), channel_id=1, replica_groups=mesh['groups'=2,'geom'=4,'design'=2,'head'=2] {'geom','design'}, dimensions={0} | all-to-all | bytes 458752 | tf_op jit(solution)/shard_map/all_to_all | solution.py:536
  47.6 13.5 %all_to_all.21.mine_ref = bf16[8,152,128]{2,1,0:T(8,128)(2,1)S(1)} all-to-all(bf16[8,152,128]{2,1,0:T(8,128)(2,1)S(1)} %shard_map.196), channel_id=1, replica_groups=mesh['groups'=2,'geom'=4,'design'=2,'head'=2] {'geom','design'}, dimensions={0} | all-to-all | bytes 622592 | tf_op jit(solution)/shard_map/all_to_all | solution.py:542
  61.1 0.0 collective-permute-start.3
  61.1 1.6 %collective-permute-done.3.other_ref = bf16[8,152,128]{2,1,0:T(8,128)(2,1)S(1)} collective-permute-done((bf16[8,152,128]{2,1,0:T(8,128)(2,1)S(1)}, bf16[8,152,128]{2,1,0:T(8,128)(2,1)S(1)}, u32[]{:S(2)}, u32[]{:S(2)}) %collective-permute-start.3) | collective-permute-done | bytes 311328 | tf_op jit(solution)/shard_map/ppermute | solution.py:543
  62.7 1.1 %shard_map.197 = (f32[192,384]{1,0:T(8,128)}, f32[192,384]{1,0:T(8,128)}, f32[192,192]{1,0:T(8,128)}, f32[192,192]{1,0:T(8,128)}, f32[192,192]{1,0:T(8,128)}, /*index=5*/f32[192,192]{1,0:T(8,128)}, f32[1,192]{1,0:T(1,128)}) custom-call(s32[1]{0:T(128)} %bitcast.head_ref, bf16[8,152,128]{2,1,0:T(8,128)(2,1)S(1)} %all_to_all.21.mine_ref, ...), custom_call_target="tpu_custom_call" | custom-call | tf_op jit(solution)/shard_map/pallas_call | solution.py:59
  (1 shorter events, 0.0 us)
Async XLA Ops:
  4.0 12.7 %all-to-all-start = ((bf16[8,16,384]{2,1,0:T(8,128)(2,1)}), bf16[8,16,384]{2,1,0:T(8,128)(2,1)S(1)}, u32[]{:S(2)}, u32[]{:S(2)}) async-start(bf16[8,16,384]{2,1,0:T(8,128)(2,1)} %get-tuple-element.48), calls=%async_computation | async-start | bytes 196608 | tf_op jit(solution)/shard_map/all_to_all | solution.py:450
  20.8 4.9 %collective-permute-start = (bf16[8,80,128]{2,1,0:T(8,128)(2,1)S(1)}, bf16[8,80,128]{2,1,0:T(8,128)(2,1)S(1)}, u32[]{:S(2)}, u32[]{:S(2)}) collective-permute-start(bf16[8,80,128]{2,1,0:T(8,128)(2,1)S(1)} %get-tuple-element.68.refs_5_), channel_id=1, source_target_pairs={{0,1},{1,0},{2,3},{3,2},{4,5},{5,4},{6,7},{7,6},{8,9},{9,8},{10,11... | collective-permute-start | bytes 491528 | tf_op jit(solution)/shard_map/ppermute | solution.py:505
  20.8 9.2 %all-to-all-start.1 = ((bf16[8,16,192]{2,1,0:T(8,128)(2,1)}), bf16[8,16,192]{2,1,0:T(8,128)(2,1)S(1)}, u32[]{:S(2)}, u32[]{:S(2)}) async-start(bf16[8,16,192]{2,1,0:T(8,128)(2,1)} %get-tuple-element.70), calls=%async_computation.1 | async-start | bytes 131072 | tf_op jit(solution)/shard_map/all_to_all | solution.py:483
  31.5 4.9 %collective-permute-start.1 = (bf16[8,72,128]{2,1,0:T(8,128)(2,1)S(1)}, bf16[8,72,128]{2,1,0:T(8,128)(2,1)S(1)}, u32[]{:S(2)}, u32[]{:S(2)}) collective-permute-start(bf16[8,72,128]{2,1,0:T(8,128)(2,1)S(1)} %get-tuple-element.77.after_ref), channel_id=1, source_target_pairs={{0,1},{1,0},{2,3},{3,2},{4,5},{5,4},{6,7},{7,6},{8,9},{9,8},{10,11... | collective-permute-start | bytes 442376 | tf_op jit(solution)/shard_map/ppermute | solution.py:527
  31.6 4.8 %collective-permute-start.2 = (bf16[4,80,128]{2,1,0:T(8,128)(2,1)S(1)}, bf16[4,80,128]{2,1,0:T(8,128)(2,1)S(1)}, u32[]{:S(2)}, u32[]{:S(2)}) collective-permute-start(bf16[4,80,128]{2,1,0:T(8,128)(2,1)S(1)} %get-tuple-element.79), channel_id=1, source_target_pairs={{0,2},{2,0},{1,3},{3,1},{4,6},{6,4},{5,7},{7,5},{8,10},{10,8},{9,1... | collective-permute-start | bytes 245768 | tf_op jit(solution)/shard_map/ppermute | solution.py:516
  61.1 1.6 %collective-permute-start.3 = (bf16[8,152,128]{2,1,0:T(8,128)(2,1)S(1)}, bf16[8,152,128]{2,1,0:T(8,128)(2,1)S(1)}, u32[]{:S(2)}, u32[]{:S(2)}) collective-permute-start(bf16[8,152,128]{2,1,0:T(8,128)(2,1)S(1)} %all_to_all.21.mine_ref), channel_id=1, source_target_pairs={{0,1},{1,0},{2,3},{3,2},{4,5},{5,4},{6,7},{7,6},{8,9},{9,8},{10,11... | collective-permute-start | bytes 933896 | tf_op jit(solution)/shard_map/ppermute | solution.py:543

commit v4 on v3

--- a/solution.py
+++ b/solution.py
@@ -37,7 +37,7 @@
     return tuple(Held(value, pltpu.VMEM) for value in values)
 
 
-def call(kernel, outs, *args, scratch=(), smem=0, final=(), raw=()):
+def call(kernel, outs, *args, scratch=(), smem=0, final=(), raw=(), update=False):
     held = [Held(arg, None) for arg in args[:smem]]
     held += [arg if isinstance(arg, Held) else Held(arg, pltpu.HBM) for arg in args[smem:]]
     specs = [pl.BlockSpec(memory_space=pltpu.SMEM)] * smem
@@ -52,10 +52,13 @@
         else pltpu.with_memory_space_constraint(arg.value, arg.space)
         for arg in held
     ]
+    if update:
+        aliases = {len(operands) - len(raw) + place: place for place in range(len(raw))}
+        return build(kernel, outs, operands, specs, scratch, range(len(outs)), aliases, pl.ANY)
     return build(kernel, outs, operands, specs, scratch, final)
 
 
-def build(kernel, outs, operands, specs, scratch, final):
+def build(kernel, outs, operands, specs, scratch, final, aliases=None, space=None):
     return pl.pallas_call(
         kernel,
         out_shape=[
@@ -66,11 +69,12 @@
         ],
         in_specs=specs,
         out_specs=[
-            pl.BlockSpec() if place in final else pl.BlockSpec(memory_space=pltpu.VMEM)
+            pl.BlockSpec(memory_space=space if place in final else pltpu.VMEM)
             for place in range(len(outs))
         ],
         scratch_shapes=list(scratch),
         compiler_params=pltpu.CompilerParams(vmem_limit_bytes=VMEM_LIMIT),
+        input_output_aliases=aliases or {},
         interpret=INTERPRET,
     )(*operands)
 
@@ -109,7 +113,8 @@
     hsum_ref[...] = hsum
     high, low = split_bf(hsum)
     wout = wout_ref[...]
-    sums = dg(high, wout, 1, 1) + dg(low, wout, 1, 1)
+    sums = dg(jnp.concatenate([high, low], axis=0), wout, 1, 1)
+    sums = sums[: hsum.shape[0]] + sums[hsum.shape[0] :]
     ids = id_ref[...]
     digits = jnp.concatenate([ids % DIGIT, ids // DIGIT], axis=0).astype(F32)
     packed = jnp.zeros((rows, 2 * width), F32)
@@ -160,7 +165,7 @@
 def attend_kernel(
     blocks, size, per_owner,
     got_ref, gain_ref, wk_ref, wv_ref, q_ref, dmix_ref,
-    rows_ref, normed_ref, k_ref, v_ref, p_ref, ds_ref, kt_ref, vt_ref, gain_out_ref,
+    rows_ref, normed_ref, k_ref, v_ref, p_ref, ds_ref, kt_ref, vt_ref,
 ):
     owners, rows, both = got_ref.shape
     width = both // 2
@@ -188,34 +193,44 @@
     unit = asum * inv
     normed = (unit * gain).astype(BF)
     normed_ref[...] = normed
-    keys = dg(wk_ref[...], normed, 0, 1).astype(BF)
-    values = dg(wv_ref[...], normed, 0, 1).astype(BF)
+    keys = dg(normed, wk_ref[...], 1, 0).astype(BF)
+    values = dg(normed, wv_ref[...], 1, 0).astype(BF)
     k_ref[...] = keys
     v_ref[...] = values
     depth = width // HEADS
     scale = 1.0 / depth**0.5
+    key_parts, value_parts = [], []
     for head in range(HEADS):
         part = slice(head * depth, (head + 1) * depth)
         q = q_ref[part, :]
         dmix = dmix_ref[part, :]
-        scores = dg(keys[part], q, 0, 0) * scale
+        scores = dg(keys[:, part], q, 1, 0) * scale
         top = jnp.max(scores, axis=0, keepdims=True)
         weight = jnp.exp(scores - top)
         probs = weight * (1.0 / jnp.sum(weight, axis=0, keepdims=True))
         probs_bf = probs.astype(BF)
         p_ref[head] = probs_bf
-        dprobs = dg(values[part], dmix, 0, 0)
+        dprobs = dg(values[:, part], dmix, 1, 0)
         inner = jnp.sum(probs * dprobs, axis=0, keepdims=True)
         dscore = (probs * (dprobs - inner) * scale).astype(BF)
         ds_ref[head] = dscore
-        kt_ref[part, :] = dg(q, dscore, 1, 1).astype(BF)
-        vt_ref[part, :] = dg(dmix, probs_bf, 1, 1).astype(BF)
-    dnorm = dg(kt_ref[...], wk_ref[...], 0, 1) + dg(vt_ref[...], wv_ref[...], 0, 1)
-    gain_out_ref[...] = jnp.sum(dnorm * unit, axis=0, keepdims=True)
+        key_parts.append(dg(dscore, q, 1, 1))
+        value_parts.append(dg(probs_bf, dmix, 1, 1))
+    kt = jnp.concatenate(key_parts, axis=1).astype(BF)
+    vt = jnp.concatenate(value_parts, axis=1).astype(BF)
+    kt_ref[...] = kt
+    vt_ref[...] = vt
+    dnorm = dg(kt, wk_ref[...], 1, 1) + dg(vt, wv_ref[...], 1, 1)
+    dgain = jnp.sum(dnorm * unit, axis=0, keepdims=True)
     scaled = dnorm * gain
     dsum = inv * scaled - asum * (inv * inv * inv) * jnp.mean(scaled * asum, axis=1, keepdims=True)
     dpool = (dsum * inv_div).astype(BF)
-    rows_ref[...] = dg(member, dpool, 1, 0).astype(BF).reshape(owners, rows, width)
+    spare = iota((total, 1), 0) % rows == blocks
+    picked = jnp.where(spare, dgain, dg(member, dpool, 1, 0))
+    picked = picked.reshape(owners, rows, width)
+    rest = picked[:, :, LANES:]
+    rest = jnp.concatenate([rest[:, : rows // 2], rest[:, rows // 2 :]], axis=2)
+    rows_ref[...] = jnp.concatenate([picked[:, :, :LANES], rest], axis=1).astype(BF)
 
 
 def put_rows(ref, chunk, start, value):
@@ -238,16 +253,15 @@
     return pieces[0] if len(pieces) == 1 else jnp.concatenate(pieces, axis=0)
 
 
-def pack_square(ref, chunk, mats, start):
+def pack_square(ref, chunk, mats):
     width = mats[0].shape[0]
-    for mat in mats:
-        put_rows(ref, chunk, start, mat[:, :LANES])
-        start += width
+    start = 0
     for first in range(0, len(mats), 2):
-        pair = jnp.concatenate([mats[first][:, LANES:], mats[first + 1][:, LANES:]], axis=1)
-        put_rows(ref, chunk, start, pair)
-        start += width
-    return start
+        left, right = mats[first : first + 2]
+        pair = jnp.concatenate([left[:, LANES:], right[:, LANES:]], axis=1)
+        for slot in (left[:, :LANES], right[:, :LANES], pair):
+            put_rows(ref, chunk, start, slot)
+            start += width
 
 
 def swap_halves(head_ref, scratch, keep_ref, send_ref):
@@ -274,45 +288,45 @@
 
 
 def finish_kernel(
-    chunk, head_ref, p_ref, ds_ref, k_ref, v_ref, kt_ref, vt_ref, normed_ref, gain_ref, x_ref, g_ref,
+    chunk, head_ref, p_ref, ds_ref, k_ref, v_ref, kt_ref, vt_ref, normed_ref, x_ref, g_ref,
     wp_ref, out_ref, keep_ref, send_ref, mixed_ref, dq_ref, pack_ref,
 ):
-    width = k_ref.shape[0]
+    width = k_ref.shape[1]
     depth = width // HEADS
     for head in range(HEADS):
         part = slice(head * depth, (head + 1) * depth)
-        mixed_ref[part, :] = dg(v_ref[part, :], p_ref[head], 1, 0).astype(BF)
-        dq_ref[part, :] = dg(k_ref[part, :], ds_ref[head], 1, 0).astype(BF)
+        mixed_ref[part, :] = dg(v_ref[:, part], p_ref[head], 0, 0).astype(BF)
+        dq_ref[part, :] = dg(k_ref[:, part], ds_ref[head], 0, 0).astype(BF)
     mixed = mixed_ref[...]
     out_ref[...] = dg(wp_ref[...], mixed, 0, 0).astype(BF)
     mats = [
         dg(x_ref[...], dq_ref[...], 1, 1),
-        dg(normed_ref[...], kt_ref[...], 0, 1),
-        dg(normed_ref[...], vt_ref[...], 0, 1),
+        dg(normed_ref[...], kt_ref[...], 0, 0),
+        dg(normed_ref[...], vt_ref[...], 0, 0),
         dg(mixed, g_ref[...], 1, 1),
     ]
-    pieces, rows, _ = pack_ref.shape
-    pack_square(pack_ref, chunk, mats, 0)
-    gain = gain_ref[...]
-    pack_ref[:, chunk:, :] = jnp.zeros((pieces, rows - chunk, LANES), F32)
-    pack_ref[0, chunk : chunk + 1, :] = gain[:, :LANES]
-    rest = width - LANES
-    pack_ref[0, chunk + 1 : chunk + 2, :] = jnp.concatenate(
-        [gain[:, LANES:], jnp.zeros((1, LANES - rest), F32)], axis=1
-    )
+    if pack_ref.shape[1] > chunk:
+        pack_ref[:, chunk:, :] = jnp.zeros((pack_ref.shape[0], pack_ref.shape[1] - chunk, LANES), F32)
+    pack_square(pack_ref, chunk, mats)
     swap_halves(head_ref, pack_ref, keep_ref, send_ref)
 
 
 def back_kernel(
     blocks, chunk, head_ref, got_ref, both_ref, slope_ref, hsum_ref, *refs,
 ):
-    dpre_ref, keep_ref, send_ref, pack_ref = refs[-4:]
+    dpre_ref, keep_ref, send_ref, gain_ref, pack_ref = refs[-5:]
     width = both_ref.shape[0]
     points = slope_ref.shape[1]
     size = points // blocks
     x_ref = both_ref.at[:, :points]
     wout_ref = both_ref.at[:, points:]
-    grad = jnp.sum(got_ref[...].astype(F32), axis=0)[: hsum_ref.shape[0]].astype(BF)
+    total = jnp.sum(got_ref[...].astype(F32), axis=0)
+    rows = total.shape[0] * 2 // 3
+    rest = total[rows:]
+    rest = jnp.concatenate([rest[:, : width - LANES], rest[:, width - LANES :]], axis=0)
+    total = jnp.concatenate([total[:rows], rest], axis=1)
+    gain_ref[...] = total[blocks : blocks + 1]
+    grad = total[: hsum_ref.shape[0]].astype(BF)
     dhid = dg(wout_ref[...], grad, 0, 1)
     for block in range(blocks):
         cols = pl.ds(block * size, size)
@@ -341,76 +355,92 @@
         refs[shift][...] = total_ref[:, pl.ds(share, 1)][:, 0].astype(BF)
 
 
-def join_kernel(shares, *refs):
-    _, out_ref = refs[-2:]
-    ka_ref, kp_ref, rp_ref = refs[:3]
+def join_kernel(shares, part, *refs):
+    out_ref = refs[-1]
+    ka_ref, kp_ref, rp_ref, gain_ref = refs[:4]
     total = ka_ref[...].astype(F32)
-    for ref in refs[3:-2]:
+    for ref in refs[4:-2]:
         total = total + ref[...].astype(F32)
-    groups, rows, _ = total.shape
-    part = rows // shares
-    total = total.astype(BF)
+    groups = total.shape[0]
+    top = out_ref.shape[1] - kp_ref.shape[1]
+    gain = gain_ref[...] * (1.0 / groups)
+    width = gain.shape[1]
+    tail = [gain[:, :LANES], jnp.concatenate([gain[:, LANES:], jnp.zeros((1, 2 * LANES - width), F32)], axis=1)]
+    tail = jnp.concatenate(tail + [jnp.zeros((top - part - 2, LANES), F32)], axis=0)
     for group in range(groups):
         for share in range(shares):
-            out_ref[group * shares + share, :part, :] = total[group, share * part : (share + 1) * part]
-    out_ref[:, part:, :] = (kp_ref[...].astype(F32) + rp_ref[...].astype(F32)).astype(BF)
-
-
-def sum_kernel(shares, part, got_ref, out_ref):
+            piece = total[group, share * part : (share + 1) * part]
+            out_ref[group * shares + share, :top, :] = jnp.concatenate([piece, tail], axis=0).astype(BF)
+    out_ref[:, top:, :] = (kp_ref[...].astype(F32) + rp_ref[...].astype(F32)).astype(BF)
+
+
+def sum_kernel(shares, part, top, got_ref, out_ref, gain_ref):
     peers = out_ref.shape[0]
+    gain = None
     for share in range(shares):
-        total = got_ref[share, :part, :].astype(F32)
+        total = got_ref[share, :top, :].astype(F32)
         for peer in range(share + shares, peers, shares):
-            total = total + got_ref[peer, :part, :].astype(F32)
-        total = total.astype(BF)
+            total = total + got_ref[peer, :top, :].astype(F32)
+        tail = total[part : part + 2]
+        gain = tail if gain is None else gain + tail
+        total = total[:part].astype(BF)
         for peer in range(peers):
             out_ref[peer, share * part : (share + 1) * part, :] = total
-    total = jnp.sum(got_ref[:, part:, :].astype(F32), axis=0).astype(BF)
+    width = gain_ref.shape[1]
+    gain_ref[...] = jnp.concatenate([gain[:1], gain[1:2, : width - LANES]], axis=1)
+    total = jnp.sum(got_ref[:, top:, :].astype(F32), axis=0).astype(BF)
     for peer in range(peers):
         out_ref[peer, shares * part :, :] = total
 
 
-def unpack_kernel(
-    shares, chunk_a, rows_a, chunk_p, head_ref, mine_ref, other_ref,
-    gin_ref, gout_ref, gq_ref, gk_ref, gv_ref, gp_ref, gain_ref, all_ref,
-):
-    peers = mine_ref.shape[0]
-    head = head_ref[0]
-    all_ref[pl.ds(head * peers, peers)] = mine_ref[...]
-    all_ref[pl.ds((1 - head) * peers, peers)] = other_ref[...]
-    part = rows_a // shares
+def unpack_kernel(shares, part, chunk_a, chunk_p, flip, head_ref, half_ref, gain_ref, *refs):
+    left_ref, right_ref, wide_ref, sems = refs[-4:]
+    targets = refs[-11:-5]
+    gain_out = refs[-5]
+    width = left_ref.shape[0]
+    rows_a = shares * part
 
     def read_a(index, offset, take):
         group, share = divmod(index, shares)
 
         def read(source, start, count):
             row = share * part + start
-            return all_ref[group * shares + source, row : row + count, :].astype(F32)
+            return half_ref[group * shares + source, row : row + count, :].astype(F32)
 
         return get_rows(read, part, offset, take)
 
     def read_p(index, offset, take):
-        return all_ref[index, rows_a + offset : rows_a + offset + take, :].astype(F32)
-
-    width = gq_ref.shape[0]
-    squares = (gq_ref, gk_ref, gv_ref, gp_ref)
-    start = 0
-    for ref in squares:
-        ref[:, :LANES] = get_rows(read_a, chunk_a, start, width)
-        start += width
+        return half_ref[index, rows_a + offset : rows_a + offset + take, :].astype(F32)
+
+    for slot in range(wide_ref.shape[1] // LANES):
+        wide_ref[:, slot * LANES : (slot + 1) * LANES] = get_rows(read_p, chunk_p, slot * width, width)
+    left_ref[:, :LANES] = get_rows(read_a, chunk_a, 0, width)
+    right_ref[:, :LANES] = get_rows(read_a, chunk_a, width, width)
+    pair = get_rows(read_a, chunk_a, 2 * width, width)
     rest = width - LANES
-    for first in range(0, len(squares), 2):
-        pair = get_rows(read_a, chunk_a, start, width)
-        squares[first][:, LANES:] = pair[:, :rest]
-        squares[first + 1][:, LANES:] = pair[:, rest:]
-        start += width
-    tail = read_a(0, chunk_a, 2)
-    gain_ref[...] = jnp.concatenate([tail[:1], tail[1:2, :rest]], axis=1)
-    start = 0
-    for ref in (gin_ref, gout_ref):
-        for lane in range(0, ref.shape[1], LANES):
-            ref[:, lane : lane + LANES] = get_rows(read_p, chunk_p, start, width)
-            start += width
+    left_ref[:, LANES:] = pair[:, :rest]
+    right_ref[:, LANES:] = pair[:, rest:]
+    if not flip:
+        extra = pltpu.make_async_copy(gain_ref, gain_out, sems.at[3])
+        extra.start()
+    half = 1 - head_ref[0] if flip else head_ref[0]
+    for which in range(2):
+
+        @pl.when(half == which)
+        def _():
+            copies = [
+                pltpu.make_async_copy(source, target, sems.at[place])
+                for place, (source, target) in enumerate(
+                    zip((left_ref, right_ref, wide_ref), targets[3 * which : 3 * which + 3])
+                )
+            ]
+            for copy in copies:
+                copy.start()
+            for copy in copies:
+                copy.wait()
+
+    if not flip:
+        extra.wait()
 
 
 def on_device(
@@ -438,14 +468,15 @@
     share = lax.axis_index("design").astype(jnp.int32).reshape(1)
     pieces = 2 * peers
     chunk_a = 6 * width // pieces
-    rows_a = round_up(chunk_a + 2, 8 * shares)
+    rows_a = round_up(chunk_a, 4 * shares)
+    part = rows_a // shares
+    top = round_up(part + 2, 8)
     chunk_p = 2 * width * hid // LANES // pieces
 
     send, hsum = call(
         functools.partial(pool_kernel, blocks),
         [((owners, rows, 2 * width), BF), ((round_up(blocks, 8), hid), F32)],
         xt, w_in, wot, anchor_feats[0], block_anchor,
-        final=(1,),
     )
     got = lax.all_to_all(send, team, 0, 0, tiled=True)
     qp, dmix, wk, wv, gain_row, qn, gn, wpn, slope = call(
@@ -462,21 +493,19 @@
             ((hid, points), BF),
         ],
         qt, gt, w_query, w_proj, w_key, w_value, norm_gain.reshape(1, width), xt, w_in,
-        final=(8,),
     )
     pair_shape = (HEADS, anchors, queries)
-    rows_out, normed, keys, values, probs, dscore, kt, vt, gain_part = call(
+    rows_out, normed, keys, values, probs, dscore, kt, vt = call(
         functools.partial(attend_kernel, blocks, size, per_owner),
         [
-            ((owners, rows, width), BF),
+            ((owners, rows * width // LANES, LANES), BF),
             ((anchors, width), BF),
-            ((width, anchors), BF),
-            ((width, anchors), BF),
+            ((anchors, width), BF),
+            ((anchors, width), BF),
             (pair_shape, BF),
             (pair_shape, BF),
-            ((width, anchors), BF),
-            ((width, anchors), BF),
-            ((1, width), F32),
+            ((anchors, width), BF),
+            ((anchors, width), BF),
         ],
         *near(got, gain_row, wk, wv, qp, dmix),
     )
@@ -485,7 +514,7 @@
     attended, keep_a, send_a = call(
         functools.partial(finish_kernel, chunk_a),
         [((width, queries), BF), shape_a, shape_a],
-        head, *near(probs, dscore, keys, values, kt, vt, normed, gain_part, qn, gn, wpn),
+        head, *near(probs, dscore, keys, values, kt, vt, normed, qn, gn, wpn),
         scratch=[
             pltpu.VMEM((width, queries), BF),
             pltpu.VMEM((width, queries), BF),
@@ -494,11 +523,11 @@
         smem=1,
         final=(0,),
     )
-    both, slope, hsum, win = call(
+    both, win = call(
         fetch_kernel,
-        [((width, points + hid), BF), ((hid, points), BF), (hsum.shape, F32), ((width, hid), BF)],
-        scratch=[pltpu.SemaphoreType.DMA((5,))],
-        raw=(xt, wot, slope, hsum, w_in) + near(send_a),
+        [((width, points + hid), BF), ((width, hid), BF)],
+        scratch=[pltpu.SemaphoreType.DMA((3,))],
+        raw=(xt, wot, w_in) + near(send_a),
     )
     swap = [(0, 1), (1, 0)]
     shape_p = ((peers, chunk_p, LANES), BF)
@@ -516,9 +545,9 @@
         lax.ppermute(send, "design", [(i, (i + shift) % shares) for i in range(shares)])
         for shift, send in enumerate(sends_d, 1)
     ]
-    dpre, keep_p, send_p = call(
+    dpre, keep_p, send_p, dgain = call(
         functools.partial(back_kernel, blocks, chunk_p),
-        [((hid, points), BF), shape_p, shape_p],
+        [((hid, points), BF), shape_p, shape_p, ((1, width), F32)],
         head, *near(back, both, slope, hsum),
         scratch=[pltpu.VMEM((pieces, chunk_p, LANES), F32)],
         smem=1,
@@ -529,27 +558,32 @@
         point_grad_kernel, [((width, points), BF)], *near(win, dpre), final=(0,), raw=near(send_p)
     )
     (joined,) = call(
-        functools.partial(join_kernel, shares),
-        [((peers, rows_a // shares + chunk_p, LANES), BF)],
-        *near(keep_d, keep_p, recv_p, *recvs_d), raw=(point_grad,),
+        functools.partial(join_kernel, shares, part),
+        [((peers, top + chunk_p, LANES), BF)],
+        *near(keep_d, keep_p, recv_p, dgain, *recvs_d), raw=(point_grad,),
     )
     scattered = lax.all_to_all(joined, crowd, 0, 0, tiled=True)
-    (summed,) = call(
-        functools.partial(sum_kernel, shares, rows_a // shares),
-        [((peers, rows_a + chunk_p, LANES), BF)],
+    summed, gain = call(
+        functools.partial(sum_kernel, shares, part, top),
+        [((peers, rows_a + chunk_p, LANES), BF), ((1, width), F32)],
         *near(scattered),
     )
     mine = lax.all_to_all(summed, crowd, 0, 0, tiled=True)
     other = lax.ppermute(mine, "head", swap)
-    square = ((width, width), F32)
-    gin, gout, gq, gk, gv, gp, gain = call(
-        functools.partial(unpack_kernel, shares, chunk_a, rows_a, chunk_p),
-        [((width, hid), F32), ((width, hid), F32), square, square, square, square, ((1, width), F32)],
-        head, *near(mine, other),
-        scratch=[pltpu.VMEM((pieces, rows_a + chunk_p, LANES), BF)],
-        smem=1,
-        final=range(7),
-    )
+    square, wide = ((width, width), F32), ((width, hid), F32)
+    grads = ()
+    for flip, half in ((False, mine), (True, other)):
+        grads = call(
+            functools.partial(unpack_kernel, shares, part, chunk_a, chunk_p, flip),
+            [square, square, wide] * 2 + [((1, width), F32)],
+            head, *near(half, gain),
+            scratch=[pltpu.VMEM(*square), pltpu.VMEM(*square), pltpu.VMEM(*wide)]
+            + [pltpu.SemaphoreType.DMA((4,))],
+            smem=1,
+            raw=grads,
+            update=True,
+        )
+    gq, gk, gin, gv, gp, gout, gain = grads
     return (
         attended.T[None], point_grad.T[None], gin, gout.T, gq, gk, gv, gp, gain.reshape(width),
     )

time: 64.3 us -> 63.2 us (0.983)
  Pallas kernels: 17.1 us -> 16.2 us
    all_to_all x1, waiting for transfers between devices: 2.38 us -> 3.42 us  [on_device(): got = lax.all_to_all(send, team, 0, 0, tiled=True)]
    ppermute x1, waiting for transfers between devices: 1.6 us -> 0.67 us  [on_device(): other = lax.ppermute(mine, 'head', swap)]
    pallas_call x11 -> x12, Pallas kernels: 17.1 us -> 16.2 us  [build(): pl.pallas_call(kernel, out_shape=[jax.ShapeDtypeStruct(shape, dtype) if I...]
  transfers between devices with their start and end apart: 6 -> 6, of which waited for: 4 -> 4; matrix products, arithmetic and copies ran while one was open for 0% -> 0% of each run, Pallas kernels for 11% -> 10%
where the time goes in v4:
time: 63.2 us; the launch traced here: 62.8 us
  blocking collectives  24.1 us (38%)
  Pallas kernels  16.2 us (26%)
  starting transfers between devices  11.3 us (18%)
  waiting for transfers between devices  10.4 us (16%)
  between operations  0.72 us (1%)
    pallas_call x12, Pallas kernels, build(): pl.pallas_call(kernel, out_shape=[jax.ShapeDtypeStruct(shape, dtype) if I...  16.2 us
    all_to_all x1, blocking collectives, on_device(): mine = lax.all_to_all(summed, crowd, 0, 0, tiled=True)  13.2 us
    all_to_all x1, blocking collectives, on_device(): scattered = lax.all_to_all(joined, crowd, 0, 0, tiled=True)  10.9 us
    all_to_all x1, starting transfers between devices, on_device(): got = lax.all_to_all(send, team, 0, 0, tiled=True)  6.35 us
    all_to_all x1, waiting for transfers between devices, on_device(): back = lax.all_to_all(rows_out, team, 0, 0, tiled=True)  4.5 us
    all_to_all x1, waiting for transfers between devices, on_device(): got = lax.all_to_all(send, team, 0, 0, tiled=True)  3.42 us
    all_to_all x1, starting transfers between devices, on_device(): back = lax.all_to_all(rows_out, team, 0, 0, tiled=True)  3.35 us
    ppermute x1, waiting for transfers between devices, on_device(): lax.ppermute(send, 'design', [(i, (i + shift) % shares) for i in range(sh...  1.81 us
  transfers between devices with their start and end apart: 6, of which 4 were waited for; matrix products, arithmetic and copies ran while one was open for 0% of the time, Pallas kernels for 10%

profile of v4, /device:TPU:0, one launch (start us, length us, event | category | flops | bytes accessed | tf_op | source)
XLA Modules:
  0.0 62.8 jit_solution(4700445138827368377)
XLA Ops:
  0.6 3.2 %shard_map.187 = (bf16[8,16,384]{2,1,0:T(8,128)(2,1)}, f32[16,384]{1,0:T(8,128)S(1)}) custom-call(bf16[192,1536]{1,0:T(8,128)(2,1)} %bitcast.22, bf16[192,384]{1,0:T(8,128)(2,1)} %refs_2_.1, bf16[192,384]{1,0:T(8,128)(2,1)} %bitcast.26, bf16[16,192]{1,0:T(8,128)(2,1)} %bitcast.31, s32[1,12]{1,0:T(1,128)} %id_ref.1), custom_call_target="tpu_custom_call" | custom-call | tf_op jit(solution)/shard_map/pallas_call | solution.py:62
  3.8 6.4 %all-to-all-start = ((bf16[8,16,384]{2,1,0:T(8,128)(2,1)}), bf16[8,16,384]{2,1,0:T(8,128)(2,1)S(1)}, u32[]{:S(2)}, u32[]{:S(2)}) async-start(bf16[8,16,384]{2,1,0:T(8,128)(2,1)} %get-tuple-element.55), calls=%async_computation | async-start | bytes 196608 | tf_op jit(solution)/shard_map/all_to_all | solution.py:481
  10.2 2.9 %shard_map.188 = (bf16[192,512]{1,0:T(8,128)(2,1)S(1)}, bf16[192,512]{1,0:T(8,128)(2,1)S(1)}, bf16[192,192]{1,0:T(8,128)(2,1)S(1)}, bf16[192,192]{1,0:T(8,128)(2...) custom-call(bf16[192,512]{1,0:T(8,128)(2,1)} %bitcast.29, ...), custom_call_target="tpu_custom_call" | custom-call | tf_op jit(solution)/shard_map/pallas_call | solution.py:62
  13.1 3.4 %all-to-all-done.got_ref = bf16[8,16,384]{2,1,0:T(8,128)(2,1)S(1)} async-done(((bf16[8,16,384]{2,1,0:T(8,128)(2,1)}), bf16[8,16,384]{2,1,0:T(8,128)(2,1)S(1)}, u32[]{:S(2)}, u32[]{:S(2)}) %all-to-all-start) | async-done | bytes 98336 | tf_op jit(solution)/shard_map/all_to_all | solution.py:481
  16.5 2.8 %shard_map.189 = (bf16[8,24,128]{2,1,0:T(8,128)(2,1)}, bf16[128,192]{1,0:T(8,128)(2,1)S(1)}, bf16[128,192]{1,0:T(8,128)(2,1)S(1)}, bf16[128,192]{1,0:T(8,128)(2,...) custom-call(bf16[8,16,384]{2,1,0:T(8,128)(2,1)S(1)} %all-to-all-done, ...), custom_call_target="tpu_custom_call" | custom-call | tf_op jit(solution)/shard_map/pallas_call | solution.py:62
  19.3 1.3 %shard_map.190 = (bf16[192,512]{1,0:T(8,128)(2,1)}, bf16[8,72,128]{2,1,0:T(8,128)(2,1)S(1)}, bf16[8,72,128]{2,1,0:T(8,128)(2,1)S(1)}) custom-call(s32[1]{0:T(128)} %bitcast.head_ref, bf16[3,128,512]{2,1,0:T(8,128)(2,1)S(1)} %get-tuple-element.61.p_ref, bf16[3,128,512]{2,1,0:T(8,128)(2,1)S(1)} %get-tuple-element.62.ds_ref, ...), custom_call_target="tpu_custom_call" | custom-call | tf_op jit(solution)/shard_map/pallas_call | solution.py:62
  20.7 0.0 collective-permute-start
  20.7 3.3 %all-to-all-start.1 = ((bf16[8,24,128]{2,1,0:T(8,128)(2,1)}), bf16[8,24,128]{2,1,0:T(8,128)(2,1)S(1)}, u32[]{:S(2)}, u32[]{:S(2)}) async-start(bf16[8,24,128]{2,1,0:T(8,128)(2,1)} %get-tuple-element.74), calls=%async_computation.1 | async-start | bytes 98304 | tf_op jit(solution)/shard_map/all_to_all | solution.py:512
  24.0 1.2 %shard_map.191 = (bf16[192,1920]{1,0:T(8,128)(2,1)S(1)}, bf16[192,384]{1,0:T(8,128)(2,1)S(1)}) custom-call(bf16[192,1536]{1,0:T(8,128)(2,1)} %bitcast.24, bf16[192,384]{1,0:T(8,128)(2,1)} %bitcast.27, bf16[192,384]{1,0:T(8,128)(2,1)} %refs_2_.1, bf16[8,72,128]{2,1,0:T(8,128)(2,1)S(1)} %get-tuple-element.72.refs_3_), custom_call_target="tpu_custom_call" | custom-call | tf_op jit(solution)/shard_map/pallas_call | solution.py:62
  25.2 0.0 collective-permute-done.got_ref
  25.2 0.1 shard_map.192
  25.3 4.5 %all-to-all-done.1.got_ref = bf16[8,24,128]{2,1,0:T(8,128)(2,1)S(1)} async-done(((bf16[8,24,128]{2,1,0:T(8,128)(2,1)}), bf16[8,24,128]{2,1,0:T(8,128)(2,1)S(1)}, u32[]{:S(2)}, u32[]{:S(2)}) %all-to-all-start.1) | async-done | bytes 49184 | tf_op jit(solution)/shard_map/all_to_all | solution.py:512
  29.8 1.5 %shard_map.193 = (bf16[384,1536]{1,0:T(8,128)(2,1)S(1)}, bf16[8,72,128]{2,1,0:T(8,128)(2,1)S(1)}, bf16[8,72,128]{2,1,0:T(8,128)(2,1)S(1)}, f32[1,192]{1,0:T(1,128)S(1)}) custom-call(s32[1]{0:T(128)} %bitcast.head_ref, bf16[8,24,128]{2,1,0:T(8,128)(2,1)S(1)} %all-to-all-done.1.got_ref, bf16[192,1920]{1,0:T(8,128)(2,1)S(1)} %get-tuple-element.75.both_ref, ...), custom_call_target="tpu_custom_call" | custom-call | tf_op jit(solution)/shard_map/pallas_call | solution.py:62
  31.3 0.1 collective-permute-start.1
  31.3 1.6 %collective-permute-start.2 = (bf16[4,72,128]{2,1,0:T(8,128)(2,1)S(1)}, bf16[4,72,128]{2,1,0:T(8,128)(2,1)S(1)}, u32[]{:S(2)}, u32[]{:S(2)}) collective-permute-start(bf16[4,72,128]{2,1,0:T(8,128)(2,1)S(1)} %get-tuple-element.84), channel_id=1, source_target_pairs={{0,2},{2,0},{1,3},{3,1},{4,6},{6,4},{5,7},{7,5},{8,10},{10,8},{9,1... | collective-permute-start | bytes 221192 | tf_op jit(solution)/shard_map/ppermute | solution.py:545
  32.9 1.3 %shard_map.194.refs_5_ = bf16[192,1536]{1,0:T(8,128)(2,1)} custom-call(bf16[192,384]{1,0:T(8,128)(2,1)S(1)} %get-tuple-element.73.win_ref, bf16[384,1536]{1,0:T(8,128)(2,1)S(1)} %get-tuple-element.80.dpre_ref, bf16[8,72,128]{2,1,0:T(8,128)(2,1)S(1)} %get-tuple-element.81.after_ref), custom_call_target="tpu_custom_call" | custom-call | tf_op jit(solution)/shard_map/pallas_call | solution.py:62
  34.2 1.8 %collective-permute-done.2.refs_4_ = bf16[4,72,128]{2,1,0:T(8,128)(2,1)S(1)} collective-permute-done((bf16[4,72,128]{2,1,0:T(8,128)(2,1)S(1)}, bf16[4,72,128]{2,1,0:T(8,128)(2,1)S(1)}, u32[]{:S(2)}, u32[]{:S(2)}) %collective-permute-start.2) | collective-permute-done | bytes 73760 | tf_op jit(solution)/shard_map/ppermute | solution.py:545
  36.0 0.0 collective-permute-done.1.refs_2_
  36.0 0.1 shard_map.195
  36.1 10.9 %all_to_all.20.got_ref = bf16[8,112,128]{2,1,0:T(8,128)(2,1)S(1)} all-to-all(bf16[8,112,128]{2,1,0:T(8,128)(2,1)S(1)} %shard_map.195), channel_id=1, replica_groups=mesh['groups'=2,'geom'=4,'design'=2,'head'=2] {'geom','design'}, dimensions={0} | all-to-all | bytes 458752 | tf_op jit(solution)/shard_map/all_to_all | solution.py:565
  47.0 13.2 %all_to_all.21.half_ref = bf16[8,144,128]{2,1,0:T(8,128)(2,1)S(1)} all-to-all(bf16[8,144,128]{2,1,0:T(8,128)(2,1)S(1)} %get-tuple-element.85), channel_id=1, replica_groups=mesh['groups'=2,'geom'=4,'design'=2,'head'=2] {'geom','design'}, dimensions={0} | all-to-all | bytes 589824 | tf_op jit(solution)/shard_map/all_to_all | solution.py:571
  60.2 0.0 collective-permute-start.3
  60.2 0.9 %shard_map.197 = (f32[192,192]{1,0:T(8,128)}, f32[192,192]{1,0:T(8,128)}, f32[192,384]{1,0:T(8,128)}, f32[192,192]{1,0:T(8,128)}, f32[192,192]{1,0:T(8,128)}, /*index=5*/f32[192,384]{1,0:T(8,128)}, f32[1,192]{1,0:T(1,128)}) custom-call(s32[1]{0:T(128)} %bitcast.head_ref, bf16[8,144,128]{2,1,0:T(8,128)(2,1)S(1)} %all_to_all.21.half_ref, ...), custom_call_target="tpu_custom_call" | custom-call | tf_op jit(solution)/shard_map/pallas_call | solution.py:62
  61.1 0.7 %collective-permute-done.3.half_ref = bf16[8,144,128]{2,1,0:T(8,128)(2,1)S(1)} collective-permute-done((bf16[8,144,128]{2,1,0:T(8,128)(2,1)S(1)}, bf16[8,144,128]{2,1,0:T(8,128)(2,1)S(1)}, u32[]{:S(2)}, u32[]{:S(2)}) %collective-permute-start.3) | collective-permute-done | bytes 294944 | tf_op jit(solution)/shard_map/ppermute | solution.py:572
  61.8 1.0 %shard_map.198 = (f32[192,192]{1,0:T(8,128)}, f32[192,192]{1,0:T(8,128)}, f32[192,384]{1,0:T(8,128)}, f32[192,192]{1,0:T(8,128)}, f32[192,192]{1,0:T(8,128)}, /*index=5*/f32[192,384]{1,0:T(8,128)}, f32[1,192]{1,0:T(1,128)}) custom-call(s32[1]{0:T(128)} %bitcast.head_ref, ...), custom_call_target="tpu_custom_call", output_to_operand_aliasing={{0}: (3, {}), {1}: (4, {}), {2}: (5, {}), {3}: (6, {}), {4}... | custom-call | tf_op jit(solution)/shard_map/pallas_call | solution.py:62
  (1 shorter events, 0.0 us)
Async XLA Ops:
  3.8 12.7 %all-to-all-start = ((bf16[8,16,384]{2,1,0:T(8,128)(2,1)}), bf16[8,16,384]{2,1,0:T(8,128)(2,1)S(1)}, u32[]{:S(2)}, u32[]{:S(2)}) async-start(bf16[8,16,384]{2,1,0:T(8,128)(2,1)} %get-tuple-element.55), calls=%async_computation | async-start | bytes 196608 | tf_op jit(solution)/shard_map/all_to_all | solution.py:481
  20.7 4.5 %collective-permute-start = (bf16[8,72,128]{2,1,0:T(8,128)(2,1)S(1)}, bf16[8,72,128]{2,1,0:T(8,128)(2,1)S(1)}, u32[]{:S(2)}, u32[]{:S(2)}) collective-permute-start(bf16[8,72,128]{2,1,0:T(8,128)(2,1)S(1)} %get-tuple-element.72.refs_3_), channel_id=1, source_target_pairs={{0,1},{1,0},{2,3},{3,2},{4,5},{5,4},{6,7},{7,6},{8,9},{9,8},{10,11... | collective-permute-start | bytes 442376 | tf_op jit(solution)/shard_map/ppermute | solution.py:534
  20.7 9.1 %all-to-all-start.1 = ((bf16[8,24,128]{2,1,0:T(8,128)(2,1)}), bf16[8,24,128]{2,1,0:T(8,128)(2,1)S(1)}, u32[]{:S(2)}, u32[]{:S(2)}) async-start(bf16[8,24,128]{2,1,0:T(8,128)(2,1)} %get-tuple-element.74), calls=%async_computation.1 | async-start | bytes 98304 | tf_op jit(solution)/shard_map/all_to_all | solution.py:512
  31.3 4.8 %collective-permute-start.1 = (bf16[8,72,128]{2,1,0:T(8,128)(2,1)S(1)}, bf16[8,72,128]{2,1,0:T(8,128)(2,1)S(1)}, u32[]{:S(2)}, u32[]{:S(2)}) collective-permute-start(bf16[8,72,128]{2,1,0:T(8,128)(2,1)S(1)} %get-tuple-element.81.after_ref), channel_id=1, source_target_pairs={{0,1},{1,0},{2,3},{3,2},{4,5},{5,4},{6,7},{7,6},{8,9},{9,8},{10,11... | collective-permute-start | bytes 442376 | tf_op jit(solution)/shard_map/ppermute | solution.py:556
  31.3 4.7 %collective-permute-start.2 = (bf16[4,72,128]{2,1,0:T(8,128)(2,1)S(1)}, bf16[4,72,128]{2,1,0:T(8,128)(2,1)S(1)}, u32[]{:S(2)}, u32[]{:S(2)}) collective-permute-start(bf16[4,72,128]{2,1,0:T(8,128)(2,1)S(1)} %get-tuple-element.84), channel_id=1, source_target_pairs={{0,2},{2,0},{1,3},{3,1},{4,6},{6,4},{5,7},{7,5},{8,10},{10,8},{9,1... | collective-permute-start | bytes 221192 | tf_op jit(solution)/shard_map/ppermute | solution.py:545
  60.2 1.6 %collective-permute-start.3 = (bf16[8,144,128]{2,1,0:T(8,128)(2,1)S(1)}, bf16[8,144,128]{2,1,0:T(8,128)(2,1)S(1)}, u32[]{:S(2)}, u32[]{:S(2)}) collective-permute-start(bf16[8,144,128]{2,1,0:T(8,128)(2,1)S(1)} %all_to_all.21.half_ref), channel_id=1, source_target_pairs={{0,1},{1,0},{2,3},{3,2},{4,5},{5,4},{6,7},{7,6},{8,9},{9,8},{10,11... | collective-permute-start | bytes 884744 | tf_op jit(solution)/shard_map/ppermute | solution.py:572

commit v5 on v4

--- a/solution.py
+++ b/solution.py
@@ -37,7 +37,7 @@
     return tuple(Held(value, pltpu.VMEM) for value in values)
 
 
-def call(kernel, outs, *args, scratch=(), smem=0, final=(), raw=(), update=False):
+def call(kernel, outs, *args, scratch=(), smem=0, final=(), raw=(), update=False, direct=()):
     held = [Held(arg, None) for arg in args[:smem]]
     held += [arg if isinstance(arg, Held) else Held(arg, pltpu.HBM) for arg in args[smem:]]
     specs = [pl.BlockSpec(memory_space=pltpu.SMEM)] * smem
@@ -53,8 +53,11 @@
         for arg in held
     ]
     if update:
-        aliases = {len(operands) - len(raw) + place: place for place in range(len(raw))}
+        first = len(operands) - len(outs)
+        aliases = {first + place: place for place in range(len(outs))} if len(raw) > 1 else {}
         return build(kernel, outs, operands, specs, scratch, range(len(outs)), aliases, pl.ANY)
+    if direct:
+        return build(kernel, outs, operands, specs, scratch, direct, None, pl.ANY)
     return build(kernel, outs, operands, specs, scratch, final)
 
 
@@ -165,7 +168,7 @@
 def attend_kernel(
     blocks, size, per_owner,
     got_ref, gain_ref, wk_ref, wv_ref, q_ref, dmix_ref,
-    rows_ref, normed_ref, k_ref, v_ref, p_ref, ds_ref, kt_ref, vt_ref,
+    rows_ref, normed_ref, kv_ref, p_ref, ds_ref, kvt_ref,
 ):
     owners, rows, both = got_ref.shape
     width = both // 2
@@ -195,8 +198,7 @@
     normed_ref[...] = normed
     keys = dg(normed, wk_ref[...], 1, 0).astype(BF)
     values = dg(normed, wv_ref[...], 1, 0).astype(BF)
-    k_ref[...] = keys
-    v_ref[...] = values
+    kv_ref[...] = jnp.concatenate([keys, values], axis=1)
     depth = width // HEADS
     scale = 1.0 / depth**0.5
     key_parts, value_parts = [], []
@@ -218,8 +220,7 @@
         value_parts.append(dg(probs_bf, dmix, 1, 1))
     kt = jnp.concatenate(key_parts, axis=1).astype(BF)
     vt = jnp.concatenate(value_parts, axis=1).astype(BF)
-    kt_ref[...] = kt
-    vt_ref[...] = vt
+    kvt_ref[...] = jnp.concatenate([kt, vt], axis=1)
     dnorm = dg(kt, wk_ref[...], 1, 1) + dg(vt, wv_ref[...], 1, 1)
     dgain = jnp.sum(dnorm * unit, axis=0, keepdims=True)
     scaled = dnorm * gain
@@ -271,38 +272,40 @@
     send_ref[...] = scratch[pl.ds((1 - head) * half, half)].astype(send_ref.dtype)
 
 
-def fetch_kernel(*refs):
-    *refs, sems = refs
-    count = len(refs) // 2
-    sources, (both, *rest) = refs[:count], refs[count + 1 :]
-    points = sources[0].shape[1]
-    targets = [both.at[:, :points], both.at[:, points:]] + rest
-    copies = [
-        pltpu.make_async_copy(source, target, sems.at[place])
-        for place, (source, target) in enumerate(zip(sources, targets))
+def fetch_kernel(mixed_ref, wp_ref, x_ref, wout_ref, win_ref, _, both_ref, win_out, out_ref, att_ref, sems):
+    points = x_ref.shape[1]
+    pairs = [
+        (x_ref, both_ref.at[:, :points]),
+        (wout_ref, both_ref.at[:, points:]),
+        (win_ref, win_out),
     ]
+    copies = [pltpu.make_async_copy(*pair, sems.at[place]) for place, pair in enumerate(pairs)]
     for copy in copies:
         copy.start()
+    att_ref[...] = dg(wp_ref[...], mixed_ref[...], 0, 0).astype(BF)
+    copies.append(pltpu.make_async_copy(att_ref, out_ref, sems.at[3]))
+    copies[3].start()
     for copy in copies:
         copy.wait()
 
 
 def finish_kernel(
-    chunk, head_ref, p_ref, ds_ref, k_ref, v_ref, kt_ref, vt_ref, normed_ref, x_ref, g_ref,
-    wp_ref, out_ref, keep_ref, send_ref, mixed_ref, dq_ref, pack_ref,
+    chunk, head_ref, p_ref, ds_ref, kv_ref, kvt_ref, normed_ref, x_ref, g_ref,
+    mixed_ref, keep_ref, send_ref, dq_ref, pack_ref,
 ):
-    width = k_ref.shape[1]
+    width = normed_ref.shape[1]
     depth = width // HEADS
+    k_ref, v_ref = kv_ref[:, :width], kv_ref[:, width:]
+    kvt = dg(normed_ref[...], kvt_ref[...], 0, 0)
     for head in range(HEADS):
         part = slice(head * depth, (head + 1) * depth)
         mixed_ref[part, :] = dg(v_ref[:, part], p_ref[head], 0, 0).astype(BF)
         dq_ref[part, :] = dg(k_ref[:, part], ds_ref[head], 0, 0).astype(BF)
     mixed = mixed_ref[...]
-    out_ref[...] = dg(wp_ref[...], mixed, 0, 0).astype(BF)
     mats = [
         dg(x_ref[...], dq_ref[...], 1, 1),
-        dg(normed_ref[...], kt_ref[...], 0, 0),
-        dg(normed_ref[...], vt_ref[...], 0, 0),
+        kvt[:, :width],
+        kvt[:, width:],
         dg(mixed, g_ref[...], 1, 1),
     ]
     if pack_ref.shape[1] > chunk:
@@ -327,17 +330,21 @@
     total = jnp.concatenate([total[:rows], rest], axis=1)
     gain_ref[...] = total[blocks : blocks + 1]
     grad = total[: hsum_ref.shape[0]].astype(BF)
-    dhid = dg(wout_ref[...], grad, 0, 1)
-    for block in range(blocks):
-        cols = pl.ds(block * size, size)
-        dpre_ref[:, cols] = (slope_ref[:, cols].astype(F32) * dhid[:, block : block + 1]).astype(BF)
+    dhid = jnp.concatenate(split_bf(dg(grad, wout_ref[...], 1, 0)), axis=0)
+    step = 4 if blocks % 4 == 0 else 1
+    for first in range(0, blocks, step):
+        cols = pl.ds(first * size, step * size)
+        shape = (dhid.shape[0], step * size)
+        pick = iota(shape, 0) % grad.shape[0] == first + iota(shape, 1) // size
+        spread = dg(dhid, pick.astype(F32).astype(BF), 0, 0)
+        dpre_ref[:, cols] = (slope_ref[:, cols].astype(F32) * spread).astype(BF)
     gin = dg(x_ref[...], dpre_ref[...], 1, 1)
-    high, low = split_bf(hsum_ref[...])
-    gout = dg(grad, high, 0, 0) + dg(grad, low, 0, 0)
+    hsum = jnp.concatenate(split_bf(hsum_ref[...]), axis=0)
+    gout = dg(jnp.concatenate([grad, grad], axis=0), hsum, 0, 0)
     start = 0
     for mat in (gin, gout):
         for lane in range(0, mat.shape[1], LANES):
-            put_rows(pack_ref, chunk, start, mat[:, lane : lane + LANES])
+            put_rows(pack_ref, chunk, start, mat[:, lane : lane + LANES].astype(BF))
             start += width
     swap_halves(head_ref, pack_ref, keep_ref, send_ref)
 
@@ -393,10 +400,10 @@
         out_ref[peer, shares * part :, :] = total
 
 
-def unpack_kernel(shares, part, chunk_a, chunk_p, flip, head_ref, half_ref, gain_ref, *refs):
+def unpack_kernel(shares, part, chunk_a, chunk_p, flip, head_ref, half_ref, gain_ref, point_ref, *refs):
     left_ref, right_ref, wide_ref, sems = refs[-4:]
-    targets = refs[-11:-5]
-    gain_out = refs[-5]
+    targets = refs[-12:-6]
+    gain_out, point_out = refs[-6:-4]
     width = left_ref.shape[0]
     rows_a = shares * part
 
@@ -421,8 +428,12 @@
     left_ref[:, LANES:] = pair[:, :rest]
     right_ref[:, LANES:] = pair[:, rest:]
     if not flip:
-        extra = pltpu.make_async_copy(gain_ref, gain_out, sems.at[3])
-        extra.start()
+        extras = [
+            pltpu.make_async_copy(gain_ref, gain_out, sems.at[3]),
+            pltpu.make_async_copy(point_ref, point_out, sems.at[4]),
+        ]
+        for extra in extras:
+            extra.start()
     half = 1 - head_ref[0] if flip else head_ref[0]
     for which in range(2):
 
@@ -440,7 +451,8 @@
                 copy.wait()
 
     if not flip:
-        extra.wait()
+        for extra in extras:
+            extra.wait()
 
 
 def on_device(
@@ -495,39 +507,34 @@
         qt, gt, w_query, w_proj, w_key, w_value, norm_gain.reshape(1, width), xt, w_in,
     )
     pair_shape = (HEADS, anchors, queries)
-    rows_out, normed, keys, values, probs, dscore, kt, vt = call(
+    rows_out, normed, kv, probs, dscore, kvt = call(
         functools.partial(attend_kernel, blocks, size, per_owner),
         [
             ((owners, rows * width // LANES, LANES), BF),
             ((anchors, width), BF),
-            ((anchors, width), BF),
-            ((anchors, width), BF),
+            ((anchors, 2 * width), BF),
             (pair_shape, BF),
             (pair_shape, BF),
-            ((anchors, width), BF),
-            ((anchors, width), BF),
+            ((anchors, 2 * width), BF),
         ],
         *near(got, gain_row, wk, wv, qp, dmix),
     )
     back = lax.all_to_all(rows_out, team, 0, 0, tiled=True)
     shape_a = ((peers, rows_a, LANES), BF)
-    attended, keep_a, send_a = call(
+    mixed, keep_a, send_a = call(
         functools.partial(finish_kernel, chunk_a),
         [((width, queries), BF), shape_a, shape_a],
-        head, *near(probs, dscore, keys, values, kt, vt, normed, qn, gn, wpn),
-        scratch=[
-            pltpu.VMEM((width, queries), BF),
-            pltpu.VMEM((width, queries), BF),
-            pltpu.VMEM((pieces, rows_a, LANES), F32),
-        ],
+        head, *near(probs, dscore, kv, kvt, normed, qn, gn),
+        scratch=[pltpu.VMEM((width, queries), BF), pltpu.VMEM((pieces, rows_a, LANES), F32)],
         smem=1,
-        final=(0,),
-    )
-    both, win = call(
+    )
+    both, win, attended = call(
         fetch_kernel,
-        [((width, points + hid), BF), ((width, hid), BF)],
-        scratch=[pltpu.SemaphoreType.DMA((3,))],
+        [((width, points + hid), BF), ((width, hid), BF), ((width, queries), BF)],
+        *near(mixed, wpn),
+        scratch=[pltpu.VMEM((width, queries), BF), pltpu.SemaphoreType.DMA((4,))],
         raw=(xt, wot, w_in) + near(send_a),
+        direct=(2,),
     )
     swap = [(0, 1), (1, 0)]
     shape_p = ((peers, chunk_p, LANES), BF)
@@ -549,18 +556,18 @@
         functools.partial(back_kernel, blocks, chunk_p),
         [((hid, points), BF), shape_p, shape_p, ((1, width), F32)],
         head, *near(back, both, slope, hsum),
-        scratch=[pltpu.VMEM((pieces, chunk_p, LANES), F32)],
+        scratch=[pltpu.VMEM((pieces, chunk_p, LANES), BF)],
         smem=1,
         raw=near(keep_d),
     )
     recv_p = lax.ppermute(send_p, "head", swap)
     (point_grad,) = call(
-        point_grad_kernel, [((width, points), BF)], *near(win, dpre), final=(0,), raw=near(send_p)
+        point_grad_kernel, [((width, points), BF)], *near(win, dpre), raw=near(send_p)
     )
     (joined,) = call(
         functools.partial(join_kernel, shares, part),
         [((peers, top + chunk_p, LANES), BF)],
-        *near(keep_d, keep_p, recv_p, dgain, *recvs_d), raw=(point_grad,),
+        *near(keep_d, keep_p, recv_p, dgain, *recvs_d), raw=near(point_grad),
     )
     scattered = lax.all_to_all(joined, crowd, 0, 0, tiled=True)
     summed, gain = call(
@@ -575,15 +582,15 @@
     for flip, half in ((False, mine), (True, other)):
         grads = call(
             functools.partial(unpack_kernel, shares, part, chunk_a, chunk_p, flip),
-            [square, square, wide] * 2 + [((1, width), F32)],
+            [square, square, wide] * 2 + [((1, width), F32), ((width, points), BF)],
             head, *near(half, gain),
             scratch=[pltpu.VMEM(*square), pltpu.VMEM(*square), pltpu.VMEM(*wide)]
-            + [pltpu.SemaphoreType.DMA((4,))],
+            + [pltpu.SemaphoreType.DMA((5,))],
             smem=1,
-            raw=grads,
+            raw=near(point_grad) + tuple(grads),
             update=True,
         )
-    gq, gk, gin, gv, gp, gout, gain = grads
+    gq, gk, gin, gv, gp, gout, gain, point_grad = grads
     return (
         attended.T[None], point_grad.T[None], gin, gout.T, gq, gk, gv, gp, gain.reshape(width),
     )

time: 63.2 us -> 62.2 us (0.984)
  Pallas kernels: 16.2 us -> 14.6 us
    pallas_call x12, Pallas kernels: 16.2 us -> 14.6 us  [build(): pl.pallas_call(kernel, out_shape=[jax.ShapeDtypeStruct(shape, dtype) if I...]
    ppermute x1, waiting for transfers between devices: 1.81 us -> 2.64 us  [on_device(): lax.ppermute(send, 'design', [(i, (i + shift) % shares) for i in range(sh...]
  transfers between devices with their start and end apart: 6 -> 6, of which waited for: 4 -> 4; matrix products, arithmetic and copies ran while one was open for 0% -> 0% of each run, Pallas kernels for 10% -> 9%
where the time goes in v5:
time: 62.2 us; the launch traced here: 61.8 us
  blocking collectives  24.1 us (39%)
  Pallas kernels  14.6 us (23%)
  starting transfers between devices  11.4 us (18%)
  waiting for transfers between devices  11 us (18%)
  between operations  0.74 us (1%)
    pallas_call x12, Pallas kernels, build(): pl.pallas_call(kernel, out_shape=[jax.ShapeDtypeStruct(shape, dtype) if I...  14.6 us
    all_to_all x1, blocking collectives, on_device(): mine = lax.all_to_all(summed, crowd, 0, 0, tiled=True)  13.2 us
    all_to_all x1, blocking collectives, on_device(): scattered = lax.all_to_all(joined, crowd, 0, 0, tiled=True)  10.9 us
    all_to_all x1, starting transfers between devices, on_device(): got = lax.all_to_all(send, team, 0, 0, tiled=True)  6.35 us
    all_to_all x1, waiting for transfers between devices, on_device(): back = lax.all_to_all(rows_out, team, 0, 0, tiled=True)  4.4 us
    all_to_all x1, waiting for transfers between devices, on_device(): got = lax.all_to_all(send, team, 0, 0, tiled=True)  3.42 us
    all_to_all x1, starting transfers between devices, on_device(): back = lax.all_to_all(rows_out, team, 0, 0, tiled=True)  3.36 us
    ppermute x1, waiting for transfers between devices, on_device(): lax.ppermute(send, 'design', [(i, (i + shift) % shares) for i in range(sh...  2.64 us
  transfers between devices with their start and end apart: 6, of which 4 were waited for; matrix products, arithmetic and copies ran while one was open for 0% of the time, Pallas kernels for 9%

profile of v5, /device:TPU:0, one launch (start us, length us, event | category | flops | bytes accessed | tf_op | source)
XLA Modules:
  0.0 61.8 jit_solution(12349742733000239147)
XLA Ops:
  0.6 3.2 %shard_map.187 = (bf16[8,16,384]{2,1,0:T(8,128)(2,1)}, f32[16,384]{1,0:T(8,128)S(1)}) custom-call(bf16[192,1536]{1,0:T(8,128)(2,1)} %bitcast.22, bf16[192,384]{1,0:T(8,128)(2,1)} %win_ref.5, bf16[192,384]{1,0:T(8,128)(2,1)} %bitcast.26, bf16[16,192]{1,0:T(8,128)(2,1)} %bitcast.31, s32[1,12]{1,0:T(1,128)} %id_ref.1), custom_call_target="tpu_custom_call" | custom-call | tf_op jit(solution)/shard_map/pallas_call | solution.py:65
  3.8 6.4 %all-to-all-start = ((bf16[8,16,384]{2,1,0:T(8,128)(2,1)}), bf16[8,16,384]{2,1,0:T(8,128)(2,1)S(1)}, u32[]{:S(2)}, u32[]{:S(2)}) async-start(bf16[8,16,384]{2,1,0:T(8,128)(2,1)} %get-tuple-element.56), calls=%async_computation | async-start | bytes 196608 | tf_op jit(solution)/shard_map/all_to_all | solution.py:493
  10.2 2.9 %shard_map.188 = (bf16[192,512]{1,0:T(8,128)(2,1)S(1)}, bf16[192,512]{1,0:T(8,128)(2,1)S(1)}, bf16[192,192]{1,0:T(8,128)(2,1)S(1)}, bf16[192,192]{1,0:T(8,128)(2...) custom-call(bf16[192,512]{1,0:T(8,128)(2,1)} %bitcast.29, ...), custom_call_target="tpu_custom_call" | custom-call | tf_op jit(solution)/shard_map/pallas_call | solution.py:65
  13.1 3.4 %all-to-all-done.got_ref = bf16[8,16,384]{2,1,0:T(8,128)(2,1)S(1)} async-done(((bf16[8,16,384]{2,1,0:T(8,128)(2,1)}), bf16[8,16,384]{2,1,0:T(8,128)(2,1)S(1)}, u32[]{:S(2)}, u32[]{:S(2)}) %all-to-all-start) | async-done | bytes 98336 | tf_op jit(solution)/shard_map/all_to_all | solution.py:493
  16.5 2.8 %shard_map.189 = (bf16[8,24,128]{2,1,0:T(8,128)(2,1)}, bf16[128,192]{1,0:T(8,128)(2,1)S(1)}, bf16[128,384]{1,0:T(8,128)(2,1)S(1)}, bf16[3,128,512]{2,1,0:T(8,128...) custom-call(bf16[8,16,384]{2,1,0:T(8,128)(2,1)S(1)} %all-to-all-done.got_ref, ...), custom_call_target="tpu_custom_call" | custom-call | tf_op jit(solution)/shard_map/pallas_call | solution.py:65
  19.3 0.7 %shard_map.190 = (bf16[192,512]{1,0:T(8,128)(2,1)S(1)}, bf16[8,72,128]{2,1,0:T(8,128)(2,1)S(1)}, bf16[8,72,128]{2,1,0:T(8,128)(2,1)S(1)}) custom-call(s32[1]{0:T(128)} %bitcast.head_ref, bf16[3,128,512]{2,1,0:T(8,128)(2,1)S(1)} %get-tuple-element.62.p_ref, bf16[3,128,512]{2,1,0:T(8,128)(2,1)S(1)} %get-tuple-element.63.ds_ref, ...), custom_call_target="tpu_custom_call" | custom-call | tf_op jit(solution)/shard_map/pallas_call | solution.py:65
  20.0 0.1 collective-permute-start
  20.0 3.4 %all-to-all-start.1 = ((bf16[8,24,128]{2,1,0:T(8,128)(2,1)}), bf16[8,24,128]{2,1,0:T(8,128)(2,1)S(1)}, u32[]{:S(2)}, u32[]{:S(2)}) async-start(bf16[8,24,128]{2,1,0:T(8,128)(2,1)} %get-tuple-element.75), calls=%async_computation.1 | async-start | bytes 98304 | tf_op jit(solution)/shard_map/all_to_all | solution.py:522
  23.4 1.3 %shard_map.191 = (bf16[192,1920]{1,0:T(8,128)(2,1)S(1)}, bf16[192,384]{1,0:T(8,128)(2,1)S(1)}, bf16[192,512]{1,0:T(8,128)(2,1)}) custom-call(bf16[192,512]{1,0:T(8,128)(2,1)S(1)} %get-tuple-element.69.mixed_ref, bf16[192,192]{1,0:T(8,128)(2,1)S(1)} %get-tuple-element.70.wp_ref, bf16[192,1536]{1,0:T(8,128)(2,1)} %bitcast.24, bf16[192,384]{1,0:T(8,128)(2,1)} %bitcast.27, ...), custom_call_target="tpu_custom_call" | custom-call | tf_op jit(solution)/shard_map/pallas_call | solution.py:65
  24.7 0.0 collective-permute-done.got_ref
  24.7 0.1 shard_map.192
  24.8 4.4 %all-to-all-done.1.got_ref = bf16[8,24,128]{2,1,0:T(8,128)(2,1)S(1)} async-done(((bf16[8,24,128]{2,1,0:T(8,128)(2,1)}), bf16[8,24,128]{2,1,0:T(8,128)(2,1)S(1)}, u32[]{:S(2)}, u32[]{:S(2)}) %all-to-all-start.1) | async-done | bytes 49184 | tf_op jit(solution)/shard_map/all_to_all | solution.py:522
  29.2 1.1 %shard_map.193 = (bf16[384,1536]{1,0:T(8,128)(2,1)S(1)}, bf16[8,72,128]{2,1,0:T(8,128)(2,1)S(1)}, bf16[8,72,128]{2,1,0:T(8,128)(2,1)S(1)}, f32[1,192]{1,0:T(1,128)S(1)}) custom-call(s32[1]{0:T(128)} %bitcast.head_ref, bf16[8,24,128]{2,1,0:T(8,128)(2,1)S(1)} %all-to-all-done.1.got_ref, bf16[192,1920]{1,0:T(8,128)(2,1)S(1)} %get-tuple-element.76.both_ref, ...), custom_call_target="tpu_custom_call" | custom-call | tf_op jit(solution)/shard_map/pallas_call | solution.py:65
  30.3 0.1 collective-permute-start.1
  30.4 1.6 %collective-permute-start.2 = (bf16[4,72,128]{2,1,0:T(8,128)(2,1)S(1)}, bf16[4,72,128]{2,1,0:T(8,128)(2,1)S(1)}, u32[]{:S(2)}, u32[]{:S(2)}) collective-permute-start(bf16[4,72,128]{2,1,0:T(8,128)(2,1)S(1)} %get-tuple-element.82), channel_id=1, source_target_pairs={{0,2},{2,0},{1,3},{3,1},{4,6},{6,4},{5,7},{7,5},{8,10},{10,8},{9,1... | collective-permute-start | bytes 221192 | tf_op jit(solution)/shard_map/ppermute | solution.py:552
  31.9 0.5 shard_map.194.refs_5_.point_ref
  32.4 2.6 %collective-permute-done.2.refs_4_ = bf16[4,72,128]{2,1,0:T(8,128)(2,1)S(1)} collective-permute-done((bf16[4,72,128]{2,1,0:T(8,128)(2,1)S(1)}, bf16[4,72,128]{2,1,0:T(8,128)(2,1)S(1)}, u32[]{:S(2)}, u32[]{:S(2)}) %collective-permute-start.2) | collective-permute-done | bytes 73760 | tf_op jit(solution)/shard_map/ppermute | solution.py:552
  35.1 0.0 collective-permute-done.1.refs_2_
  35.1 0.1 shard_map.195
  35.1 10.9 %all_to_all.20.got_ref = bf16[8,112,128]{2,1,0:T(8,128)(2,1)S(1)} all-to-all(bf16[8,112,128]{2,1,0:T(8,128)(2,1)S(1)} %shard_map.195), channel_id=1, replica_groups=mesh['groups'=2,'geom'=4,'design'=2,'head'=2] {'geom','design'}, dimensions={0} | all-to-all | bytes 458752 | tf_op jit(solution)/shard_map/all_to_all | solution.py:572
  46.1 13.2 %all_to_all.21.half_ref = bf16[8,144,128]{2,1,0:T(8,128)(2,1)S(1)} all-to-all(bf16[8,144,128]{2,1,0:T(8,128)(2,1)S(1)} %get-tuple-element.85), channel_id=1, replica_groups=mesh['groups'=2,'geom'=4,'design'=2,'head'=2] {'geom','design'}, dimensions={0} | all-to-all | bytes 589824 | tf_op jit(solution)/shard_map/all_to_all | solution.py:578
  59.3 0.0 collective-permute-start.3
  59.3 1.1 %shard_map.197 = (f32[192,192]{1,0:T(8,128)}, f32[192,192]{1,0:T(8,128)}, f32[192,384]{1,0:T(8,128)}, f32[192,192]{1,0:T(8,128)}, f32[192,192]{1,0:T(8,128)}, /*...) custom-call(s32[1]{0:T(128)} %bitcast.head_ref, bf16[8,144,128]{2,1,0:T(8,128)(2,1)S(1)} %all_to_all.21.half_ref, ...), custom_call_target="tpu_custom_call" | custom-call | tf_op jit(solution)/shard_map/pallas_call | solution.py:65
  60.4 0.5 collective-permute-done.3.half_ref
  60.9 1.0 %shard_map.198 = (f32[192,192]{1,0:T(8,128)}, f32[192,192]{1,0:T(8,128)}, f32[192,384]{1,0:T(8,128)}, f32[192,192]{1,0:T(8,128)}, f32[192,192]{1,0:T(8,128)}, /*...) custom-call(s32[1]{0:T(128)} %bitcast.head_ref, ...), custom_call_target="tpu_custom_call", output_to_operand_aliasing={{0}: (4, {}), {1}: (5, {}), {2}: (6, {}), {3}: (7, {}), {4}... | custom-call | tf_op jit(solution)/shard_map/pallas_call | solution.py:65
  (1 shorter events, 0.0 us)
Async XLA Ops:
  3.8 12.7 %all-to-all-start = ((bf16[8,16,384]{2,1,0:T(8,128)(2,1)}), bf16[8,16,384]{2,1,0:T(8,128)(2,1)S(1)}, u32[]{:S(2)}, u32[]{:S(2)}) async-start(bf16[8,16,384]{2,1,0:T(8,128)(2,1)} %get-tuple-element.56), calls=%async_computation | async-start | bytes 196608 | tf_op jit(solution)/shard_map/all_to_all | solution.py:493
  20.0 4.7 %collective-permute-start = (bf16[8,72,128]{2,1,0:T(8,128)(2,1)S(1)}, bf16[8,72,128]{2,1,0:T(8,128)(2,1)S(1)}, u32[]{:S(2)}, u32[]{:S(2)}) collective-permute-start(bf16[8,72,128]{2,1,0:T(8,128)(2,1)S(1)} %get-tuple-element.71._), channel_id=1, source_target_pairs={{0,1},{1,0},{2,3},{3,2},{4,5},{5,4},{6,7},{7,6},{8,9},{9,8},{10,11... | collective-permute-start | bytes 442376 | tf_op jit(solution)/shard_map/ppermute | solution.py:541
  20.0 9.1 %all-to-all-start.1 = ((bf16[8,24,128]{2,1,0:T(8,128)(2,1)}), bf16[8,24,128]{2,1,0:T(8,128)(2,1)S(1)}, u32[]{:S(2)}, u32[]{:S(2)}) async-start(bf16[8,24,128]{2,1,0:T(8,128)(2,1)} %get-tuple-element.75), calls=%async_computation.1 | async-start | bytes 98304 | tf_op jit(solution)/shard_map/all_to_all | solution.py:522
  30.3 4.8 %collective-permute-start.1 = (bf16[8,72,128]{2,1,0:T(8,128)(2,1)S(1)}, bf16[8,72,128]{2,1,0:T(8,128)(2,1)S(1)}, u32[]{:S(2)}, u32[]{:S(2)}) collective-permute-start(bf16[8,72,128]{2,1,0:T(8,128)(2,1)S(1)} %get-tuple-element.80.after_ref), channel_id=1, source_target_pairs={{0,1},{1,0},{2,3},{3,2},{4,5},{5,4},{6,7},{7,6},{8,9},{9,8},{10,11... | collective-permute-start | bytes 442376 | tf_op jit(solution)/shard_map/ppermute | solution.py:563
  30.4 4.7 %collective-permute-start.2 = (bf16[4,72,128]{2,1,0:T(8,128)(2,1)S(1)}, bf16[4,72,128]{2,1,0:T(8,128)(2,1)S(1)}, u32[]{:S(2)}, u32[]{:S(2)}) collective-permute-start(bf16[4,72,128]{2,1,0:T(8,128)(2,1)S(1)} %get-tuple-element.82), channel_id=1, source_target_pairs={{0,2},{2,0},{1,3},{3,1},{4,6},{6,4},{5,7},{7,5},{8,10},{10,8},{9,1... | collective-permute-start | bytes 221192 | tf_op jit(solution)/shard_map/ppermute | solution.py:552
  59.3 1.6 %collective-permute-start.3 = (bf16[8,144,128]{2,1,0:T(8,128)(2,1)S(1)}, bf16[8,144,128]{2,1,0:T(8,128)(2,1)S(1)}, u32[]{:S(2)}, u32[]{:S(2)}) collective-permute-start(bf16[8,144,128]{2,1,0:T(8,128)(2,1)S(1)} %all_to_all.21.half_ref), channel_id=1, source_target_pairs={{0,1},{1,0},{2,3},{3,2},{4,5},{5,4},{6,7},{7,6},{8,9},{9,8},{10,11... | collective-permute-start | bytes 884744 | tf_op jit(solution)/shard_map/ppermute | solution.py:579

commit v6 on v5

--- a/solution.py
+++ b/solution.py
@@ -17,6 +17,7 @@
 F32 = jnp.float32
 GELU_C = 0.7978845608028654
 GELU_A = 0.044715
+LOG2E = 1.4426950408889634
 
 
 def dg(a, b, ca, cb):
@@ -54,7 +55,7 @@
     ]
     if update:
         first = len(operands) - len(outs)
-        aliases = {first + place: place for place in range(len(outs))} if len(raw) > 1 else {}
+        aliases = {first + place: place for place in range(len(outs))} if len(raw) > 2 else {}
         return build(kernel, outs, operands, specs, scratch, range(len(outs)), aliases, pl.ANY)
     if direct:
         return build(kernel, outs, operands, specs, scratch, direct, None, pl.ANY)
@@ -206,9 +207,9 @@
         part = slice(head * depth, (head + 1) * depth)
         q = q_ref[part, :]
         dmix = dmix_ref[part, :]
-        scores = dg(keys[:, part], q, 1, 0) * scale
+        scores = dg(keys[:, part], q, 1, 0)
         top = jnp.max(scores, axis=0, keepdims=True)
-        weight = jnp.exp(scores - top)
+        weight = jnp.exp2((scores - top) * (scale * LOG2E))
         probs = weight * (1.0 / jnp.sum(weight, axis=0, keepdims=True))
         probs_bf = probs.astype(BF)
         p_ref[head] = probs_bf
@@ -272,7 +273,7 @@
     send_ref[...] = scratch[pl.ds((1 - head) * half, half)].astype(send_ref.dtype)
 
 
-def fetch_kernel(mixed_ref, wp_ref, x_ref, wout_ref, win_ref, _, both_ref, win_out, out_ref, att_ref, sems):
+def fetch_kernel(mixed_ref, wp_ref, x_ref, wout_ref, win_ref, _, both_ref, win_out, att_ref, sems):
     points = x_ref.shape[1]
     pairs = [
         (x_ref, both_ref.at[:, :points]),
@@ -283,8 +284,6 @@
     for copy in copies:
         copy.start()
     att_ref[...] = dg(wp_ref[...], mixed_ref[...], 0, 0).astype(BF)
-    copies.append(pltpu.make_async_copy(att_ref, out_ref, sems.at[3]))
-    copies[3].start()
     for copy in copies:
         copy.wait()
 
@@ -400,10 +399,10 @@
         out_ref[peer, shares * part :, :] = total
 
 
-def unpack_kernel(shares, part, chunk_a, chunk_p, flip, head_ref, half_ref, gain_ref, point_ref, *refs):
+def unpack_kernel(shares, part, chunk_a, chunk_p, flip, head_ref, half_ref, gain_ref, att_ref, point_ref, *refs):
     left_ref, right_ref, wide_ref, sems = refs[-4:]
-    targets = refs[-12:-6]
-    gain_out, point_out = refs[-6:-4]
+    targets = refs[-13:-7]
+    gain_out, point_out, att_out = refs[-7:-4]
     width = left_ref.shape[0]
     rows_a = shares * part
 
@@ -431,6 +430,7 @@
         extras = [
             pltpu.make_async_copy(gain_ref, gain_out, sems.at[3]),
             pltpu.make_async_copy(point_ref, point_out, sems.at[4]),
+            pltpu.make_async_copy(att_ref, att_out, sems.at[5]),
         ]
         for extra in extras:
             extra.start()
@@ -532,9 +532,8 @@
         fetch_kernel,
         [((width, points + hid), BF), ((width, hid), BF), ((width, queries), BF)],
         *near(mixed, wpn),
-        scratch=[pltpu.VMEM((width, queries), BF), pltpu.SemaphoreType.DMA((4,))],
+        scratch=[pltpu.SemaphoreType.DMA((3,))],
         raw=(xt, wot, w_in) + near(send_a),
-        direct=(2,),
     )
     swap = [(0, 1), (1, 0)]
     shape_p = ((peers, chunk_p, LANES), BF)
@@ -582,15 +581,15 @@
     for flip, half in ((False, mine), (True, other)):
         grads = call(
             functools.partial(unpack_kernel, shares, part, chunk_a, chunk_p, flip),
-            [square, square, wide] * 2 + [((1, width), F32), ((width, points), BF)],
+            [square, square, wide] * 2 + [((1, width), F32), ((width, points), BF), ((width, queries), BF)],
             head, *near(half, gain),
             scratch=[pltpu.VMEM(*square), pltpu.VMEM(*square), pltpu.VMEM(*wide)]
-            + [pltpu.SemaphoreType.DMA((5,))],
+            + [pltpu.SemaphoreType.DMA((6,))],
             smem=1,
-            raw=near(point_grad) + tuple(grads),
+            raw=near(attended, point_grad) + tuple(grads),
             update=True,
         )
-    gq, gk, gin, gv, gp, gout, gain, point_grad = grads
+    gq, gk, gin, gv, gp, gout, gain, point_grad, attended = grads
     return (
         attended.T[None], point_grad.T[None], gin, gout.T, gq, gk, gv, gp, gain.reshape(width),
     )

time: 62.2 us -> 62.2 us (level)
  no operation moved by 1% of the time
where the time goes in v6:
time: 62.2 us; the launch traced here: 61.8 us
  blocking collectives  24.1 us (39%)
  Pallas kernels  14.6 us (23%)
  starting transfers between devices  11.4 us (18%)
  waiting for transfers between devices  11 us (18%)
  between operations  0.74 us (1%)
    pallas_call x12, Pallas kernels, build(): pl.pallas_call(kernel, out_shape=[jax.ShapeDtypeStruct(shape, dtype) if I...  14.6 us
    all_to_all x1, blocking collectives, on_device(): mine = lax.all_to_all(summed, crowd, 0, 0, tiled=True)  13.2 us
    all_to_all x1, blocking collectives, on_device(): scattered = lax.all_to_all(joined, crowd, 0, 0, tiled=True)  10.9 us
    all_to_all x1, starting transfers between devices, on_device(): got = lax.all_to_all(send, team, 0, 0, tiled=True)  6.35 us
    all_to_all x1, waiting for transfers between devices, on_device(): back = lax.all_to_all(rows_out, team, 0, 0, tiled=True)  4.49 us
    all_to_all x1, waiting for transfers between devices, on_device(): got = lax.all_to_all(send, team, 0, 0, tiled=True)  3.42 us
    all_to_all x1, starting transfers between devices, on_device(): back = lax.all_to_all(rows_out, team, 0, 0, tiled=True)  3.36 us
    ppermute x1, waiting for transfers between devices, on_device(): lax.ppermute(send, 'design', [(i, (i + shift) % shares) for i in range(sh...  2.64 us
  transfers between devices with their start and end apart: 6, of which 4 were waited for; matrix products, arithmetic and copies ran while one was open for 0% of the time, Pallas kernels for 9%

profile of v6, /device:TPU:0, one launch (start us, length us, event | category | flops | bytes accessed | tf_op | source)
XLA Modules:
  0.0 61.8 jit_solution(12576236317155502553)
XLA Ops:
  0.6 3.2 %shard_map.187 = (bf16[8,16,384]{2,1,0:T(8,128)(2,1)}, f32[16,384]{1,0:T(8,128)S(1)}) custom-call(bf16[192,1536]{1,0:T(8,128)(2,1)} %bitcast.22, bf16[192,384]{1,0:T(8,128)(2,1)} %win_ref.5, bf16[192,384]{1,0:T(8,128)(2,1)} %bitcast.26, bf16[16,192]{1,0:T(8,128)(2,1)} %bitcast.32, s32[1,12]{1,0:T(1,128)} %id_ref.1), custom_call_target="tpu_custom_call" | custom-call | tf_op jit(solution)/shard_map/pallas_call | solution.py:66
  3.8 6.4 %all-to-all-start = ((bf16[8,16,384]{2,1,0:T(8,128)(2,1)}), bf16[8,16,384]{2,1,0:T(8,128)(2,1)S(1)}, u32[]{:S(2)}, u32[]{:S(2)}) async-start(bf16[8,16,384]{2,1,0:T(8,128)(2,1)} %get-tuple-element.58), calls=%async_computation | async-start | bytes 196608 | tf_op jit(solution)/shard_map/all_to_all | solution.py:493
  10.2 2.9 %shard_map.188 = (bf16[192,512]{1,0:T(8,128)(2,1)S(1)}, bf16[192,512]{1,0:T(8,128)(2,1)S(1)}, bf16[192,192]{1,0:T(8,128)(2,1)S(1)}, bf16[192,192]{1,0:T(8,128)(2...) custom-call(bf16[192,512]{1,0:T(8,128)(2,1)} %bitcast.30, ...), custom_call_target="tpu_custom_call" | custom-call | tf_op jit(solution)/shard_map/pallas_call | solution.py:66
  13.1 3.4 %all-to-all-done.got_ref = bf16[8,16,384]{2,1,0:T(8,128)(2,1)S(1)} async-done(((bf16[8,16,384]{2,1,0:T(8,128)(2,1)}), bf16[8,16,384]{2,1,0:T(8,128)(2,1)S(1)}, u32[]{:S(2)}, u32[]{:S(2)}) %all-to-all-start) | async-done | bytes 98336 | tf_op jit(solution)/shard_map/all_to_all | solution.py:493
  16.5 2.8 %shard_map.189 = (bf16[8,24,128]{2,1,0:T(8,128)(2,1)}, bf16[128,192]{1,0:T(8,128)(2,1)S(1)}, bf16[128,384]{1,0:T(8,128)(2,1)S(1)}, bf16[3,128,512]{2,1,0:T(8,128...) custom-call(bf16[8,16,384]{2,1,0:T(8,128)(2,1)S(1)} %all-to-all-done.got_ref, ...), custom_call_target="tpu_custom_call" | custom-call | tf_op jit(solution)/shard_map/pallas_call | solution.py:66
  19.3 0.7 %shard_map.190 = (bf16[192,512]{1,0:T(8,128)(2,1)S(1)}, bf16[8,72,128]{2,1,0:T(8,128)(2,1)S(1)}, bf16[8,72,128]{2,1,0:T(8,128)(2,1)S(1)}) custom-call(s32[1]{0:T(128)} %bitcast.head_ref, bf16[3,128,512]{2,1,0:T(8,128)(2,1)S(1)} %get-tuple-element.64.p_ref, bf16[3,128,512]{2,1,0:T(8,128)(2,1)S(1)} %get-tuple-element.65.ds_ref, ...), custom_call_target="tpu_custom_call" | custom-call | tf_op jit(solution)/shard_map/pallas_call | solution.py:66
  20.0 0.1 collective-permute-start
  20.0 3.4 %all-to-all-start.1 = ((bf16[8,24,128]{2,1,0:T(8,128)(2,1)}), bf16[8,24,128]{2,1,0:T(8,128)(2,1)S(1)}, u32[]{:S(2)}, u32[]{:S(2)}) async-start(bf16[8,24,128]{2,1,0:T(8,128)(2,1)} %get-tuple-element.74), calls=%async_computation.1 | async-start | bytes 98304 | tf_op jit(solution)/shard_map/all_to_all | solution.py:522
  23.4 1.2 %shard_map.192 = (bf16[192,1920]{1,0:T(8,128)(2,1)S(1)}, bf16[192,384]{1,0:T(8,128)(2,1)S(1)}, bf16[192,512]{1,0:T(8,128)(2,1)S(1)}) custom-call(bf16[192,512]{1,0:T(8,128)(2,1)S(1)} %get-tuple-element.75.mixed_ref, bf16[192,192]{1,0:T(8,128)(2,1)S(1)} %get-tuple-element.76.wp_ref, bf16[192,1536]{1,0:T(8,128)(2,1)} %bitcast.24, bf16[192,384]{1,0:T(8,128)(2,1)} %bitcast.27, ...), custom_call_target="tpu_custom_call" | custom-call | tf_op jit(solution)/shard_map/pallas_call | solution.py:66
  24.6 0.0 collective-permute-done.got_ref
  24.6 0.1 shard_map.191
  24.7 4.5 %all-to-all-done.1.got_ref = bf16[8,24,128]{2,1,0:T(8,128)(2,1)S(1)} async-done(((bf16[8,24,128]{2,1,0:T(8,128)(2,1)}), bf16[8,24,128]{2,1,0:T(8,128)(2,1)S(1)}, u32[]{:S(2)}, u32[]{:S(2)}) %all-to-all-start.1) | async-done | bytes 49184 | tf_op jit(solution)/shard_map/all_to_all | solution.py:522
  29.2 1.1 %shard_map.193 = (bf16[384,1536]{1,0:T(8,128)(2,1)S(1)}, bf16[8,72,128]{2,1,0:T(8,128)(2,1)S(1)}, bf16[8,72,128]{2,1,0:T(8,128)(2,1)S(1)}, f32[1,192]{1,0:T(1,128)S(1)}) custom-call(s32[1]{0:T(128)} %bitcast.head_ref, bf16[8,24,128]{2,1,0:T(8,128)(2,1)S(1)} %all-to-all-done.1.got_ref, bf16[192,1920]{1,0:T(8,128)(2,1)S(1)} %get-tuple-element.77.both_ref, ...), custom_call_target="tpu_custom_call" | custom-call | tf_op jit(solution)/shard_map/pallas_call | solution.py:66
  30.3 0.1 collective-permute-start.1
  30.4 1.6 %collective-permute-start.2 = (bf16[4,72,128]{2,1,0:T(8,128)(2,1)S(1)}, bf16[4,72,128]{2,1,0:T(8,128)(2,1)S(1)}, u32[]{:S(2)}, u32[]{:S(2)}) collective-permute-start(bf16[4,72,128]{2,1,0:T(8,128)(2,1)S(1)} %get-tuple-element.83), channel_id=1, source_target_pairs={{0,2},{2,0},{1,3},{3,1},{4,6},{6,4},{5,7},{7,5},{8,10},{10,8},{9,1... | collective-permute-start | bytes 221192 | tf_op jit(solution)/shard_map/ppermute | solution.py:551
  31.9 0.5 shard_map.194.refs_5_.point_ref
  32.4 2.6 %collective-permute-done.2.refs_4_ = bf16[4,72,128]{2,1,0:T(8,128)(2,1)S(1)} collective-permute-done((bf16[4,72,128]{2,1,0:T(8,128)(2,1)S(1)}, bf16[4,72,128]{2,1,0:T(8,128)(2,1)S(1)}, u32[]{:S(2)}, u32[]{:S(2)}) %collective-permute-start.2) | collective-permute-done | bytes 73760 | tf_op jit(solution)/shard_map/ppermute | solution.py:551
  35.1 0.0 collective-permute-done.1.refs_2_
  35.1 0.1 shard_map.195
  35.1 10.9 %all_to_all.20.got_ref = bf16[8,112,128]{2,1,0:T(8,128)(2,1)S(1)} all-to-all(bf16[8,112,128]{2,1,0:T(8,128)(2,1)S(1)} %shard_map.195), channel_id=1, replica_groups=mesh['groups'=2,'geom'=4,'design'=2,'head'=2] {'geom','design'}, dimensions={0} | all-to-all | bytes 458752 | tf_op jit(solution)/shard_map/all_to_all | solution.py:571
  46.0 13.2 %all_to_all.21.half_ref = bf16[8,144,128]{2,1,0:T(8,128)(2,1)S(1)} all-to-all(bf16[8,144,128]{2,1,0:T(8,128)(2,1)S(1)} %get-tuple-element.86), channel_id=1, replica_groups=mesh['groups'=2,'geom'=4,'design'=2,'head'=2] {'geom','design'}, dimensions={0} | all-to-all | bytes 589824 | tf_op jit(solution)/shard_map/all_to_all | solution.py:577
  59.3 0.0 collective-permute-start.3
  59.3 1.2 %shard_map.197 = (f32[192,192]{1,0:T(8,128)}, f32[192,192]{1,0:T(8,128)}, f32[192,384]{1,0:T(8,128)}, f32[192,192]{1,0:T(8,128)}, f32[192,192]{1,0:T(8,128)}, /*...) custom-call(s32[1]{0:T(128)} %bitcast.head_ref, ...), custom_call_target="tpu_custom_call" | custom-call | tf_op jit(solution)/shard_map/pallas_call | solution.py:66
  60.4 0.4 collective-permute-done.3.half_ref
  60.8 1.0 %shard_map.198 = (f32[192,192]{1,0:T(8,128)}, f32[192,192]{1,0:T(8,128)}, f32[192,384]{1,0:T(8,128)}, f32[192,192]{1,0:T(8,128)}, f32[192,192]{1,0:T(8,128)}, /*...) custom-call(s32[1]{0:T(128)} %bitcast.head_ref, ...), custom_call_target="tpu_custom_call", output_to_operand_aliasing={{0}: (5, {}), {1}: (6, {}), {2}: (7, {}), {3}: (8, {}), {4}... | custom-call | tf_op jit(solution)/shard_map/pallas_call | solution.py:66
  (1 shorter events, 0.0 us)
Async XLA Ops:
  3.8 12.7 %all-to-all-start = ((bf16[8,16,384]{2,1,0:T(8,128)(2,1)}), bf16[8,16,384]{2,1,0:T(8,128)(2,1)S(1)}, u32[]{:S(2)}, u32[]{:S(2)}) async-start(bf16[8,16,384]{2,1,0:T(8,128)(2,1)} %get-tuple-element.58), calls=%async_computation | async-start | bytes 196608 | tf_op jit(solution)/shard_map/all_to_all | solution.py:493
  20.0 4.6 %collective-permute-start = (bf16[8,72,128]{2,1,0:T(8,128)(2,1)S(1)}, bf16[8,72,128]{2,1,0:T(8,128)(2,1)S(1)}, u32[]{:S(2)}, u32[]{:S(2)}) collective-permute-start(bf16[8,72,128]{2,1,0:T(8,128)(2,1)S(1)} %get-tuple-element.72._), channel_id=1, source_target_pairs={{0,1},{1,0},{2,3},{3,2},{4,5},{5,4},{6,7},{7,6},{8,9},{9,8},{10,11... | collective-permute-start | bytes 442376 | tf_op jit(solution)/shard_map/ppermute | solution.py:540
  20.0 9.1 %all-to-all-start.1 = ((bf16[8,24,128]{2,1,0:T(8,128)(2,1)}), bf16[8,24,128]{2,1,0:T(8,128)(2,1)S(1)}, u32[]{:S(2)}, u32[]{:S(2)}) async-start(bf16[8,24,128]{2,1,0:T(8,128)(2,1)} %get-tuple-element.74), calls=%async_computation.1 | async-start | bytes 98304 | tf_op jit(solution)/shard_map/all_to_all | solution.py:522
  30.3 4.8 %collective-permute-start.1 = (bf16[8,72,128]{2,1,0:T(8,128)(2,1)S(1)}, bf16[8,72,128]{2,1,0:T(8,128)(2,1)S(1)}, u32[]{:S(2)}, u32[]{:S(2)}) collective-permute-start(bf16[8,72,128]{2,1,0:T(8,128)(2,1)S(1)} %get-tuple-element.81.after_ref), channel_id=1, source_target_pairs={{0,1},{1,0},{2,3},{3,2},{4,5},{5,4},{6,7},{7,6},{8,9},{9,8},{10,11... | collective-permute-start | bytes 442376 | tf_op jit(solution)/shard_map/ppermute | solution.py:562
  30.4 4.7 %collective-permute-start.2 = (bf16[4,72,128]{2,1,0:T(8,128)(2,1)S(1)}, bf16[4,72,128]{2,1,0:T(8,128)(2,1)S(1)}, u32[]{:S(2)}, u32[]{:S(2)}) collective-permute-start(bf16[4,72,128]{2,1,0:T(8,128)(2,1)S(1)} %get-tuple-element.83), channel_id=1, source_target_pairs={{0,2},{2,0},{1,3},{3,1},{4,6},{6,4},{5,7},{7,5},{8,10},{10,8},{9,1... | collective-permute-start | bytes 221192 | tf_op jit(solution)/shard_map/ppermute | solution.py:551
  59.3 1.6 %collective-permute-start.3 = (bf16[8,144,128]{2,1,0:T(8,128)(2,1)S(1)}, bf16[8,144,128]{2,1,0:T(8,128)(2,1)S(1)}, u32[]{:S(2)}, u32[]{:S(2)}) collective-permute-start(bf16[8,144,128]{2,1,0:T(8,128)(2,1)S(1)} %all_to_all.21.half_ref), channel_id=1, source_target_pairs={{0,1},{1,0},{2,3},{3,2},{4,5},{5,4},{6,7},{7,6},{8,9},{9,8},{10,11... | collective-permute-start | bytes 884744 | tf_op jit(solution)/shard_map/ppermute | solution.py:578

commit v7 on v6

--- a/solution.py
+++ b/solution.py
@@ -262,7 +262,7 @@
         left, right = mats[first : first + 2]
         pair = jnp.concatenate([left[:, LANES:], right[:, LANES:]], axis=1)
         for slot in (left[:, :LANES], right[:, :LANES], pair):
-            put_rows(ref, chunk, start, slot)
+            put_rows(ref, chunk, start, slot.astype(BF))
             start += width
 
 
@@ -308,7 +308,7 @@
         dg(mixed, g_ref[...], 1, 1),
     ]
     if pack_ref.shape[1] > chunk:
-        pack_ref[:, chunk:, :] = jnp.zeros((pack_ref.shape[0], pack_ref.shape[1] - chunk, LANES), F32)
+        pack_ref[:, chunk:, :] = jnp.zeros((pack_ref.shape[0], pack_ref.shape[1] - chunk, LANES), BF)
     pack_square(pack_ref, chunk, mats)
     swap_halves(head_ref, pack_ref, keep_ref, send_ref)
 
@@ -525,7 +525,7 @@
         functools.partial(finish_kernel, chunk_a),
         [((width, queries), BF), shape_a, shape_a],
         head, *near(probs, dscore, kv, kvt, normed, qn, gn),
-        scratch=[pltpu.VMEM((width, queries), BF), pltpu.VMEM((pieces, rows_a, LANES), F32)],
+        scratch=[pltpu.VMEM((width, queries), BF), pltpu.VMEM((pieces, rows_a, LANES), BF)],
         smem=1,
     )
     both, win, attended = call(

time: 62.2 us -> 62.2 us (level)
  no operation moved by 1% of the time
where the time goes in v7:
time: 62.2 us; the launch traced here: 61.8 us
  blocking collectives  24.1 us (39%)
  Pallas kernels  14.6 us (23%)
  starting transfers between devices  11.4 us (18%)
  waiting for transfers between devices  11 us (18%)
  between operations  0.74 us (1%)
    pallas_call x12, Pallas kernels, build(): pl.pallas_call(kernel, out_shape=[jax.ShapeDtypeStruct(shape, dtype) if I...  14.6 us
    all_to_all x1, blocking collectives, on_device(): mine = lax.all_to_all(summed, crowd, 0, 0, tiled=True)  13.2 us
    all_to_all x1, blocking collectives, on_device(): scattered = lax.all_to_all(joined, crowd, 0, 0, tiled=True)  10.9 us
    all_to_all x1, starting transfers between devices, on_device(): got = lax.all_to_all(send, team, 0, 0, tiled=True)  6.35 us
    all_to_all x1, waiting for transfers between devices, on_device(): back = lax.all_to_all(rows_out, team, 0, 0, tiled=True)  4.49 us
    all_to_all x1, waiting for transfers between devices, on_device(): got = lax.all_to_all(send, team, 0, 0, tiled=True)  3.42 us
    all_to_all x1, starting transfers between devices, on_device(): back = lax.all_to_all(rows_out, team, 0, 0, tiled=True)  3.36 us
    ppermute x1, waiting for transfers between devices, on_device(): lax.ppermute(send, 'design', [(i, (i + shift) % shares) for i in range(sh...  2.64 us
  transfers between devices with their start and end apart: 6, of which 4 were waited for; matrix products, arithmetic and copies ran while one was open for 0% of the time, Pallas kernels for 9%

profile of v7, /device:TPU:0, one launch (start us, length us, event | category | flops | bytes accessed | tf_op | source)
XLA Modules:
  0.0 61.8 jit_solution(7105988498834447403)
XLA Ops:
  0.6 3.2 %shard_map.187 = (bf16[8,16,384]{2,1,0:T(8,128)(2,1)}, f32[16,384]{1,0:T(8,128)S(1)}) custom-call(bf16[192,1536]{1,0:T(8,128)(2,1)} %bitcast.22, bf16[192,384]{1,0:T(8,128)(2,1)} %win_ref.5, bf16[192,384]{1,0:T(8,128)(2,1)} %bitcast.26, bf16[16,192]{1,0:T(8,128)(2,1)} %bitcast.32, s32[1,12]{1,0:T(1,128)} %id_ref.1), custom_call_target="tpu_custom_call" | custom-call | tf_op jit(solution)/shard_map/pallas_call | solution.py:66
  3.8 6.4 %all-to-all-start = ((bf16[8,16,384]{2,1,0:T(8,128)(2,1)}), bf16[8,16,384]{2,1,0:T(8,128)(2,1)S(1)}, u32[]{:S(2)}, u32[]{:S(2)}) async-start(bf16[8,16,384]{2,1,0:T(8,128)(2,1)} %get-tuple-element.58), calls=%async_computation | async-start | bytes 196608 | tf_op jit(solution)/shard_map/all_to_all | solution.py:493
  10.2 2.9 %shard_map.188 = (bf16[192,512]{1,0:T(8,128)(2,1)S(1)}, bf16[192,512]{1,0:T(8,128)(2,1)S(1)}, bf16[192,192]{1,0:T(8,128)(2,1)S(1)}, bf16[192,192]{1,0:T(8,128)(2...) custom-call(bf16[192,512]{1,0:T(8,128)(2,1)} %bitcast.30, ...), custom_call_target="tpu_custom_call" | custom-call | tf_op jit(solution)/shard_map/pallas_call | solution.py:66
  13.1 3.4 %all-to-all-done.got_ref = bf16[8,16,384]{2,1,0:T(8,128)(2,1)S(1)} async-done(((bf16[8,16,384]{2,1,0:T(8,128)(2,1)}), bf16[8,16,384]{2,1,0:T(8,128)(2,1)S(1)}, u32[]{:S(2)}, u32[]{:S(2)}) %all-to-all-start) | async-done | bytes 98336 | tf_op jit(solution)/shard_map/all_to_all | solution.py:493
  16.5 2.8 %shard_map.189 = (bf16[8,24,128]{2,1,0:T(8,128)(2,1)}, bf16[128,192]{1,0:T(8,128)(2,1)S(1)}, bf16[128,384]{1,0:T(8,128)(2,1)S(1)}, bf16[3,128,512]{2,1,0:T(8,128...) custom-call(bf16[8,16,384]{2,1,0:T(8,128)(2,1)S(1)} %all-to-all-done.got_ref, ...), custom_call_target="tpu_custom_call" | custom-call | tf_op jit(solution)/shard_map/pallas_call | solution.py:66
  19.3 0.6 %shard_map.190 = (bf16[192,512]{1,0:T(8,128)(2,1)S(1)}, bf16[8,72,128]{2,1,0:T(8,128)(2,1)S(1)}, bf16[8,72,128]{2,1,0:T(8,128)(2,1)S(1)}) custom-call(s32[1]{0:T(128)} %bitcast.head_ref, bf16[3,128,512]{2,1,0:T(8,128)(2,1)S(1)} %get-tuple-element.64.p_ref, bf16[3,128,512]{2,1,0:T(8,128)(2,1)S(1)} %get-tuple-element.65.ds_ref, ...), custom_call_target="tpu_custom_call" | custom-call | tf_op jit(solution)/shard_map/pallas_call | solution.py:66
  20.0 0.1 collective-permute-start
  20.0 3.4 %all-to-all-start.1 = ((bf16[8,24,128]{2,1,0:T(8,128)(2,1)}), bf16[8,24,128]{2,1,0:T(8,128)(2,1)S(1)}, u32[]{:S(2)}, u32[]{:S(2)}) async-start(bf16[8,24,128]{2,1,0:T(8,128)(2,1)} %get-tuple-element.74), calls=%async_computation.1 | async-start | bytes 98304 | tf_op jit(solution)/shard_map/all_to_all | solution.py:522
  23.4 1.2 %shard_map.192 = (bf16[192,1920]{1,0:T(8,128)(2,1)S(1)}, bf16[192,384]{1,0:T(8,128)(2,1)S(1)}, bf16[192,512]{1,0:T(8,128)(2,1)S(1)}) custom-call(bf16[192,512]{1,0:T(8,128)(2,1)S(1)} %get-tuple-element.75.mixed_ref, bf16[192,192]{1,0:T(8,128)(2,1)S(1)} %get-tuple-element.76.wp_ref, bf16[192,1536]{1,0:T(8,128)(2,1)} %bitcast.24, bf16[192,384]{1,0:T(8,128)(2,1)} %bitcast.27, ...), custom_call_target="tpu_custom_call" | custom-call | tf_op jit(solution)/shard_map/pallas_call | solution.py:66
  24.6 0.0 collective-permute-done.got_ref
  24.6 0.1 shard_map.191
  24.7 4.5 %all-to-all-done.1.got_ref = bf16[8,24,128]{2,1,0:T(8,128)(2,1)S(1)} async-done(((bf16[8,24,128]{2,1,0:T(8,128)(2,1)}), bf16[8,24,128]{2,1,0:T(8,128)(2,1)S(1)}, u32[]{:S(2)}, u32[]{:S(2)}) %all-to-all-start.1) | async-done | bytes 49184 | tf_op jit(solution)/shard_map/all_to_all | solution.py:522
  29.2 1.1 %shard_map.193 = (bf16[384,1536]{1,0:T(8,128)(2,1)S(1)}, bf16[8,72,128]{2,1,0:T(8,128)(2,1)S(1)}, bf16[8,72,128]{2,1,0:T(8,128)(2,1)S(1)}, f32[1,192]{1,0:T(1,128)S(1)}) custom-call(s32[1]{0:T(128)} %bitcast.head_ref, bf16[8,24,128]{2,1,0:T(8,128)(2,1)S(1)} %all-to-all-done.1.got_ref, bf16[192,1920]{1,0:T(8,128)(2,1)S(1)} %get-tuple-element.77.both_ref, ...), custom_call_target="tpu_custom_call" | custom-call | tf_op jit(solution)/shard_map/pallas_call | solution.py:66
  30.3 0.1 collective-permute-start.1
  30.4 1.6 %collective-permute-start.2 = (bf16[4,72,128]{2,1,0:T(8,128)(2,1)S(1)}, bf16[4,72,128]{2,1,0:T(8,128)(2,1)S(1)}, u32[]{:S(2)}, u32[]{:S(2)}) collective-permute-start(bf16[4,72,128]{2,1,0:T(8,128)(2,1)S(1)} %get-tuple-element.83), channel_id=1, source_target_pairs={{0,2},{2,0},{1,3},{3,1},{4,6},{6,4},{5,7},{7,5},{8,10},{10,8},{9,1... | collective-permute-start | bytes 221192 | tf_op jit(solution)/shard_map/ppermute | solution.py:551
  31.9 0.5 shard_map.194.refs_5_.point_ref
  32.4 2.6 %collective-permute-done.2.refs_4_ = bf16[4,72,128]{2,1,0:T(8,128)(2,1)S(1)} collective-permute-done((bf16[4,72,128]{2,1,0:T(8,128)(2,1)S(1)}, bf16[4,72,128]{2,1,0:T(8,128)(2,1)S(1)}, u32[]{:S(2)}, u32[]{:S(2)}) %collective-permute-start.2) | collective-permute-done | bytes 73760 | tf_op jit(solution)/shard_map/ppermute | solution.py:551
  35.1 0.0 collective-permute-done.1.refs_2_
  35.1 0.1 shard_map.195
  35.1 10.9 %all_to_all.20.got_ref = bf16[8,112,128]{2,1,0:T(8,128)(2,1)S(1)} all-to-all(bf16[8,112,128]{2,1,0:T(8,128)(2,1)S(1)} %shard_map.195), channel_id=1, replica_groups=mesh['groups'=2,'geom'=4,'design'=2,'head'=2] {'geom','design'}, dimensions={0} | all-to-all | bytes 458752 | tf_op jit(solution)/shard_map/all_to_all | solution.py:571
  46.0 13.2 %all_to_all.21.half_ref = bf16[8,144,128]{2,1,0:T(8,128)(2,1)S(1)} all-to-all(bf16[8,144,128]{2,1,0:T(8,128)(2,1)S(1)} %get-tuple-element.86), channel_id=1, replica_groups=mesh['groups'=2,'geom'=4,'design'=2,'head'=2] {'geom','design'}, dimensions={0} | all-to-all | bytes 589824 | tf_op jit(solution)/shard_map/all_to_all | solution.py:577
  59.3 0.0 collective-permute-start.3
  59.3 1.2 %shard_map.197 = (f32[192,192]{1,0:T(8,128)}, f32[192,192]{1,0:T(8,128)}, f32[192,384]{1,0:T(8,128)}, f32[192,192]{1,0:T(8,128)}, f32[192,192]{1,0:T(8,128)}, /*...) custom-call(s32[1]{0:T(128)} %bitcast.head_ref, ...), custom_call_target="tpu_custom_call" | custom-call | tf_op jit(solution)/shard_map/pallas_call | solution.py:66
  60.4 0.4 collective-permute-done.3.half_ref
  60.8 1.0 %shard_map.198 = (f32[192,192]{1,0:T(8,128)}, f32[192,192]{1,0:T(8,128)}, f32[192,384]{1,0:T(8,128)}, f32[192,192]{1,0:T(8,128)}, f32[192,192]{1,0:T(8,128)}, /*...) custom-call(s32[1]{0:T(128)} %bitcast.head_ref, ...), custom_call_target="tpu_custom_call", output_to_operand_aliasing={{0}: (5, {}), {1}: (6, {}), {2}: (7, {}), {3}: (8, {}), {4}... | custom-call | tf_op jit(solution)/shard_map/pallas_call | solution.py:66
  (1 shorter events, 0.0 us)
Async XLA Ops:
  3.8 12.7 %all-to-all-start = ((bf16[8,16,384]{2,1,0:T(8,128)(2,1)}), bf16[8,16,384]{2,1,0:T(8,128)(2,1)S(1)}, u32[]{:S(2)}, u32[]{:S(2)}) async-start(bf16[8,16,384]{2,1,0:T(8,128)(2,1)} %get-tuple-element.58), calls=%async_computation | async-start | bytes 196608 | tf_op jit(solution)/shard_map/all_to_all | solution.py:493
  20.0 4.6 %collective-permute-start = (bf16[8,72,128]{2,1,0:T(8,128)(2,1)S(1)}, bf16[8,72,128]{2,1,0:T(8,128)(2,1)S(1)}, u32[]{:S(2)}, u32[]{:S(2)}) collective-permute-start(bf16[8,72,128]{2,1,0:T(8,128)(2,1)S(1)} %get-tuple-element.72._), channel_id=1, source_target_pairs={{0,1},{1,0},{2,3},{3,2},{4,5},{5,4},{6,7},{7,6},{8,9},{9,8},{10,11... | collective-permute-start | bytes 442376 | tf_op jit(solution)/shard_map/ppermute | solution.py:540
  20.0 9.1 %all-to-all-start.1 = ((bf16[8,24,128]{2,1,0:T(8,128)(2,1)}), bf16[8,24,128]{2,1,0:T(8,128)(2,1)S(1)}, u32[]{:S(2)}, u32[]{:S(2)}) async-start(bf16[8,24,128]{2,1,0:T(8,128)(2,1)} %get-tuple-element.74), calls=%async_computation.1 | async-start | bytes 98304 | tf_op jit(solution)/shard_map/all_to_all | solution.py:522
  30.3 4.8 %collective-permute-start.1 = (bf16[8,72,128]{2,1,0:T(8,128)(2,1)S(1)}, bf16[8,72,128]{2,1,0:T(8,128)(2,1)S(1)}, u32[]{:S(2)}, u32[]{:S(2)}) collective-permute-start(bf16[8,72,128]{2,1,0:T(8,128)(2,1)S(1)} %get-tuple-element.81.after_ref), channel_id=1, source_target_pairs={{0,1},{1,0},{2,3},{3,2},{4,5},{5,4},{6,7},{7,6},{8,9},{9,8},{10,11... | collective-permute-start | bytes 442376 | tf_op jit(solution)/shard_map/ppermute | solution.py:562
  30.4 4.7 %collective-permute-start.2 = (bf16[4,72,128]{2,1,0:T(8,128)(2,1)S(1)}, bf16[4,72,128]{2,1,0:T(8,128)(2,1)S(1)}, u32[]{:S(2)}, u32[]{:S(2)}) collective-permute-start(bf16[4,72,128]{2,1,0:T(8,128)(2,1)S(1)} %get-tuple-element.83), channel_id=1, source_target_pairs={{0,2},{2,0},{1,3},{3,1},{4,6},{6,4},{5,7},{7,5},{8,10},{10,8},{9,1... | collective-permute-start | bytes 221192 | tf_op jit(solution)/shard_map/ppermute | solution.py:551
  59.3 1.6 %collective-permute-start.3 = (bf16[8,144,128]{2,1,0:T(8,128)(2,1)S(1)}, bf16[8,144,128]{2,1,0:T(8,128)(2,1)S(1)}, u32[]{:S(2)}, u32[]{:S(2)}) collective-permute-start(bf16[8,144,128]{2,1,0:T(8,128)(2,1)S(1)} %all_to_all.21.half_ref), channel_id=1, source_target_pairs={{0,1},{1,0},{2,3},{3,2},{4,5},{5,4},{6,7},{7,6},{8,9},{9,8},{10,11... | collective-permute-start | bytes 884744 | tf_op jit(solution)/shard_map/ppermute | solution.py:578
